TPU v7x, 32 devices: a whole 2x2x4 slice. The times are simulated.
32 devices in a mesh: prow: 8 (over y, x, core), pcol: 4 (over z).
Axes of the slice: x: 2, y: 2, z: 4, core: 2. Of those that a mesh axis runs over, the one named last changes fastest.
Arguments:
- skeleton: float32 [2048, 32768], P('prow', 'pcol'), as said below
- pivots: int32 [2, 512], replicated, may hold values from 0 to 2047, as said below
Outputs:
- factored: float32 [2048, 32768], P('prow', 'pcol')
Inputs may be any that keep to these rules, and one draw needn't show every extreme that they name: `pivots`: all 1024 entries are distinct. In each panel's list, entries g * 64 to (g + 1) * 64 - 1 are rows of the g-th block of 256 rows. `skeleton`: each step's pivot block D is invertible with a condition number below 10.
All inputs are finite; a program needn't handle non-finite values.
Results may differ from a plain program's by a relative error of at most 0.0001.
Values sent between devices are 32-bit elements; how exact they have to be, the bound alone decides.
No kernel may reach another device: no remote copies, remote signals or barrier semaphores. Data moves between devices by JAX's collectives and lax.ppermute only.
A program may use at most 128 MiB of HBM per device.

v0:
```python
import jax
import jax.numpy as jnp
from jax import lax
from jax.sharding import PartitionSpec as P

NB = 512
STEPS = 2


highest = lax.Precision.HIGHEST


def broadcast(value, axis, source):
    kept = jnp.where(lax.axis_index(axis) == source, value, 0).astype(value.dtype)
    return lax.psum(kept, axis)


def invert_block(pivot_block):
    normal_matrix = jnp.dot(pivot_block, pivot_block.T, precision=highest)
    factor = jnp.linalg.cholesky(normal_matrix)
    unit = jnp.eye(pivot_block.shape[0], dtype=jnp.float32)
    normal_inverse = jax.scipy.linalg.cho_solve((factor, True), unit)
    return jnp.dot(pivot_block.T, normal_inverse, precision=highest)


def to_cyclic(matrix):
    rows_dev, local_cols = matrix.shape
    col_devices = lax.axis_size("pcol")
    blocks = local_cols // NB
    shaped = matrix.reshape(rows_dev, blocks // col_devices, col_devices, NB)
    moved = lax.all_to_all(shaped, "pcol", split_axis=2, concat_axis=1, tiled=True)
    return moved.reshape(rows_dev, local_cols)


def spread(values, source):
    return jax.tree.map(lambda part: broadcast(part, "pcol", source), values)


def on_device(skeleton, pivots):
    rows_dev, local_cols = skeleton.shape
    row_devices = lax.axis_size("prow")
    col_devices = lax.axis_size("pcol")
    share = NB // row_devices
    row_place = lax.axis_index("prow")
    col_place = lax.axis_index("pcol")
    row_ids = row_place * rows_dev + jnp.arange(rows_dev, dtype=jnp.int32)
    within = jnp.arange(local_cols, dtype=jnp.int32)
    matrix = to_cyclic(skeleton)
    column_ids = (within // NB * col_devices + col_place) * NB + within % NB
    sources = [step % col_devices for step in range(STEPS)]
    offsets = [step // col_devices * NB for step in range(STEPS)]
    identity_block = jnp.eye(NB, dtype=jnp.float32)

    def owned(step):
        return (
            lax.dynamic_slice_in_dim(pivots[step], row_place * share, share) - row_place * rows_dev
        )

    def factor_step(matrix, upper, step, pending):
        offset = offsets[step]
        source = sources[step]
        at_source = col_place == source
        pivot_block = jnp.where(at_source, upper[:, offset : offset + NB], identity_block)
        chosen = pivots[: step + 1].reshape(-1)
        active = jnp.all(row_ids[:, None] != chosen[None, :], axis=1, keepdims=True)
        panel_cols = matrix[:, offset : offset + NB]
        carried = None
        inverse = invert_block(pivot_block)
        lower = jnp.where(active, jnp.dot(panel_cols, inverse, precision=highest), 0.0)
        if pending is None:
            lower = spread(lower, source)
        else:
            next_solved = jnp.dot(pending[:, offset : offset + NB], inverse, precision=highest)
            lower, carried = spread((lower, next_solved), source)
        update = jnp.dot(lower, upper, precision=highest)
        matrix = matrix - jnp.where(column_ids[None, :] >= (step + 1) * NB, update, 0.0)
        kept = jnp.where(at_source & active, lower, matrix[:, offset : offset + NB])
        matrix = matrix.at[:, offset : offset + NB].set(kept)
        return (matrix, carried)

    step = 0
    upper = lax.all_gather(jnp.take(matrix, owned(step), axis=0), "prow", axis=0, tiled=True)
    following = lax.all_gather(
        jnp.take(matrix, owned(step + 1), axis=0), "prow", axis=0, tiled=True
    )
    matrix, carried = factor_step(matrix, upper, step, following)
    following = following - jnp.dot(carried, upper, precision=highest)
    matrix, unused = factor_step(matrix, following, step + 1, None)
    return matrix


def solution(mesh):
    placed = (P("prow", "pcol"), P())
    return jax.shard_map(
        on_device, mesh=mesh, in_specs=placed, out_specs=P("prow", "pcol"), check_vma=False
    )
```

profile of v0, /device:TPU:0, one launch (start us, length us, event | category | flops | bytes accessed | tf_op | source)
XLA Modules:
  0.0 871.8 jit_solution(5044628824908122724)
XLA Ops:
  6.5 10.8 %reshape.151 = f32[256,4,4,512]{3,2,1,0:T(4,128)} reshape(f32[256,8192]{1,0:T(8,128)} %param.11) | data formatting | bytes 16777216 | tf_op jit(solution)/shard_map/reshape | solution.py:30
  17.3 9.9 %copy.12 = f32[256,4,4,512]{0,3,1,2:T(8,128)} copy(f32[256,4,4,512]{3,2,1,0:T(4,128)} %reshape.151) | data formatting | bytes 16777216 | tf_op jit(solution)/shard_map/reshape | solution.py:30
  27.3 6.5 all-to-all-start
  33.9 183.9 %all-to-all-done = f32[256,4,4,512]{0,3,1,2:T(8,128)} async-done(((f32[256,4,4,512]{0,3,1,2:T(8,128)}), f32[256,4,4,512]{0,3,1,2:T(8,128)}, u32[]{:S(2)}, u32[]{:S(2)}) %all-to-all-start) | async-done | bytes 8388640 | tf_op jit(solution)/shard_map/all_to_all | solution.py:31
  217.8 8.9 %copy.13 = f32[256,8192]{1,0:T(8,128)} copy(f32[256,8192]{0,1:T(8,128)} %bitcast.2) | data formatting | bytes 16777216 | tf_op jit(solution)/shard_map/reshape | solution.py:32
  226.7 5.6 gather_fusion
  232.3 1.6 broadcast_select_fusion.1
  233.9 5.6 gather_fusion.1
  239.5 1.6 broadcast_select_fusion
  242.0 81.0 %all-gather.3.cloned.1.call-done = f32[512,8192]{1,0:T(8,128)} async-done(((f32[64,8192]{1,0:T(8,128)}), f32[512,8192]{1,0:T(8,128)}) %all-gather.3.cloned.1.call-update) | async-done | bytes 16777232 | tf_op jit(solution)/shard_map/all_gather | solution.py:82
  322.9 3.5 fusion.25
  328.0 11.7 %cholesky.286 = f32[128,128]{1,0:T(8,128)S(1)} custom-call(f32[128,128]{1,0:T(8,128)S(1)} %cholesky.426), custom_call_target="Cholesky" | custom-call | tf_op jit(solution)/shard_map/jit(cholesky)/cholesky | solution.py:20
  339.7 9.8 %custom-call.29 = f32[1,128,128]{1,2,0:T(8,128)S(1)} custom-call(f32[1,128,128]{2,1,0:T(8,128)S(1)} %get-tuple-element.93), custom_call_target="InvertDiagBlocksLowerTriangular" | custom-call | tf_op jit(solution)/shard_map/jit(cholesky)/cholesky | solution.py:20
  352.2 11.9 %cholesky.305 = f32[128,128]{1,0:T(8,128)S(1)} custom-call(f32[128,128]{1,0:T(8,128)S(1)} %cholesky.430), custom_call_target="Cholesky" | custom-call | tf_op jit(solution)/shard_map/jit(cholesky)/cholesky | solution.py:20
  364.1 9.8 %custom-call.30 = f32[1,128,128]{1,2,0:T(8,128)S(1)} custom-call(f32[1,128,128]{2,1,0:T(8,128)S(1)} %get-tuple-element.90), custom_call_target="InvertDiagBlocksLowerTriangular" | custom-call | tf_op jit(solution)/shard_map/jit(cholesky)/cholesky | solution.py:20
  375.5 11.7 %cholesky.326 = f32[128,128]{1,0:T(8,128)S(1)} custom-call(f32[128,128]{1,0:T(8,128)S(1)} %cholesky.435), custom_call_target="Cholesky" | custom-call | tf_op jit(solution)/shard_map/jit(cholesky)/cholesky | solution.py:20
  387.2 9.8 %custom-call.31 = f32[1,128,128]{1,2,0:T(8,128)S(1)} custom-call(f32[1,128,128]{2,1,0:T(8,128)S(1)} %get-tuple-element.87), custom_call_target="InvertDiagBlocksLowerTriangular" | custom-call | tf_op jit(solution)/shard_map/jit(cholesky)/cholesky | solution.py:20
  398.5 11.9 %cholesky.343 = f32[128,128]{1,0:T(8,128)S(1)} custom-call(f32[128,128]{1,0:T(8,128)S(1)} %convolution_subtract_fusion.18), custom_call_target="Cholesky" | custom-call | tf_op jit(solution)/shard_map/jit(cholesky)/cholesky | solution.py:20
  415.5 7.9 while.6
  423.4 39.3 %custom-call.32 = f32[4,128,128]{1,2,0:T(8,128)S(1)} custom-call(f32[4,128,128]{2,1,0:T(8,128)S(1)} %get-tuple-element.46), custom_call_target="InvertDiagBlocksLowerTriangular" | custom-call | tf_op jit(solution)/shard_map/jit(_cho_solve)/triangular_solve | solution.py:22
  468.9 3.1 fusion.6
  472.1 3.7 fusion.4
  475.7 4.0 convolution_select_fusion.2
  481.2 67.7 %all-reduce.7.cloned.1.call-done = (f32[256,512]{0,1:T(8,128)}, f32[512,512]{1,0:T(8,128)}) async-done(((f32[256,512]{0,1:T(8,128)}, f32[512,512]{1,0:T(8,128)}), (f32[256,512]{0,1:T(8,128)}, f32[512,512]{1,0:T(8,128)})) %all-reduce.7.cloned.1.call-update) | async-done | bytes 1572880 | tf_op jit(solution)/shard_map/psum | solution.py:15
  548.9 31.4 %convolution_subtract_fusion = f32[512,8192]{1,0:T(8,128)S(1)} fusion(f32[512,8192]{1,0:T(8,128)} %all-gather.5.cloned.1.call-done, f32[512,512]{1,0:T(8,128)} %get-tuple-element.65, f32[512,8192]{1,0:T(8,128)} %all-gather.3.cloned.1.call-done), kind=kOutput, calls=%fused_computation.6 | convolution fusion | flops 25773998080 | bytes 51380224 | tf_op jit(solution)/shard_map/dot_general | solution.py:87
  580.3 5.7 copy-done
  586.0 1.9 fusion.26
  589.5 11.7 %cholesky.358 = f32[128,128]{1,0:T(8,128)S(1)} custom-call(f32[128,128]{1,0:T(8,128)S(1)} %cholesky.439), custom_call_target="Cholesky" | custom-call | tf_op jit(solution)/shard_map/jit(cholesky)/cholesky | solution.py:20
  601.3 9.8 %custom-call.33 = f32[1,128,128]{1,2,0:T(8,128)S(1)} custom-call(f32[1,128,128]{2,1,0:T(8,128)S(1)} %get-tuple-element.83), custom_call_target="InvertDiagBlocksLowerTriangular" | custom-call | tf_op jit(solution)/shard_map/jit(cholesky)/cholesky | solution.py:20
  613.7 11.9 %cholesky.377 = f32[128,128]{1,0:T(8,128)S(1)} custom-call(f32[128,128]{1,0:T(8,128)S(1)} %cholesky.443), custom_call_target="Cholesky" | custom-call | tf_op jit(solution)/shard_map/jit(cholesky)/cholesky | solution.py:20
  626.9 9.8 %custom-call.34 = f32[1,128,128]{1,2,0:T(8,128)S(1)} custom-call(f32[1,128,128]{2,1,0:T(8,128)S(1)} %get-tuple-element.80), custom_call_target="InvertDiagBlocksLowerTriangular" | custom-call | tf_op jit(solution)/shard_map/jit(cholesky)/cholesky | solution.py:20
  638.3 11.7 %cholesky.398 = f32[128,128]{1,0:T(8,128)S(1)} custom-call(f32[128,128]{1,0:T(8,128)S(1)} %cholesky.448), custom_call_target="Cholesky" | custom-call | tf_op jit(solution)/shard_map/jit(cholesky)/cholesky | solution.py:20
  650.8 9.8 %custom-call.35 = f32[1,128,128]{1,2,0:T(8,128)S(1)} custom-call(f32[1,128,128]{2,1,0:T(8,128)S(1)} %get-tuple-element.77), custom_call_target="InvertDiagBlocksLowerTriangular" | custom-call | tf_op jit(solution)/shard_map/jit(cholesky)/cholesky | solution.py:20
  662.0 12.1 %cholesky.415 = f32[128,128]{1,0:T(8,128)S(1)} custom-call(f32[128,128]{1,0:T(8,128)S(1)} %convolution_subtract_fusion.17), custom_call_target="Cholesky" | custom-call | tf_op jit(solution)/shard_map/jit(cholesky)/cholesky | solution.py:20
  677.5 8.0 while.7
  678.1 1.4 bitcast_dynamic-update-slice_fusion.5
  680.1 1.4 bitcast_dynamic-update-slice_fusion.5
  684.2 1.4 bitcast_dynamic-update-slice_fusion.5
  685.6 39.3 %custom-call.36 = f32[4,128,128]{1,2,0:T(8,128)S(1)} custom-call(f32[4,128,128]{2,1,0:T(8,128)S(1)} %get-tuple-element.47), custom_call_target="InvertDiagBlocksLowerTriangular" | custom-call | tf_op jit(solution)/shard_map/jit(_cho_solve)/triangular_solve | solution.py:22
  731.1 3.1 fusion.14
  734.2 36.9 %fusion.1 = f32[256,8192]{0,1:T(8,128)S(1)} fusion(f32[256,8192]{0,1:T(8,128)} %bitcast.2, f32[256,512]{0,1:T(8,128)S(1)} %copy-done.2, f32[512,8192]{1,0:T(8,128)} %all-gather.3.cloned.1.call-done, pred[8192]{0:T(1024)(128)(4,1)S(1)} %broadcast_compare_fusion.1), kind=kOutput, calls=%fused_computation.10 | convolution fusion | flops 12889096192 | bytes 34086912 | tf_op jit(solution)/shard_map/dot_general | solution.py:75
  771.2 3.4 copy-done.1
  774.6 3.3 fusion.2
  778.0 2.5 fusion.81
  780.5 35.2 %all-reduce.5.cloned.1.call-done = f32[256,512]{0,1:T(8,128)} async-done(((f32[256,512]{0,1:T(8,128)}), f32[256,512]{0,1:T(8,128)}) %all-reduce.5.cloned.1.call-update) | async-done | bytes 524304 | tf_op jit(solution)/shard_map/psum | solution.py:15
  815.8 37.9 %fusion = f32[256,8192]{0,1:T(8,128)} fusion(f32[256,8192]{0,1:T(8,128)} %fusion.81, f32[256,512]{0,1:T(8,128)} %all-reduce.5.cloned.1.call-done, f32[512,8192]{1,0:T(8,128)} %copy-done, pred[8192]{0:T(1024)(128)(4,1)S(1)} %broadcast_compare_fusion), kind=kOutput, calls=%fused_computation.8 | convolution fusion | flops 12889096192 | bytes 34086912 | tf_op jit(solution)/shard_map/dot_general | solution.py:75
  853.6 2.5 fusion.47
  856.1 8.9 %copy.20 = f32[256,8192]{1,0:T(8,128)} copy(f32[256,8192]{0,1:T(8,128)} %fusion.47) | data formatting | bytes 16777216 | tf_op jit(solution)/shard_map/scatter | solution.py:78
  (130 shorter events, 46.4 us)
Async XLA Ops:
  27.3 6.5 copy-start.6
  27.3 190.5 %all-to-all-start = ((f32[256,4,4,512]{0,3,1,2:T(8,128)}), f32[256,4,4,512]{0,3,1,2:T(8,128)}, u32[]{:S(2)}, u32[]{:S(2)}) async-start(f32[256,4,4,512]{0,3,1,2:T(8,128)} %copy.12), calls=%async_computation | async-start | bytes 16777216 | tf_op jit(solution)/shard_map/all_to_all | solution.py:31
  33.7 289.2 %all-gather.3.cloned.1.call-start = ((), (), s32[]{:S(2)}) async-start(), calls=%async_computation.1 | async-start | bytes 18874368 | tf_op jit(solution)/shard_map/all_gather | solution.py:82
  233.9 241.9 %all-gather.5.cloned.1.call-start = ((), (), s32[]{:S(2)}) async-start(), calls=%async_computation.2 | async-start | bytes 18874368 | tf_op jit(solution)/shard_map/all_gather | solution.py:83
  241.1 307.8 %all-reduce.7.cloned.1.call-start = ((), (), s32[]{:S(2)}) async-start(), calls=%async_computation.4 | async-start | bytes 3145728 | tf_op jit(solution)/shard_map/psum | solution.py:15
  327.0 1.0 copy-start.4
  479.8 335.9 %all-reduce.5.cloned.1.call-start = ((), (), s32[]{:S(2)}) async-start(), calls=%async_computation.3 | async-start | bytes 1048576 | tf_op jit(solution)/shard_map/psum | solution.py:15
  580.3 5.7 copy-start
  588.5 1.0 copy-start.3
  677.5 56.8 %copy-start.2 = (f32[256,512]{0,1:T(8,128)S(1)}, f32[256,512]{0,1:T(8,128)}, u32[]{:S(2)}) copy-start(f32[256,512]{0,1:T(8,128)} %get-tuple-element.64) | copy-start | bytes 1572868
  771.2 3.4 copy-start.1
  815.7 37.9 %copy-start.5 = (f32[256,512]{0,1:T(8,128)S(1)}, f32[256,512]{0,1:T(8,128)}, u32[]{:S(2)}) copy-start(f32[256,512]{0,1:T(8,128)} %all-reduce.5.cloned.1.call-done) | copy-start | bytes 1572868
Sparse Core Ops, SparseCore 0:
  234.0 88.8 all-gather.2
  324.8 90.0 all-gather.4
  479.9 68.9 all-reduce.6
  778.0 37.6 all-reduce.4
where the time goes:
time: 878 us; the launch traced here: 872 us
  waiting for transfers between devices  368 us (42%)
  other arithmetic  248 us (28%)
  matrix products  152 us (17%)
  local copies, waits for them, and re-layouts  77.5 us (9%)
  between operations  18.9 us (2%)
    all_to_all x1, waiting for transfers between devices, to_cyclic(): lax.all_to_all(shaped, 'pcol', split_axis=2, concat_axis=1, tiled=True)  184 us
    another operation x30, other arithmetic, invert_block(): factor = jnp.linalg.cholesky(normal_matrix)  159 us
    psum x2, waiting for transfers between devices, broadcast(): return lax.psum(kept, axis)  103 us
    all_gather x1, waiting for transfers between devices, on_device(): lax.all_gather(jnp.take(matrix, owned(step), axis=0), 'prow', axis=0, til...  81 us
    another operation x5, other arithmetic, invert_block(): normal_inverse = jax.scipy.linalg.cho_solve((factor, True), unit)  78.9 us
    dot_general x2, matrix products, factor_step(): update = jnp.dot(lower, upper, precision=highest)  74.8 us
    dot_general x1, matrix products, on_device(): following = following - jnp.dot(carried, upper, precision=highest)  31.4 us
    reshape x2, local copies, waits for them, and re-layouts, to_cyclic(): shaped = matrix.reshape(rows_dev, blocks // col_devices, col_devices, NB)  20.7 us
  transfers between devices with their start and end apart: 5, of which 4 were waited for; matrix products, arithmetic and copies ran while one was open for 18% of the time, Pallas kernels for 0%

commit v1 on v0

v1 whole, which is shorter than its diff:
```python
import jax
import jax.numpy as jnp
from jax import lax
from jax.experimental import pallas as pl
from jax.experimental.pallas import tpu as pltpu
from jax.sharding import PartitionSpec as P

NB = 512
f32 = jnp.float32
bf16 = jnp.bfloat16
highest = lax.Precision.HIGHEST


def dot(a, b):
    return jnp.dot(a, b, preferred_element_type=f32)


def split2(x):
    hi = x.astype(bf16)
    return hi, (x - hi.astype(f32)).astype(bf16)


def dot3(a, b):
    ah, al = split2(a)
    bh, bl = split2(b)
    return dot(ah, bh) + (dot(ah, bl) + dot(al, bh))


def dot6(a, b):
    return jnp.dot(a, b, preferred_element_type=f32, precision=highest)


def select(onehot, x):
    y = x * 0.5
    hi = y.astype(bf16)
    rest = y - hi.astype(f32)
    mid = rest.astype(bf16)
    low = (rest - mid.astype(f32)).astype(bf16)
    return 2.0 * ((dot(onehot, hi) + dot(onehot, mid)) + dot(onehot, low))


def cost(flops, nbytes):
    return pl.CostEstimate(flops=int(flops), transcendentals=0, bytes_accessed=int(nbytes))


def params(n):
    return pltpu.CompilerParams(dimension_semantics=("arbitrary",) * n, vmem_limit_bytes=56 << 20)


def panel_rows(pidx, skeleton):
    rows = skeleton.shape[0]
    piv = pidx.shape[0]
    rest = rows - piv
    width = 2 * NB

    def body(idx_ref, x_ref, s_ref, st_ref, gp_ref, gn_ref):
        col = lax.broadcasted_iota(jnp.int32, (piv, rows), 1)
        sp = (col == idx_ref[...]).astype(f32)
        free = 1.0 - jnp.sum(sp, axis=0, keepdims=True)
        before = lax.broadcasted_iota(jnp.int32, (rows, rows), 0) < lax.broadcasted_iota(jnp.int32, (rows, rows), 1)
        rank = dot(jnp.broadcast_to(free, (8, rows)).astype(bf16), before.astype(f32).astype(bf16))[0:1]
        place = lax.broadcasted_iota(jnp.int32, (rest, rows), 0).astype(f32)
        sn = jnp.where(rank == place, free, 0.0)
        onehot = jnp.concatenate([sp, sn], axis=0)
        st_ref[...] = onehot.T.astype(bf16)
        s_ref[...] = onehot.astype(bf16)
        x = select(onehot.astype(bf16), x_ref[...])
        gp_ref[...] = x[0:piv]
        gn_ref[...] = x[piv:]

    full = lambda shape: pl.BlockSpec(shape, lambda i: (0, 0))
    shapes = [((rows, rows), bf16), ((rows, rows), bf16), ((piv, width), f32), ((rest, width), f32)]
    return pl.pallas_call(
        body,
        grid=(1,),
        in_specs=[full((piv, 1)), full((rows, width))],
        out_specs=[full(s) for s, _ in shapes],
        out_shape=[jax.ShapeDtypeStruct(s, d) for s, d in shapes],
        compiler_params=params(1),
        cost_estimate=cost(6 * rows * rows * width, 8 * rows * width),
        name="panel_rows",
    )(pidx, skeleton)


def pick(scalars, onehot, skeleton, k, devs, piv):
    rows, local = skeleton.shape
    per = local // NB // devs
    sizes = (piv, rows - piv)

    def body(sc_ref, s_ref, *refs):
        for i in range(per):
            x = select(s_ref[...], refs[i][...])
            refs[per][:, i * NB : (i + 1) * NB] = x[0:piv]
            refs[per + 1][:, i * NB : (i + 1) * NB] = x[piv:]

    block = lambda i: pl.BlockSpec((rows, NB), lambda _, sc: (0, lax.rem(sc[0] + k, devs) + devs * i))
    return pl.pallas_call(
        body,
        grid_spec=pltpu.PrefetchScalarGridSpec(
            num_scalar_prefetch=1,
            grid=(1,),
            in_specs=[pl.BlockSpec((rows, rows), lambda _, sc: (0, 0))] + [block(i) for i in range(per)],
            out_specs=[pl.BlockSpec((n, per * NB), lambda _, sc: (0, 0)) for n in sizes],
        ),
        out_shape=[jax.ShapeDtypeStruct((n, per * NB), f32) for n in sizes],
        compiler_params=params(1),
        cost_estimate=cost(6 * rows * rows * per * NB, 8 * rows * per * NB),
        name="pick",
    )(scalars, onehot, *[skeleton] * per)


def invert(d_ref, x_ref, r_ref):
    n = d_ref.shape[0]
    eye = lax.broadcasted_iota(jnp.int32, (n, n), 0) == lax.broadcasted_iota(jnp.int32, (n, n), 1)

    def total(v):
        return jnp.sum(jnp.sum(v, axis=0, keepdims=True), axis=1, keepdims=True)

    d = d_ref[...]
    size = jnp.max(jnp.max(jnp.abs(d), axis=0, keepdims=True), axis=1, keepdims=True)
    unit = 1.0 / size
    d = d * unit
    d_ref[...] = d
    dh = d.astype(bf16)
    power = lax.dot_general(dh, dh, (((1,), (1,)), ((), ())), preferred_element_type=f32)
    norm = jnp.sqrt(total(power * power))
    norms = [norm]
    for _ in range(3):
        ph = (power * (1.0 / norm)).astype(bf16)
        power = dot(ph, ph)
        norm = jnp.sqrt(total(power * power))
        norms.append(norm)
    bound = norms[-1]
    for value in reversed(norms[:-1]):
        bound = value * jnp.sqrt(bound)
    x_ref[...] = d.T * (1.7 / bound)

    def residual(product):
        r = jnp.where(eye, 1.0, 0.0) - product
        r_ref[...] = r
        return jnp.sum(r * r)

    def coarse(carry):
        x = x_ref[...]
        x_ref[...] = x + dot(x.astype(bf16), r_ref[...].astype(bf16))
        return carry[0] + 1, residual(dot(d_ref[...].astype(bf16), x_ref[...].astype(bf16)))

    def fine(carry):
        x = x_ref[...]
        x_ref[...] = x + dot3(x, r_ref[...])
        return carry[0] + 1, residual(dot3(d_ref[...], x_ref[...]))

    first = residual(dot(d_ref[...].astype(bf16), x_ref[...].astype(bf16)))
    done = lax.while_loop(lambda c: (c[1] > 1.0) & (c[0] < 24), coarse, (jnp.int32(0), first))
    start = residual(dot3(d_ref[...], x_ref[...]))
    lax.while_loop(lambda c: (c[1] > 4e-6) & (c[0] < 24), fine, (done[0] * 0, start))
    residual(dot6(d_ref[...], x_ref[...]))
    x = x_ref[...]
    x_ref[...] = (x + dot3(x, r_ref[...])) * unit


def natural(sc_ref, count, share):
    n = count * share
    at = lax.broadcasted_iota(jnp.int32, (share, n), 1) - lax.broadcasted_iota(jnp.int32, (share, n), 0)
    return jnp.concatenate([(at == sc_ref[2 + m] * share).astype(f32) for m in range(count)], axis=0).astype(bf16)


def place(x, onehot):
    y = x * 0.5
    hi = y.astype(bf16)
    rest = y - hi.astype(f32)
    mid = rest.astype(bf16)
    low = (rest - mid.astype(f32)).astype(bf16)
    return 2.0 * ((dot(hi, onehot) + dot(mid, onehot)) + dot(low, onehot))


def multipliers(scalars, blocks, panel_rest, share):
    rest = panel_rest.shape[0]
    half = share // 2
    width = 2 * NB
    count = len(blocks)

    def body(sc_ref, *refs):
        b_refs = refs[:count]
        pn_ref, l_ref, l0_ref, w0, w1, d_ref, x0, x1, r_ref, lp = refs[count:]

        @pl.when(sc_ref[0] != 0)
        def _():
            l_ref[...] = jnp.zeros_like(l_ref)
            l0_ref[...] = jnp.zeros_like(l0_ref)

        @pl.when(sc_ref[0] == 0)
        def _():
            for m in range(count):
                w0[m * share : (m + 1) * share, :] = b_refs[m][0:share, :]
                w1[m * share : (m + 1) * share, :] = b_refs[m][share : 2 * share, :]
            d_ref[...] = w0[:, 0:NB]
            invert(d_ref, x0, r_ref)
            lp[...] = dot3(w1[:, 0:NB], x0[...])
            d_ref[...] = w1[:, NB:width] - dot3(lp[...], w0[:, NB:width])
            invert(d_ref, x1, r_ref)
            l0 = dot3(pn_ref[:, 0:NB], x0[...])
            l1 = dot3(pn_ref[:, NB:width] - dot3(l0, w0[:, NB:width]), x1[...])
            l_ref[half:, 0:NB] = l0 - dot3(l1, lp[...])
            l_ref[half:, NB:width] = l1
            l_ref[0:half, 0:NB] = lp[0:half, :]
            l_ref[0:half, NB:width] = lp[half:share, :]
            back = natural(sc_ref, count, share)
            l0_ref[0:share, :] = place(lp[0:share, :], back)
            l0_ref[share:, :] = place(l0, back)

    full = lambda shape: pl.BlockSpec(shape, lambda i, sc: (0, 0))
    square = pltpu.VMEM((NB, NB), f32)
    return pl.pallas_call(
        body,
        grid_spec=pltpu.PrefetchScalarGridSpec(
            num_scalar_prefetch=1,
            grid=(1,),
            in_specs=[full((2 * share, width))] * count + [full((rest, width))],
            out_specs=[full((half + rest, width)), full((share + rest, NB))],
            scratch_shapes=[pltpu.VMEM((NB, width), f32)] * 2 + [square] * 5,
        ),
        out_shape=[jax.ShapeDtypeStruct((half + rest, width), f32), jax.ShapeDtypeStruct((share + rest, NB), f32)],
        compiler_params=params(1),
        cost_estimate=cost(30e9, 8 << 20),
        name="multipliers",
    )(scalars, *blocks, panel_rest)


def settle(scalars, parts, lower0, share, count):
    half = share // 2
    width = 2 * NB
    tall = lower0.shape[0]
    rest = tall - share

    def body(sc_ref, *refs):
        l0_ref, lh, fixed = refs[-3:]
        low = refs[0][...]
        for ref in refs[1:-3]:
            low = low + ref[...]
        fixed[...] = l0_ref[...]

        @pl.when(sc_ref[0] == 1)
        def _():
            fixed[share:, :] = place(low[half:, NB:width], natural(sc_ref, count, share))

        for n, piece in enumerate(split2(low)):
            at = n * tall
            lh[at : at + half, 0:NB] = piece[0:half, 0:NB]
            lh[at + half : at + share, 0:NB] = piece[0:half, NB:width]
            lh[at : at + share, NB:width] = jnp.zeros((share, NB), bf16)
            lh[at + share : at + tall, :] = piece[half:, :]

    full = lambda shape: pl.BlockSpec(shape, lambda i, sc: (0, 0))
    return pl.pallas_call(
        body,
        grid_spec=pltpu.PrefetchScalarGridSpec(
            num_scalar_prefetch=1,
            grid=(1,),
            in_specs=[full((half + rest, width))] * len(parts) + [full((tall, NB))],
            out_specs=[full((2 * tall, width)), full((tall, NB))],
        ),
        out_shape=[jax.ShapeDtypeStruct((2 * tall, width), bf16), jax.ShapeDtypeStruct((tall, NB), f32)],
        compiler_params=params(1),
        cost_estimate=cost(1e9, 4 * tall * width * (len(parts) + 2)),
        name="settle",
    )(scalars, *parts, lower0)


def came_from(sc, k, devs):
    return lax.rem(sc[0] + devs - k, devs)


def product(scalars, k, lh, fixed, blocks, share, devs):
    tall = fixed.shape[0]
    rest = tall - share
    piv = 2 * share
    width = 2 * NB
    total = blocks[0].shape[1]
    steps = total // NB
    count = len(blocks)
    piece = NB // 2

    def body(sc_ref, lh_ref, fixed_ref, *refs):
        b_refs = refs[:count]
        vp_ref, pn_ref, uh, ul = refs[count:]
        for j in range(2):
            cols = slice(j * piece, (j + 1) * piece)
            for m in range(count):
                hi, lo = split2(b_refs[m][:, cols])
                for t in range(2):
                    at = slice(t * NB + m * share, t * NB + (m + 1) * share)
                    uh[at, cols] = hi[t * share : (t + 1) * share]
                    ul[at, cols] = lo[t * share : (t + 1) * share]
            big = dot(lh_ref[...], uh[:, cols])
            prod = big[0:tall] + (big[tall:] + dot(lh_ref[0:tall, :], ul[:, cols]))
            vp_ref[0:share, cols] = b_refs[0][0:share, cols]
            vp_ref[share:piv, cols] = b_refs[0][share:piv, cols] - prod[0:share]
            pn_ref[:, cols] = prod[share:]

        @pl.when((pl.program_id(0) == 0) & (came_from(sc_ref, k, devs) == 0) & (sc_ref[0] == 0))
        def _():
            vp_ref[share:piv, :] = fixed_ref[0:share, :]

    full = lambda shape: pl.BlockSpec(shape, lambda i, sc: (0, 0))
    moving = lambda n: pl.BlockSpec((n, NB), lambda i, sc: (0, i))
    return pl.pallas_call(
        body,
        grid_spec=pltpu.PrefetchScalarGridSpec(
            num_scalar_prefetch=1,
            grid=(steps,),
            in_specs=[full((2 * tall, width)), full((tall, NB))] + [moving(piv)] * count,
            out_specs=[moving(piv), moving(rest)],
            scratch_shapes=[pltpu.VMEM((width, NB), bf16), pltpu.VMEM((width, NB), bf16)],
        ),
        out_shape=[jax.ShapeDtypeStruct((piv, total), f32), jax.ShapeDtypeStruct((rest, total), f32)],
        compiler_params=params(1),
        cost_estimate=cost(6 * tall * width * total, 4 * (width + piv + rest) * total),
        name="product",
    )(scalars, lh, fixed, *blocks)


def finish(scalars, k, st, fixed, done, prod, others, out, out_shape, devs):
    rows = st.shape[0]
    piv = done.shape[0]
    rest = rows - piv
    total = others.shape[1]
    tile = NB
    steps = total // tile

    def body(sc_ref, st_ref, fixed_ref, d_ref, p_ref, n_ref, *refs):
        o_ref, v = refs[-2:]
        v[0:piv, :] = d_ref[...]
        v[piv:, :] = n_ref[...] - p_ref[...]

        @pl.when((pl.program_id(0) == 0) & (came_from(sc_ref, k, devs) == 0) & (sc_ref[0] < 2))
        def _():
            v[piv:, :] = fixed_ref[piv // 2 :, :]

        o_ref[...] = select(st_ref[...], v[...])

    full = lambda shape: pl.BlockSpec(shape, lambda i, sc: (0, 0))
    moving = lambda n: pl.BlockSpec((n, tile), lambda i, sc: (0, i))
    operands = [st, fixed, done, prod, others]
    in_specs = [full((rows, rows)), full((fixed.shape[0], NB)), moving(piv), moving(rest), moving(rest)]
    aliases = {}
    if out is not None:
        aliases = {1 + len(operands): 0}
        operands.append(out)
        in_specs.append(pl.BlockSpec(memory_space=pl.ANY))
    return pl.pallas_call(
        body,
        grid_spec=pltpu.PrefetchScalarGridSpec(
            num_scalar_prefetch=1,
            grid=(steps,),
            in_specs=in_specs,
            out_specs=pl.BlockSpec((rows, tile), lambda i, sc: (0, came_from(sc, k, devs) * steps + i)),
            scratch_shapes=[pltpu.VMEM((rows, tile), f32)],
        ),
        out_shape=out_shape,
        input_output_aliases=aliases,
        compiler_params=params(1),
        cost_estimate=cost(6 * rows * rows * total, 4 * (rows + rest) * total),
        name="finish",
    )(scalars, *operands)


def across(x, size, move):
    return lax.ppermute(x, "prow", [(i, move(i)) for i in range(size)])


def gather_rows(x, size):
    blocks = [x]
    if size == 8:
        one = lambda i: i ^ (2 if i % 2 == 0 else 4)
        two = lambda i: i ^ (4 if i % 2 == 0 else 2)
        a = across(x, size, one)
        b = across(x, size, two)
        blocks += [a, b, across(a, size, two)]
    else:
        blocks += [across(x, size, lambda i, m=m: i ^ m) for m in range(2, size, 2)]
    return blocks + [across(block, size, lambda i: i ^ 1) for block in blocks]


def block_ids(row, size):
    even = row % 2 == 0
    if size == 8:
        ids = [row, jnp.where(even, row ^ 2, row ^ 4), jnp.where(even, row ^ 4, row ^ 2), row ^ 6]
        mate = row ^ 1
        ids += [mate, jnp.where(even, mate ^ 4, mate ^ 2), jnp.where(even, mate ^ 2, mate ^ 4), mate ^ 6]
        return ids
    ids = [row ^ m for m in range(0, size, 2)]
    return ids + [i ^ 1 for i in ids]


def on_device(skeleton, pivots):
    rows, local = skeleton.shape
    size = lax.axis_size("prow")
    devs = lax.axis_size("pcol")
    row = lax.axis_index("prow")
    col = lax.axis_index("pcol")
    share = NB // size
    scalars = jnp.stack([col, row] + block_ids(row, size)).astype(jnp.int32)
    own = lax.dynamic_slice_in_dim(pivots, row * share, share, axis=1) - row * rows
    pidx = own.reshape(2 * share, 1)
    onehot, st, panel_piv, panel_rest = panel_rows(pidx, skeleton)

    def shift(x, k):
        return lax.ppermute(x, "pcol", [(i, (i + k) % devs) for i in range(devs)])

    def send(x, pairs):
        return lax.ppermute(x, "pcol", pairs)

    order = rotations(devs)
    picked = {k: pick(scalars, onehot, skeleton, k, devs, 2 * share) for k in order + [0]}
    piv = {k: shift(picked[k][0], k) if k else picked[k][0] for k in [0] + order}
    panel = gather_rows(panel_piv, size)
    lower, lower0 = multipliers(scalars, panel, panel_rest, share)
    reach = devs // 2
    moved = send(lower, [(0, reach)])
    parts = [lower, moved]
    while reach > 1:
        reach //= 2
        direct = send(lower, [(0, reach)])
        onward = send(moved, [(i, i + reach) for i in range(2 * reach, devs, 2 * reach)])
        parts += [direct, onward]
        moved = moved + direct + onward if reach > 1 else moved
    rest = {k: shift(picked[k][1], k) if k else picked[k][1] for k in [0] + order}
    lh, fixed = settle(scalars, parts, lower0, share, len(panel))
    shape = jax.ShapeDtypeStruct((rows, local), f32)
    ready = {}
    for k in [0] + order:
        blocks = gather_rows(piv[k], size)
        ready[k] = product(scalars, k, lh, fixed, blocks, share, devs)
    out = None
    for k in [0] + order:
        out = finish(scalars, k, st, fixed, *ready[k], rest[k], out, shape, devs)
    return out


def rotations(devs):
    return sorted(range(1, devs), key=lambda k: (-min(k, devs - k), -k))


def solution(mesh):
    placed = (P("prow", "pcol"), P())
    return jax.shard_map(on_device, mesh=mesh, in_specs=placed, out_specs=P("prow", "pcol"), check_vma=False)
```

time: 878 us -> 381 us (0.43)
  other arithmetic: 248 us -> 0.75 us
  waiting for transfers between devices: 368 us -> 158 us
  matrix products: 152 us -> 0 us
  Pallas kernels: 0 us -> 116 us
  starting transfers between devices: 7.07 us -> 100 us
  local copies, waits for them, and re-layouts: 77.5 us -> 4.17 us
  between operations: 18.9 us -> 0.37 us
    another operation x36 -> x0, other arithmetic: 239 us -> none  [the longest x30 159 us: invert_block(): factor = jnp.linalg.cholesky(normal_matrix)]
    all_to_all x1 -> x0, waiting for transfers between devices: 184 us -> none  [to_cyclic(): lax.all_to_all(shaped, 'pcol', split_axis=2, concat_axis=1, tiled=True)]
    ppermute x0 -> x44, waiting for transfers between devices: none -> 158 us  [the longest x6 102 us: shift(): return lax.ppermute(x, 'pcol', [(i, (i + k) % devs) for i in range(devs)])]
    dot_general x10 -> x0, matrix products: 129 us -> none  [the longest x2 74.8 us: factor_step(): update = jnp.dot(lower, upper, precision=highest)]
    pallas_call x0 -> x15, Pallas kernels: none -> 116 us  [the longest x1 35.6 us: multipliers(): pl.pallas_call(body, grid_spec=pltpu.PrefetchScalarGridSpec(num_scalar_pr...]
    psum x2 -> x0, waiting for transfers between devices: 103 us -> none  [broadcast(): return lax.psum(kept, axis)]
    ppermute x0 -> x44, starting transfers between devices: none -> 100 us  [the longest x3 54.9 us: send(): return lax.ppermute(x, 'pcol', pairs)]
    all_gather x2 -> x0, waiting for transfers between devices: 81 us -> none  [the longest x1 81 us: on_device(): lax.all_gather(jnp.take(matrix, owned(step), axis=0), 'prow', axis=0, til...]
  transfers between devices with their start and end apart: 5 -> 44, of which waited for: 4 -> 10; matrix products, arithmetic and copies ran while one was open for 18% -> 0% of each run, Pallas kernels for 0% -> 28%
where the time goes in v1:
time: 381 us; the launch traced here: 380 us
  waiting for transfers between devices  158 us (41%)
  Pallas kernels  116 us (30%)
  starting transfers between devices  100 us (26%)
  local copies, waits for them, and re-layouts  4.17 us (1%)
    ppermute x6, waiting for transfers between devices, shift(): return lax.ppermute(x, 'pcol', [(i, (i + k) % devs) for i in range(devs)])  102 us
    ppermute x3, starting transfers between devices, send(): return lax.ppermute(x, 'pcol', pairs)  54.9 us
    ppermute x35, waiting for transfers between devices, across(): return lax.ppermute(x, 'prow', [(i, move(i)) for i in range(size)])  46.3 us
    pallas_call x1, Pallas kernels, multipliers(): pl.pallas_call(body, grid_spec=pltpu.PrefetchScalarGridSpec(num_scalar_pr...  35.6 us
    pallas_call x4, Pallas kernels, product(): pl.pallas_call(body, grid_spec=pltpu.PrefetchScalarGridSpec(num_scalar_pr...  32.1 us
    ppermute x6, starting transfers between devices, shift(): return lax.ppermute(x, 'pcol', [(i, (i + k) % devs) for i in range(devs)])  23.8 us
    pallas_call x4, Pallas kernels, finish(): pl.pallas_call(body, grid_spec=pltpu.PrefetchScalarGridSpec(num_scalar_pr...  22.9 us
    ppermute x35, starting transfers between devices, across(): return lax.ppermute(x, 'prow', [(i, move(i)) for i in range(size)])  21.7 us
  transfers between devices with their start and end apart: 44, of which 10 were waited for; matrix products, arithmetic and copies ran while one was open for 0% of the time, Pallas kernels for 28%

profile of v1, /device:TPU:0, one launch (start us, length us, event | category | flops | bytes accessed | tf_op | source)
XLA Modules:
  0.0 380.4 jit_solution(13634493925715070299)
XLA Ops:
  0.0 0.8 dynamic-slice_subtract_fusion
  0.8 0.8 reshape.4.idx_ref
  1.5 3.0 panel_rows.1
  4.5 3.0 collective-permute-start
  7.5 1.5 collective-permute-start.1
  9.0 0.7 stack.40.sc_ref
  9.7 4.8 %pick.7 = (f32[128,2048]{1,0:T(8,128)}, f32[128,2048]{1,0:T(8,128)}) custom-call(s32[10]{0:T(128)} %stack.40.sc_ref, bf16[256,256]{1,0:T(8,128)(2,1)} %get-tuple-element.36.s_ref, f32[256,8192]{1,0:T(8,128)} %refs_3_.7, f32[256,8192]{1,0:T(8,128)} %refs_3_.7, f32[256,8192]{1,0:T(8,128)} %refs_3_.7, f32[256,8192]{1,0:T(8,128)} %refs_3_.7), custom_call_target="tpu_custom_call" | custom-call | flops 805306368 | bytes 4194304 | tf_op jit(solution)/shard_map/pick/pallas_call | solution.py:97
  15.0 5.0 %collective-permute-done.refs_1_ = f32[128,1024]{1,0:T(8,128)S(1)} collective-permute-done((f32[128,1024]{1,0:T(8,128)}, f32[128,1024]{1,0:T(8,128)S(1)}, u32[]{:S(2)}, u32[]{:S(2)}) %collective-permute-start) | collective-permute-done | bytes 524320 | tf_op jit(solution)/shard_map/ppermute | solution.py:369
  20.0 2.5 collective-permute-start.2
  23.0 4.7 %pick.6 = (f32[128,2048]{1,0:T(8,128)}, f32[128,2048]{1,0:T(8,128)}) custom-call(s32[10]{0:T(128)} %stack.40.sc_ref, bf16[256,256]{1,0:T(8,128)(2,1)} %get-tuple-element.36.s_ref, f32[256,8192]{1,0:T(8,128)} %refs_3_.7, f32[256,8192]{1,0:T(8,128)} %refs_3_.7, f32[256,8192]{1,0:T(8,128)} %refs_3_.7, f32[256,8192]{1,0:T(8,128)} %refs_3_.7), custom_call_target="tpu_custom_call" | custom-call | flops 805306368 | bytes 4194304 | tf_op jit(solution)/shard_map/pick/pallas_call | solution.py:97
  27.7 4.8 %pick.5 = (f32[128,2048]{1,0:T(8,128)}, f32[128,2048]{1,0:T(8,128)}) custom-call(s32[10]{0:T(128)} %stack.40.sc_ref, bf16[256,256]{1,0:T(8,128)(2,1)} %get-tuple-element.36.s_ref, f32[256,8192]{1,0:T(8,128)} %refs_3_.7, f32[256,8192]{1,0:T(8,128)} %refs_3_.7, f32[256,8192]{1,0:T(8,128)} %refs_3_.7, f32[256,8192]{1,0:T(8,128)} %refs_3_.7), custom_call_target="tpu_custom_call" | custom-call | flops 805306368 | bytes 4194304 | tf_op jit(solution)/shard_map/pick/pallas_call | solution.py:97
  32.5 15.2 %collective-permute-done.2.refs_3_ = f32[128,1024]{1,0:T(8,128)S(1)} collective-permute-done((f32[128,1024]{1,0:T(8,128)S(1)}, f32[128,1024]{1,0:T(8,128)S(1)}, u32[]{:S(2)}, u32[]{:S(2)}) %collective-permute-start.2) | collective-permute-done | bytes 524320 | tf_op jit(solution)/shard_map/ppermute | solution.py:369
  47.7 0.6 collective-permute-start.40
  48.5 0.8 copy-done.33
  49.3 3.0 collective-permute-start.28
  52.4 3.9 %collective-permute-start.19 = (f32[128,2048]{1,0:T(8,128)}, f32[128,2048]{1,0:T(8,128)S(1)}, u32[]{:S(2)}, u32[]{:S(2)}) collective-permute-start(f32[128,2048]{1,0:T(8,128)} %get-tuple-element.41), channel_id=1, source_target_pairs={{0,3},{1,0},{2,1},{3,2},{4,7},{5,4},{6,5},{7,6},{8,11},{9,8},{10,9... | collective-permute-start | bytes 3145736 | tf_op jit(solution)/shard_map/ppermute | solution.py:409
  56.8 4.8 %pick.4 = (f32[128,2048]{1,0:T(8,128)}, f32[128,2048]{1,0:T(8,128)}) custom-call(s32[10]{0:T(128)} %stack.40.sc_ref, bf16[256,256]{1,0:T(8,128)(2,1)} %get-tuple-element.36.s_ref, f32[256,8192]{1,0:T(8,128)} %refs_3_.7, f32[256,8192]{1,0:T(8,128)} %refs_3_.7, f32[256,8192]{1,0:T(8,128)} %refs_3_.7, f32[256,8192]{1,0:T(8,128)} %refs_3_.7), custom_call_target="tpu_custom_call" | custom-call | flops 805306368 | bytes 4194304 | tf_op jit(solution)/shard_map/pick/pallas_call | solution.py:97
  61.5 1.4 collective-permute-start.10
  63.0 58.5 %collective-permute-done.28.refs_0_ = f32[128,2048]{1,0:T(8,128)S(1)} collective-permute-done((f32[128,2048]{1,0:T(8,128)}, f32[128,2048]{1,0:T(8,128)S(1)}, u32[]{:S(2)}, u32[]{:S(2)}) %collective-permute-start.28) | collective-permute-done | bytes 1048608 | tf_op jit(solution)/shard_map/ppermute | solution.py:409
  121.5 1.8 collective-permute-start.39
  123.3 20.7 %collective-permute-done.36.n_ref = f32[128,2048]{1,0:T(8,128)S(1)} collective-permute-done((f32[128,2048]{1,0:T(8,128)}, f32[128,2048]{1,0:T(8,128)S(1)}, u32[]{:S(2)}, u32[]{:S(2)}) %collective-permute-start.36) | collective-permute-done | bytes 1048608 | tf_op jit(solution)/shard_map/ppermute | solution.py:409
  144.7 23.1 %collective-permute-done.10.refs_0_ = f32[128,2048]{1,0:T(8,128)S(1)} collective-permute-done((f32[128,2048]{1,0:T(8,128)}, f32[128,2048]{1,0:T(8,128)S(1)}, u32[]{:S(2)}, u32[]{:S(2)}) %collective-permute-start.10) | collective-permute-done | bytes 1048608 | tf_op jit(solution)/shard_map/ppermute | solution.py:409
  167.7 1.5 collective-permute-start.29
  169.2 0.7 collective-permute-start.30
  170.9 1.3 collective-permute-start.21
  172.2 35.6 %multipliers.1 = (f32[160,1024]{1,0:T(8,128)}, f32[192,512]{1,0:T(8,128)}) custom-call(s32[10]{0:T(128)} %stack.40.sc_ref, f32[128,1024]{1,0:T(8,128)} %get-tuple-element.30.refs_0_, f32[128,1024]{1,0:T(8,128)} %copy-done.28, f32[128,1024]{1,0:T(8,128)} %copy-done.29, f32[128,1024]{1,0:T(8,128)} %copy-done.31, f32[128,1024]{1,0:T(8,128)} %copy-done.30, ...), custom_call_target="tpu_custom_call" | custom-call | flops 30000001024 | bytes 8388608 | tf_op jit(solution)/shard_map/multipliers/pallas_call | solution.py:214
  207.9 34.3 %collective-permute-start.7 = (f32[160,1024]{1,0:T(8,128)}, f32[160,1024]{1,0:T(8,128)S(1)}, u32[]{:S(2)}, u32[]{:S(2)}) collective-permute-start(f32[160,1024]{1,0:T(8,128)} %get-tuple-element.32.refs_0_), channel_id=1, source_target_pairs={{0,2},{4,6},{8,10},{12,14},{16,18},{20,22},{24,26},{28,30}} | collective-permute-start | bytes 1966088 | tf_op jit(solution)/shard_map/ppermute | solution.py:412
  242.3 1.6 collective-permute-start.11
  244.3 19.9 %collective-permute-start.8 = (f32[160,1024]{1,0:T(8,128)}, f32[160,1024]{1,0:T(8,128)S(1)}, u32[]{:S(2)}, u32[]{:S(2)}) collective-permute-start(f32[160,1024]{1,0:T(8,128)} %get-tuple-element.32.refs_0_), channel_id=1, source_target_pairs={{0,1},{4,5},{8,9},{12,13},{16,17},{20,21},{24,25},{28,29}} | collective-permute-start | bytes 1966088 | tf_op jit(solution)/shard_map/ppermute | solution.py:412
  264.3 0.7 collective-permute-start.9
  265.1 3.0 collective-permute-done.11.refs_1_
  268.2 9.8 %collective-permute-done.8.refs_2_ = f32[160,1024]{1,0:T(8,128)S(1)} collective-permute-done((f32[160,1024]{1,0:T(8,128)}, f32[160,1024]{1,0:T(8,128)S(1)}, u32[]{:S(2)}, u32[]{:S(2)}) %collective-permute-start.8) | collective-permute-done | bytes 655392 | tf_op jit(solution)/shard_map/ppermute | solution.py:412
  277.9 0.8 copy-done.26
  278.8 0.9 collective-permute-start.22
  280.0 3.0 collective-permute-done.31.refs_3_
  283.3 1.5 collective-permute-start.35
  284.8 9.5 %collective-permute-done.22.refs_3_ = f32[128,2048]{1,0:T(8,128)S(1)} collective-permute-done((f32[128,2048]{1,0:T(8,128)}, f32[128,2048]{1,0:T(8,128)S(1)}, u32[]{:S(2)}, u32[]{:S(2)}) %collective-permute-start.22) | collective-permute-done | bytes 1048608 | tf_op jit(solution)/shard_map/ppermute | solution.py:369
  295.0 10.6 %collective-permute-done.13.refs_3_ = f32[128,2048]{1,0:T(8,128)S(1)} collective-permute-done((f32[128,2048]{1,0:T(8,128)S(1)}, f32[128,2048]{1,0:T(8,128)S(1)}, u32[]{:S(2)}, u32[]{:S(2)}) %collective-permute-start.13) | collective-permute-done | bytes 1048608 | tf_op jit(solution)/shard_map/ppermute | solution.py:369
  306.6 3.7 settle.1
  310.3 15.0 %collective-permute-start.18 = (f32[128,2048]{1,0:T(8,128)}, f32[128,2048]{1,0:T(8,128)}, u32[]{:S(2)}, u32[]{:S(2)}) collective-permute-start(f32[128,2048]{1,0:T(8,128)} %get-tuple-element.40), channel_id=1, source_target_pairs={{0,1},{1,2},{2,3},{3,0},{4,5},{5,6},{6,7},{7,4},{8,9},{9,10},{10,1... | collective-permute-start | bytes 3145736 | tf_op jit(solution)/shard_map/ppermute | solution.py:409
  325.3 8.0 %product.7 = (f32[128,2048]{1,0:T(8,128)}, f32[128,2048]{1,0:T(8,128)}) custom-call(s32[10]{0:T(128)} %stack.40.sc_ref, bf16[384,1024]{1,0:T(8,128)(2,1)} %get-tuple-element.35.lh_ref, f32[192,512]{1,0:T(8,128)} %get-tuple-element.34.fixed_ref, f32[128,2048]{1,0:T(8,128)} %get-tuple-element.49.refs_0_, f32[128,2048]{1,0:T(8,128)} %copy-done.1, ...), custom_call_target="tpu_custom_call" | custom-call | flops 2415919104 | bytes 10485760 | tf_op jit(solution)/shard_map/product/pallas_call | solution.py:307
  333.3 5.7 %finish.4.refs_0_ = f32[256,8192]{1,0:T(8,128)} custom-call(s32[10]{0:T(128)} %stack.40.sc_ref, bf16[256,256]{1,0:T(8,128)(2,1)} %get-tuple-element.29.st_ref, f32[192,512]{1,0:T(8,128)} %get-tuple-element.34.fixed_ref, f32[128,2048]{1,0:T(8,128)} %get-tuple-element.50.d_ref, f32[128,2048]{1,0:T(8,128)} %get-tuple-element.51.p_ref, ...), custom_call_target="tpu_custom_call" | custom-call | flops 805306368 | bytes 3145728 | tf_op jit(solution)/shard_map/finish/pallas_call | solution.py:351
  339.1 8.1 %product.6 = (f32[128,2048]{1,0:T(8,128)}, f32[128,2048]{1,0:T(8,128)}) custom-call(s32[10]{0:T(128)} %stack.40.sc_ref, bf16[384,1024]{1,0:T(8,128)(2,1)} %get-tuple-element.35.lh_ref, f32[192,512]{1,0:T(8,128)} %get-tuple-element.34.fixed_ref, f32[128,2048]{1,0:T(8,128)} %copy-done.7, f32[128,2048]{1,0:T(8,128)} %collective-permute-done.29.refs_1_, ...), custom_call_target="tpu_custom_call" | custom-call | flops 2415919104 | bytes 10485760 | tf_op jit(solution)/shard_map/product/pallas_call | solution.py:307
  347.2 5.7 %finish.5.refs_0_ = f32[256,8192]{1,0:T(8,128)} custom-call(s32[10]{0:T(128)} %stack.40.sc_ref, bf16[256,256]{1,0:T(8,128)(2,1)} %get-tuple-element.29.st_ref, f32[192,512]{1,0:T(8,128)} %get-tuple-element.34.fixed_ref, f32[128,2048]{1,0:T(8,128)} %get-tuple-element.46.d_ref, f32[128,2048]{1,0:T(8,128)} %get-tuple-element.47.p_ref, ...), custom_call_target="tpu_custom_call", output_to_operand_aliasing={{}: (6, {})} | custom-call | flops 805306368 | bytes 3145728 | tf_op jit(solution)/shard_map/finish/pallas_call | solution.py:351
  352.9 8.0 %product.5 = (f32[128,2048]{1,0:T(8,128)}, f32[128,2048]{1,0:T(8,128)}) custom-call(s32[10]{0:T(128)} %stack.40.sc_ref, bf16[384,1024]{1,0:T(8,128)(2,1)} %get-tuple-element.35.lh_ref, f32[192,512]{1,0:T(8,128)} %get-tuple-element.34.fixed_ref, f32[128,2048]{1,0:T(8,128)} %copy-done.6, f32[128,2048]{1,0:T(8,128)} %collective-permute-done.20.refs_1_, ...), custom_call_target="tpu_custom_call" | custom-call | flops 2415919104 | bytes 10485760 | tf_op jit(solution)/shard_map/product/pallas_call | solution.py:307
  360.9 5.7 %finish.6.refs_0_ = f32[256,8192]{1,0:T(8,128)} custom-call(s32[10]{0:T(128)} %stack.40.sc_ref, bf16[256,256]{1,0:T(8,128)(2,1)} %get-tuple-element.29.st_ref, f32[192,512]{1,0:T(8,128)} %get-tuple-element.34.fixed_ref, f32[128,2048]{1,0:T(8,128)} %get-tuple-element.42.d_ref, f32[128,2048]{1,0:T(8,128)} %get-tuple-element.43.p_ref, ...), custom_call_target="tpu_custom_call", output_to_operand_aliasing={{}: (6, {})} | custom-call | flops 805306368 | bytes 3145728 | tf_op jit(solution)/shard_map/finish/pallas_call | solution.py:351
  366.6 8.0 %product.4 = (f32[128,2048]{1,0:T(8,128)}, f32[128,2048]{1,0:T(8,128)}) custom-call(s32[10]{0:T(128)} %stack.40.sc_ref, bf16[384,1024]{1,0:T(8,128)(2,1)} %get-tuple-element.35.lh_ref, f32[192,512]{1,0:T(8,128)} %get-tuple-element.34.fixed_ref, f32[128,2048]{1,0:T(8,128)} %copy-done.3, f32[128,2048]{1,0:T(8,128)} %copy-done.13, f32[128,2048]{1,0:T(8,128)} %copy-done.14, ...), custom_call_target="tpu_custom_call" | custom-call | flops 2415919104 | bytes 10485760 | tf_op jit(solution)/shard_map/product/pallas_call | solution.py:307
  374.7 5.7 %finish.7 = f32[256,8192]{1,0:T(8,128)} custom-call(s32[10]{0:T(128)} %stack.40.sc_ref, bf16[256,256]{1,0:T(8,128)(2,1)} %get-tuple-element.29.st_ref, f32[192,512]{1,0:T(8,128)} %get-tuple-element.34.fixed_ref, f32[128,2048]{1,0:T(8,128)} %get-tuple-element.38.d_ref, f32[128,2048]{1,0:T(8,128)} %get-tuple-element.39.p_ref, ...), custom_call_target="tpu_custom_call", output_to_operand_aliasing={{}: (6, {})} | custom-call | flops 805306368 | bytes 3145728 | tf_op jit(solution)/shard_map/finish/pallas_call | solution.py:351
  (130 shorter events, 6.5 us)
Async XLA Ops:
  4.5 15.5 %collective-permute-start = (f32[128,1024]{1,0:T(8,128)}, f32[128,1024]{1,0:T(8,128)S(1)}, u32[]{:S(2)}, u32[]{:S(2)}) collective-permute-start(f32[128,1024]{1,0:T(8,128)} %get-tuple-element.30.refs_0_), channel_id=1, source_target_pairs={{0,8},{4,20},{8,0},{12,28},{16,24},{20,4},{24,16},{28,12},{1,9},{5... | collective-permute-start | bytes 1572872 | tf_op jit(solution)/shard_map/ppermute | solution.py:369
  7.5 15.0 %collective-permute-start.1 = (f32[128,1024]{1,0:T(8,128)}, f32[128,1024]{1,0:T(8,128)S(1)}, u32[]{:S(2)}, u32[]{:S(2)}) collective-permute-start(f32[128,1024]{1,0:T(8,128)} %get-tuple-element.30.refs_0_), channel_id=1, source_target_pairs={{0,16},{4,12},{8,24},{12,4},{16,0},{20,28},{24,8},{28,20},{1,17},{... | collective-permute-start | bytes 1572872 | tf_op jit(solution)/shard_map/ppermute | solution.py:369
  9.0 13.5 %collective-permute-start.3 = (f32[128,1024]{1,0:T(8,128)}, f32[128,1024]{1,0:T(8,128)S(1)}, u32[]{:S(2)}, u32[]{:S(2)}) collective-permute-start(f32[128,1024]{1,0:T(8,128)} %get-tuple-element.30.refs_0_), channel_id=1, source_target_pairs={{0,4},{4,0},{8,12},{12,8},{16,20},{20,16},{24,28},{28,24},{1,5},{5... | collective-permute-start | bytes 1572872 | tf_op jit(solution)/shard_map/ppermute | solution.py:369
  14.4 38.0 %collective-permute-start.37 = (f32[128,2048]{1,0:T(8,128)}, f32[128,2048]{1,0:T(8,128)S(1)}, u32[]{:S(2)}, u32[]{:S(2)}) collective-permute-start(f32[128,2048]{1,0:T(8,128)} %get-tuple-element.49.refs_0_), channel_id=1, source_target_pairs={{0,8},{4,20},{8,0},{12,28},{16,24},{20,4},{24,16},{28,12},{1,9},{5... | collective-permute-start | bytes 3145736 | tf_op jit(solution)/shard_map/ppermute | solution.py:369
  15.0 41.3 %collective-permute-start.38 = (f32[128,2048]{1,0:T(8,128)}, f32[128,2048]{1,0:T(8,128)S(1)}, u32[]{:S(2)}, u32[]{:S(2)}) collective-permute-start(f32[128,2048]{1,0:T(8,128)} %get-tuple-element.49.refs_0_), channel_id=1, source_target_pairs={{0,16},{4,12},{8,24},{12,4},{16,0},{20,28},{24,8},{28,20},{1,17},{... | collective-permute-start | bytes 3145736 | tf_op jit(solution)/shard_map/ppermute | solution.py:369
  20.0 27.7 %collective-permute-start.2 = (f32[128,1024]{1,0:T(8,128)S(1)}, f32[128,1024]{1,0:T(8,128)S(1)}, u32[]{:S(2)}, u32[]{:S(2)}) collective-permute-start(f32[128,1024]{1,0:T(8,128)S(1)} %collective-permute-done.refs_1_), channel_id=1, source_target_pairs={{0,16},{4,12},{8,24},{12,4},{16,0},{20,28},{24,8},{28,20},{1,17},{... | collective-permute-start | bytes 1572872 | tf_op jit(solution)/shard_map/ppermute | solution.py:369
  22.5 25.9 %collective-permute-start.4 = (f32[128,1024]{1,0:T(8,128)S(1)}, f32[128,1024]{1,0:T(8,128)S(1)}, u32[]{:S(2)}, u32[]{:S(2)}) collective-permute-start(f32[128,1024]{1,0:T(8,128)S(1)} %collective-permute-done.refs_1_), channel_id=1, source_target_pairs={{0,4},{4,0},{8,12},{12,8},{16,20},{20,16},{24,28},{28,24},{1,5},{5... | collective-permute-start | bytes 1572872 | tf_op jit(solution)/shard_map/ppermute | solution.py:369
  22.5 29.8 %collective-permute-start.5 = (f32[128,1024]{1,0:T(8,128)S(1)}, f32[128,1024]{1,0:T(8,128)S(1)}, u32[]{:S(2)}, u32[]{:S(2)}) collective-permute-start(f32[128,1024]{1,0:T(8,128)S(1)} %collective-permute-done.1.refs_2_), channel_id=1, source_target_pairs={{0,4},{4,0},{8,12},{12,8},{16,20},{20,16},{24,28},{28,24},{1,5},{5... | collective-permute-start | bytes 1572872 | tf_op jit(solution)/shard_map/ppermute | solution.py:369
  47.7 13.8 %collective-permute-start.40 = (f32[128,2048]{1,0:T(8,128)S(1)}, f32[128,2048]{1,0:T(8,128)}, u32[]{:S(2)}, u32[]{:S(2)}) collective-permute-start(f32[128,2048]{1,0:T(8,128)S(1)} %copy-done), channel_id=1, source_target_pairs={{0,4},{4,0},{8,12},{12,8},{16,20},{20,16},{24,28},{28,24},{1,5},{5... | collective-permute-start | bytes 3145736 | tf_op jit(solution)/shard_map/ppermute | solution.py:369
  49.3 72.1 %collective-permute-start.28 = (f32[128,2048]{1,0:T(8,128)}, f32[128,2048]{1,0:T(8,128)S(1)}, u32[]{:S(2)}, u32[]{:S(2)}) collective-permute-start(f32[128,2048]{1,0:T(8,128)} %get-tuple-element.45), channel_id=1, source_target_pairs={{0,2},{1,3},{2,0},{3,1},{4,6},{5,7},{6,4},{7,5},{8,10},{9,11},{10,... | collective-permute-start | bytes 3145736 | tf_op jit(solution)/shard_map/ppermute | solution.py:409
  52.3 91.6 %collective-permute-start.36 = (f32[128,2048]{1,0:T(8,128)}, f32[128,2048]{1,0:T(8,128)S(1)}, u32[]{:S(2)}, u32[]{:S(2)}) collective-permute-start(f32[128,2048]{1,0:T(8,128)} %get-tuple-element.48), channel_id=1, source_target_pairs={{0,2},{1,3},{2,0},{3,1},{4,6},{5,7},{6,4},{7,5},{8,10},{9,11},{10,... | collective-permute-start | bytes 3145736 | tf_op jit(solution)/shard_map/ppermute | solution.py:409
  52.4 91.6 %collective-permute-start.19 = (f32[128,2048]{1,0:T(8,128)}, f32[128,2048]{1,0:T(8,128)S(1)}, u32[]{:S(2)}, u32[]{:S(2)}) collective-permute-start(f32[128,2048]{1,0:T(8,128)} %get-tuple-element.41), channel_id=1, source_target_pairs={{0,3},{1,0},{2,1},{3,2},{4,7},{5,4},{6,5},{7,6},{8,11},{9,8},{10,9... | collective-permute-start | bytes 3145736 | tf_op jit(solution)/shard_map/ppermute | solution.py:409
  56.3 88.3 %collective-permute-start.27 = (f32[128,2048]{1,0:T(8,128)}, f32[128,2048]{1,0:T(8,128)S(1)}, u32[]{:S(2)}, u32[]{:S(2)}) collective-permute-start(f32[128,2048]{1,0:T(8,128)} %get-tuple-element.44), channel_id=1, source_target_pairs={{0,3},{1,0},{2,1},{3,2},{4,7},{5,4},{6,5},{7,6},{8,11},{9,8},{10,9... | collective-permute-start | bytes 3145736 | tf_op jit(solution)/shard_map/ppermute | solution.py:409
  61.5 106.2 %collective-permute-start.10 = (f32[128,2048]{1,0:T(8,128)}, f32[128,2048]{1,0:T(8,128)S(1)}, u32[]{:S(2)}, u32[]{:S(2)}) collective-permute-start(f32[128,2048]{1,0:T(8,128)} %get-tuple-element.37), channel_id=1, source_target_pairs={{0,1},{1,2},{2,3},{3,0},{4,5},{5,6},{6,7},{7,4},{8,9},{9,10},{10,1... | collective-permute-start | bytes 3145736 | tf_op jit(solution)/shard_map/ppermute | solution.py:409
  121.5 48.4 %collective-permute-start.39 = (f32[128,2048]{1,0:T(8,128)S(1)}, f32[128,2048]{1,0:T(8,128)S(1)}, u32[]{:S(2)}, u32[]{:S(2)}) collective-permute-start(f32[128,2048]{1,0:T(8,128)S(1)} %collective-permute-done.37.refs_1_), channel_id=1, source_target_pairs={{0,16},{4,12},{8,24},{12,4},{16,0},{20,28},{24,8},{28,20},{1,17},{... | collective-permute-start | bytes 3145736 | tf_op jit(solution)/shard_map/ppermute | solution.py:369
  143.9 26.0 %collective-permute-start.41 = (f32[128,2048]{1,0:T(8,128)S(1)}, f32[128,2048]{1,0:T(8,128)S(1)}, u32[]{:S(2)}, u32[]{:S(2)}) collective-permute-start(f32[128,2048]{1,0:T(8,128)S(1)} %collective-permute-done.37.refs_1_), channel_id=1, source_target_pairs={{0,4},{4,0},{8,12},{12,8},{16,20},{20,16},{24,28},{28,24},{1,5},{5... | collective-permute-start | bytes 3145736 | tf_op jit(solution)/shard_map/ppermute | solution.py:369
  144.0 98.2 %copy-start.6 = (f32[128,2048]{1,0:T(8,128)}, f32[128,2048]{1,0:T(8,128)S(1)}, u32[]{:S(2)}) copy-start(f32[128,2048]{1,0:T(8,128)S(1)} %collective-permute-done.19.refs_0_) | copy-start | bytes 3145732
  144.0 26.5 %collective-permute-start.42 = (f32[128,2048]{1,0:T(8,128)S(1)}, f32[128,2048]{1,0:T(8,128)S(1)}, u32[]{:S(2)}, u32[]{:S(2)}) collective-permute-start(f32[128,2048]{1,0:T(8,128)S(1)} %collective-permute-done.38.refs_2_), channel_id=1, source_target_pairs={{0,4},{4,0},{8,12},{12,8},{16,20},{20,16},{24,28},{28,24},{1,5},{5... | collective-permute-start | bytes 3145736 | tf_op jit(solution)/shard_map/ppermute | solution.py:369
  144.5 24.7 %collective-permute-start.6 = (f32[128,1024]{1,0:T(8,128)S(1)}, f32[128,1024]{1,0:T(8,128)S(1)}, u32[]{:S(2)}, u32[]{:S(2)}) collective-permute-start(f32[128,1024]{1,0:T(8,128)S(1)} %copy-done.32), channel_id=1, source_target_pairs={{0,4},{4,0},{8,12},{12,8},{16,20},{20,16},{24,28},{28,24},{1,5},{5... | collective-permute-start | bytes 1572872 | tf_op jit(solution)/shard_map/ppermute | solution.py:369
  167.7 126.6 %copy-start.3 = (f32[128,2048]{1,0:T(8,128)}, f32[128,2048]{1,0:T(8,128)S(1)}, u32[]{:S(2)}) copy-start(f32[128,2048]{1,0:T(8,128)S(1)} %collective-permute-done.10.refs_0_) | copy-start | bytes 3145732
  167.7 40.1 %collective-permute-start.29 = (f32[128,2048]{1,0:T(8,128)S(1)}, f32[128,2048]{1,0:T(8,128)}, u32[]{:S(2)}, u32[]{:S(2)}) collective-permute-start(f32[128,2048]{1,0:T(8,128)S(1)} %collective-permute-done.28.refs_0_), channel_id=1, source_target_pairs={{0,8},{4,20},{8,0},{12,28},{16,24},{20,4},{24,16},{28,12},{1,9},{5... | collective-permute-start | bytes 3145736 | tf_op jit(solution)/shard_map/ppermute | solution.py:369
  169.2 73.0 %collective-permute-start.30 = (f32[128,2048]{1,0:T(8,128)S(1)}, f32[128,2048]{1,0:T(8,128)}, u32[]{:S(2)}, u32[]{:S(2)}) collective-permute-start(f32[128,2048]{1,0:T(8,128)S(1)} %collective-permute-done.28.refs_0_), channel_id=1, source_target_pairs={{0,16},{4,12},{8,24},{12,4},{16,0},{20,28},{24,8},{28,20},{1,17},{... | collective-permute-start | bytes 3145736 | tf_op jit(solution)/shard_map/ppermute | solution.py:369
  169.9 72.4 %collective-permute-start.32 = (f32[128,2048]{1,0:T(8,128)S(1)}, f32[128,2048]{1,0:T(8,128)}, u32[]{:S(2)}, u32[]{:S(2)}) collective-permute-start(f32[128,2048]{1,0:T(8,128)S(1)} %collective-permute-done.28.refs_0_), channel_id=1, source_target_pairs={{0,4},{4,0},{8,12},{12,8},{16,20},{20,16},{24,28},{28,24},{1,5},{5... | collective-permute-start | bytes 3145736 | tf_op jit(solution)/shard_map/ppermute | solution.py:369
  169.9 73.9 %collective-permute-start.20 = (f32[128,2048]{1,0:T(8,128)S(1)}, f32[128,2048]{1,0:T(8,128)}, u32[]{:S(2)}, u32[]{:S(2)}) collective-permute-start(f32[128,2048]{1,0:T(8,128)S(1)} %collective-permute-done.19.refs_0_), channel_id=1, source_target_pairs={{0,8},{4,20},{8,0},{12,28},{16,24},{20,4},{24,16},{28,12},{1,9},{5... | collective-permute-start | bytes 3145736 | tf_op jit(solution)/shard_map/ppermute | solution.py:369
  170.9 73.4 %collective-permute-start.21 = (f32[128,2048]{1,0:T(8,128)S(1)}, f32[128,2048]{1,0:T(8,128)S(1)}, u32[]{:S(2)}, u32[]{:S(2)}) collective-permute-start(f32[128,2048]{1,0:T(8,128)S(1)} %collective-permute-done.19.refs_0_), channel_id=1, source_target_pairs={{0,16},{4,12},{8,24},{12,4},{16,0},{20,28},{24,8},{28,20},{1,17},{... | collective-permute-start | bytes 3145736 | tf_op jit(solution)/shard_map/ppermute | solution.py:369
  172.2 92.7 %copy-start.9 = (f32[128,2048]{1,0:T(8,128)S(1)}, f32[128,2048]{1,0:T(8,128)}, u32[]{:S(2)}) copy-start(f32[128,2048]{1,0:T(8,128)} %copy-done.8) | copy-start | bytes 3145732
  207.9 56.4 %collective-permute-start.7 = (f32[160,1024]{1,0:T(8,128)}, f32[160,1024]{1,0:T(8,128)S(1)}, u32[]{:S(2)}, u32[]{:S(2)}) collective-permute-start(f32[160,1024]{1,0:T(8,128)} %get-tuple-element.32.refs_0_), channel_id=1, source_target_pairs={{0,2},{4,6},{8,10},{12,14},{16,18},{20,22},{24,26},{28,30}} | collective-permute-start | bytes 1966088 | tf_op jit(solution)/shard_map/ppermute | solution.py:412
  242.2 22.8 %collective-permute-start.23 = (f32[128,2048]{1,0:T(8,128)S(1)}, f32[128,2048]{1,0:T(8,128)S(1)}, u32[]{:S(2)}, u32[]{:S(2)}) collective-permute-start(f32[128,2048]{1,0:T(8,128)S(1)} %collective-permute-done.19.refs_0_), channel_id=1, source_target_pairs={{0,4},{4,0},{8,12},{12,8},{16,20},{20,16},{24,28},{28,24},{1,5},{5... | collective-permute-start | bytes 3145736 | tf_op jit(solution)/shard_map/ppermute | solution.py:369
  242.3 25.8 %collective-permute-start.11 = (f32[128,2048]{1,0:T(8,128)S(1)}, f32[128,2048]{1,0:T(8,128)S(1)}, u32[]{:S(2)}, u32[]{:S(2)}) collective-permute-start(f32[128,2048]{1,0:T(8,128)S(1)} %collective-permute-done.10.refs_0_), channel_id=1, source_target_pairs={{0,8},{4,20},{8,0},{12,28},{16,24},{20,4},{24,16},{28,12},{1,9},{5... | collective-permute-start | bytes 3145736 | tf_op jit(solution)/shard_map/ppermute | solution.py:369
  243.9 24.3 %collective-permute-start.12 = (f32[128,2048]{1,0:T(8,128)S(1)}, f32[128,2048]{1,0:T(8,128)S(1)}, u32[]{:S(2)}, u32[]{:S(2)}) collective-permute-start(f32[128,2048]{1,0:T(8,128)S(1)} %collective-permute-done.10.refs_0_), channel_id=1, source_target_pairs={{0,16},{4,12},{8,24},{12,4},{16,0},{20,28},{24,8},{28,20},{1,17},{... | collective-permute-start | bytes 3145736 | tf_op jit(solution)/shard_map/ppermute | solution.py:369
  244.3 94.7 %copy-start.12 = (f32[128,2048]{1,0:T(8,128)}, f32[128,2048]{1,0:T(8,128)S(1)}, u32[]{:S(2)}) copy-start(f32[128,2048]{1,0:T(8,128)S(1)} %collective-permute-done.21.refs_2_) | copy-start | bytes 3145732
  244.3 33.6 %collective-permute-start.8 = (f32[160,1024]{1,0:T(8,128)}, f32[160,1024]{1,0:T(8,128)S(1)}, u32[]{:S(2)}, u32[]{:S(2)}) collective-permute-start(f32[160,1024]{1,0:T(8,128)} %get-tuple-element.32.refs_0_), channel_id=1, source_target_pairs={{0,1},{4,5},{8,9},{12,13},{16,17},{20,21},{24,25},{28,29}} | collective-permute-start | bytes 1966088 | tf_op jit(solution)/shard_map/ppermute | solution.py:412
  264.3 14.5 %collective-permute-start.9 = (f32[160,1024]{1,0:T(8,128)S(1)}, f32[160,1024]{1,0:T(8,128)S(1)}, u32[]{:S(2)}, u32[]{:S(2)}) collective-permute-start(f32[160,1024]{1,0:T(8,128)S(1)} %collective-permute-done.7.refs_1_), channel_id=1, source_target_pairs={{2,3},{6,7},{10,11},{14,15},{18,19},{22,23},{26,27},{30,31}} | collective-permute-start | bytes 1966088 | tf_op jit(solution)/shard_map/ppermute | solution.py:412
  265.0 14.7 %collective-permute-start.43 = (f32[128,2048]{1,0:T(8,128)S(1)}, f32[128,2048]{1,0:T(8,128)S(1)}, u32[]{:S(2)}, u32[]{:S(2)}) collective-permute-start(f32[128,2048]{1,0:T(8,128)S(1)} %copy-done.9), channel_id=1, source_target_pairs={{0,4},{4,0},{8,12},{12,8},{16,20},{20,16},{24,28},{28,24},{1,5},{5... | collective-permute-start | bytes 3145736 | tf_op jit(solution)/shard_map/ppermute | solution.py:369
  268.1 15.0 %collective-permute-start.31 = (f32[128,2048]{1,0:T(8,128)}, f32[128,2048]{1,0:T(8,128)S(1)}, u32[]{:S(2)}, u32[]{:S(2)}) collective-permute-start(f32[128,2048]{1,0:T(8,128)} %collective-permute-done.29.refs_1_), channel_id=1, source_target_pairs={{0,16},{4,12},{8,24},{12,4},{16,0},{20,28},{24,8},{28,20},{1,17},{... | collective-permute-start | bytes 3145736 | tf_op jit(solution)/shard_map/ppermute | solution.py:369
  268.2 14.9 %collective-permute-start.33 = (f32[128,2048]{1,0:T(8,128)}, f32[128,2048]{1,0:T(8,128)S(1)}, u32[]{:S(2)}, u32[]{:S(2)}) collective-permute-start(f32[128,2048]{1,0:T(8,128)} %collective-permute-done.29.refs_1_), channel_id=1, source_target_pairs={{0,4},{4,0},{8,12},{12,8},{16,20},{20,16},{24,28},{28,24},{1,5},{5... | collective-permute-start | bytes 3145736 | tf_op jit(solution)/shard_map/ppermute | solution.py:369
  277.9 5.3 %collective-permute-start.34 = (f32[128,2048]{1,0:T(8,128)}, f32[128,2048]{1,0:T(8,128)S(1)}, u32[]{:S(2)}, u32[]{:S(2)}) collective-permute-start(f32[128,2048]{1,0:T(8,128)} %collective-permute-done.30.refs_2_), channel_id=1, source_target_pairs={{0,4},{4,0},{8,12},{12,8},{16,20},{20,16},{24,28},{28,24},{1,5},{5... | collective-permute-start | bytes 3145736 | tf_op jit(solution)/shard_map/ppermute | solution.py:369
  278.8 15.5 %collective-permute-start.22 = (f32[128,2048]{1,0:T(8,128)}, f32[128,2048]{1,0:T(8,128)S(1)}, u32[]{:S(2)}, u32[]{:S(2)}) collective-permute-start(f32[128,2048]{1,0:T(8,128)} %collective-permute-done.20.refs_1_), channel_id=1, source_target_pairs={{0,16},{4,12},{8,24},{12,4},{16,0},{20,28},{24,8},{28,20},{1,17},{... | collective-permute-start | bytes 3145736 | tf_op jit(solution)/shard_map/ppermute | solution.py:369
  279.7 14.6 %collective-permute-start.24 = (f32[128,2048]{1,0:T(8,128)}, f32[128,2048]{1,0:T(8,128)S(1)}, u32[]{:S(2)}, u32[]{:S(2)}) collective-permute-start(f32[128,2048]{1,0:T(8,128)} %collective-permute-done.20.refs_1_), channel_id=1, source_target_pairs={{0,4},{4,0},{8,12},{12,8},{16,20},{20,16},{24,28},{28,24},{1,5},{5... | collective-permute-start | bytes 3145736 | tf_op jit(solution)/shard_map/ppermute | solution.py:369
  283.1 11.8 %collective-permute-start.25 = (f32[128,2048]{1,0:T(8,128)S(1)}, f32[128,2048]{1,0:T(8,128)S(1)}, u32[]{:S(2)}, u32[]{:S(2)}) collective-permute-start(f32[128,2048]{1,0:T(8,128)S(1)} %collective-permute-done.21.refs_2_), channel_id=1, source_target_pairs={{0,4},{4,0},{8,12},{12,8},{16,20},{20,16},{24,28},{28,24},{1,5},{5... | collective-permute-start | bytes 3145736 | tf_op jit(solution)/shard_map/ppermute | solution.py:369
  283.1 22.4 %collective-permute-start.13 = (f32[128,2048]{1,0:T(8,128)S(1)}, f32[128,2048]{1,0:T(8,128)S(1)}, u32[]{:S(2)}, u32[]{:S(2)}) collective-permute-start(f32[128,2048]{1,0:T(8,128)S(1)} %collective-permute-done.11.refs_1_), channel_id=1, source_target_pairs={{0,16},{4,12},{8,24},{12,4},{16,0},{20,28},{24,8},{28,20},{1,17},{... | collective-permute-start | bytes 3145736 | tf_op jit(solution)/shard_map/ppermute | solution.py:369
  283.3 22.3 %collective-permute-start.35 = (f32[128,2048]{1,0:T(8,128)S(1)}, f32[128,2048]{1,0:T(8,128)S(1)}, u32[]{:S(2)}, u32[]{:S(2)}) collective-permute-start(f32[128,2048]{1,0:T(8,128)S(1)} %collective-permute-done.31.refs_3_), channel_id=1, source_target_pairs={{0,4},{4,0},{8,12},{12,8},{16,20},{20,16},{24,28},{28,24},{1,5},{5... | collective-permute-start | bytes 3145736 | tf_op jit(solution)/shard_map/ppermute | solution.py:369
  294.3 16.0 %collective-permute-start.26 = (f32[128,2048]{1,0:T(8,128)S(1)}, f32[128,2048]{1,0:T(8,128)}, u32[]{:S(2)}, u32[]{:S(2)}) collective-permute-start(f32[128,2048]{1,0:T(8,128)S(1)} %collective-permute-done.22.refs_3_), channel_id=1, source_target_pairs={{0,4},{4,0},{8,12},{12,8},{16,20},{20,16},{24,28},{28,24},{1,5},{5... | collective-permute-start | bytes 3145736 | tf_op jit(solution)/shard_map/ppermute | solution.py:369
  294.3 72.3 %collective-permute-start.14 = (f32[128,2048]{1,0:T(8,128)S(1)}, f32[128,2048]{1,0:T(8,128)}, u32[]{:S(2)}, u32[]{:S(2)}) collective-permute-start(f32[128,2048]{1,0:T(8,128)S(1)} %collective-permute-done.10.refs_0_), channel_id=1, source_target_pairs={{0,4},{4,0},{8,12},{12,8},{16,20},{20,16},{24,28},{28,24},{1,5},{5... | collective-permute-start | bytes 3145736 | tf_op jit(solution)/shard_map/ppermute | solution.py:369
  294.9 71.7 %collective-permute-start.15 = (f32[128,2048]{1,0:T(8,128)S(1)}, f32[128,2048]{1,0:T(8,128)}, u32[]{:S(2)}, u32[]{:S(2)}) collective-permute-start(f32[128,2048]{1,0:T(8,128)S(1)} %collective-permute-done.11.refs_1_), channel_id=1, source_target_pairs={{0,4},{4,0},{8,12},{12,8},{16,20},{20,16},{24,28},{28,24},{1,5},{5... | collective-permute-start | bytes 3145736 | tf_op jit(solution)/shard_map/ppermute | solution.py:369
  305.5 61.1 %collective-permute-start.16 = (f32[128,2048]{1,0:T(8,128)S(1)}, f32[128,2048]{1,0:T(8,128)}, u32[]{:S(2)}, u32[]{:S(2)}) collective-permute-start(f32[128,2048]{1,0:T(8,128)S(1)} %collective-permute-done.12.refs_2_), channel_id=1, source_target_pairs={{0,4},{4,0},{8,12},{12,8},{16,20},{20,16},{24,28},{28,24},{1,5},{5... | collective-permute-start | bytes 3145736 | tf_op jit(solution)/shard_map/ppermute | solution.py:369
  305.6 61.0 %collective-permute-start.17 = (f32[128,2048]{1,0:T(8,128)S(1)}, f32[128,2048]{1,0:T(8,128)}, u32[]{:S(2)}, u32[]{:S(2)}) collective-permute-start(f32[128,2048]{1,0:T(8,128)S(1)} %collective-permute-done.13.refs_3_), channel_id=1, source_target_pairs={{0,4},{4,0},{8,12},{12,8},{16,20},{20,16},{24,28},{28,24},{1,5},{5... | collective-permute-start | bytes 3145736 | tf_op jit(solution)/shard_map/ppermute | solution.py:369
  310.3 64.4 %collective-permute-start.18 = (f32[128,2048]{1,0:T(8,128)}, f32[128,2048]{1,0:T(8,128)}, u32[]{:S(2)}, u32[]{:S(2)}) collective-permute-start(f32[128,2048]{1,0:T(8,128)} %get-tuple-element.40), channel_id=1, source_target_pairs={{0,1},{1,2},{2,3},{3,0},{4,5},{5,6},{6,7},{7,4},{8,9},{9,10},{10,1... | collective-permute-start | bytes 3145736 | tf_op jit(solution)/shard_map/ppermute | solution.py:409
  (32 other events, 989.2 us)

commit v2 on v1

--- a/solution.py
+++ b/solution.py
@@ -47,66 +47,52 @@
     return pltpu.CompilerParams(dimension_semantics=("arbitrary",) * n, vmem_limit_bytes=56 << 20)
 
 
-def panel_rows(pidx, skeleton):
+def pick(scalars, onehot, skeleton, columns, piv, own=None):
     rows = skeleton.shape[0]
-    piv = pidx.shape[0]
     rest = rows - piv
-    width = 2 * NB
-
-    def body(idx_ref, x_ref, s_ref, st_ref, gp_ref, gn_ref):
-        col = lax.broadcasted_iota(jnp.int32, (piv, rows), 1)
-        sp = (col == idx_ref[...]).astype(f32)
+    per = len(columns)
+    make = own is not None
+
+    def order(own_ref, s_ref, st_ref):
+        share = piv // 2
+        line = lax.broadcasted_iota(jnp.int32, (rows, share), 0)
+        chosen = jnp.concatenate([(line == own_ref[t : t + 1, :]).astype(f32) for t in range(2)], axis=1)
+        sp = chosen.T
         free = 1.0 - jnp.sum(sp, axis=0, keepdims=True)
         before = lax.broadcasted_iota(jnp.int32, (rows, rows), 0) < lax.broadcasted_iota(jnp.int32, (rows, rows), 1)
         rank = dot(jnp.broadcast_to(free, (8, rows)).astype(bf16), before.astype(f32).astype(bf16))[0:1]
-        place = lax.broadcasted_iota(jnp.int32, (rest, rows), 0).astype(f32)
-        sn = jnp.where(rank == place, free, 0.0)
-        onehot = jnp.concatenate([sp, sn], axis=0)
-        st_ref[...] = onehot.T.astype(bf16)
-        s_ref[...] = onehot.astype(bf16)
-        x = select(onehot.astype(bf16), x_ref[...])
-        gp_ref[...] = x[0:piv]
-        gn_ref[...] = x[piv:]
-
-    full = lambda shape: pl.BlockSpec(shape, lambda i: (0, 0))
-    shapes = [((rows, rows), bf16), ((rows, rows), bf16), ((piv, width), f32), ((rest, width), f32)]
-    return pl.pallas_call(
-        body,
-        grid=(1,),
-        in_specs=[full((piv, 1)), full((rows, width))],
-        out_specs=[full(s) for s, _ in shapes],
-        out_shape=[jax.ShapeDtypeStruct(s, d) for s, d in shapes],
-        compiler_params=params(1),
-        cost_estimate=cost(6 * rows * rows * width, 8 * rows * width),
-        name="panel_rows",
-    )(pidx, skeleton)
-
-
-def pick(scalars, onehot, skeleton, k, devs, piv):
-    rows, local = skeleton.shape
-    per = local // NB // devs
-    sizes = (piv, rows - piv)
-
-    def body(sc_ref, s_ref, *refs):
+        place_of = lax.broadcasted_iota(jnp.int32, (rest, rows), 0).astype(f32)
+        full_order = jnp.concatenate([sp, jnp.where(rank == place_of, free, 0.0)], axis=0)
+        st_ref[...] = full_order.T.astype(bf16)
+        s_ref[...] = full_order.astype(bf16)
+
+    def body(sc_ref, s_in, *refs):
+        piv_ref, rest_ref = refs[per : per + 2]
+        if make:
+            order(s_in, *refs[per + 2 :])
+            s_in = refs[per + 2]
         for i in range(per):
-            x = select(s_ref[...], refs[i][...])
-            refs[per][:, i * NB : (i + 1) * NB] = x[0:piv]
-            refs[per + 1][:, i * NB : (i + 1) * NB] = x[piv:]
-
-    block = lambda i: pl.BlockSpec((rows, NB), lambda _, sc: (0, lax.rem(sc[0] + k, devs) + devs * i))
+            x = select(s_in[...], refs[i][...])
+            piv_ref[:, i * NB : (i + 1) * NB] = x[0:piv]
+            rest_ref[:, i * NB : (i + 1) * NB] = x[piv:]
+
+    whole = lambda shape: pl.BlockSpec(shape, lambda _, sc: (0, 0))
+    block = lambda at: pl.BlockSpec((rows, NB), lambda _, sc: (0, at(sc)))
+    shapes = [((piv, per * NB), f32), ((rest, per * NB), f32)] + [((rows, rows), bf16)] * (2 if make else 0)
+    source = own if make else onehot
     return pl.pallas_call(
         body,
         grid_spec=pltpu.PrefetchScalarGridSpec(
             num_scalar_prefetch=1,
             grid=(1,),
-            in_specs=[pl.BlockSpec((rows, rows), lambda _, sc: (0, 0))] + [block(i) for i in range(per)],
-            out_specs=[pl.BlockSpec((n, per * NB), lambda _, sc: (0, 0)) for n in sizes],
-        ),
-        out_shape=[jax.ShapeDtypeStruct((n, per * NB), f32) for n in sizes],
+            in_specs=[whole(source.shape)] + [block(at) for at in columns],
+            out_specs=[whole(x) for x, _ in shapes],
+        ),
+        out_shape=[jax.ShapeDtypeStruct(x, d) for x, d in shapes],
         compiler_params=params(1),
         cost_estimate=cost(6 * rows * rows * per * NB, 8 * rows * per * NB),
         name="pick",
-    )(scalars, onehot, *[skeleton] * per)
+    )(scalars, source, *[skeleton] * per)
 
 
 def invert(d_ref, x_ref, r_ref):
@@ -174,20 +160,14 @@
     return 2.0 * ((dot(hi, onehot) + dot(mid, onehot)) + dot(low, onehot))
 
 
-def multipliers(scalars, blocks, panel_rest, share):
+def first_step(scalars, blocks, panel_rest, share):
     rest = panel_rest.shape[0]
-    half = share // 2
     width = 2 * NB
     count = len(blocks)
 
     def body(sc_ref, *refs):
         b_refs = refs[:count]
-        pn_ref, l_ref, l0_ref, w0, w1, d_ref, x0, x1, r_ref, lp = refs[count:]
-
-        @pl.when(sc_ref[0] != 0)
-        def _():
-            l_ref[...] = jnp.zeros_like(l_ref)
-            l0_ref[...] = jnp.zeros_like(l0_ref)
+        pn_ref, lp, d1, l0, bp, w0, w1, d_ref, x0, r_ref = refs[count:]
 
         @pl.when(sc_ref[0] == 0)
         def _():
@@ -196,35 +176,73 @@
                 w1[m * share : (m + 1) * share, :] = b_refs[m][share : 2 * share, :]
             d_ref[...] = w0[:, 0:NB]
             invert(d_ref, x0, r_ref)
-            lp[...] = dot3(w1[:, 0:NB], x0[...])
-            d_ref[...] = w1[:, NB:width] - dot3(lp[...], w0[:, NB:width])
-            invert(d_ref, x1, r_ref)
-            l0 = dot3(pn_ref[:, 0:NB], x0[...])
-            l1 = dot3(pn_ref[:, NB:width] - dot3(l0, w0[:, NB:width]), x1[...])
-            l_ref[half:, 0:NB] = l0 - dot3(l1, lp[...])
-            l_ref[half:, NB:width] = l1
-            l_ref[0:half, 0:NB] = lp[0:half, :]
-            l_ref[0:half, NB:width] = lp[half:share, :]
-            back = natural(sc_ref, count, share)
-            l0_ref[0:share, :] = place(lp[0:share, :], back)
-            l0_ref[share:, :] = place(l0, back)
+            low = dot3(w1[:, 0:NB], x0[...])
+            lp[...] = low
+            d1[...] = w1[:, NB:width] - dot3(low, w0[:, NB:width])
+            mine = dot3(pn_ref[:, 0:NB], x0[...])
+            l0[...] = mine
+            bp[...] = pn_ref[:, NB:width] - dot3(mine, w0[:, NB:width])
 
     full = lambda shape: pl.BlockSpec(shape, lambda i, sc: (0, 0))
     square = pltpu.VMEM((NB, NB), f32)
+    shapes = [(NB, NB), (NB, NB), (rest, NB), (rest, NB)]
     return pl.pallas_call(
         body,
         grid_spec=pltpu.PrefetchScalarGridSpec(
             num_scalar_prefetch=1,
             grid=(1,),
             in_specs=[full((2 * share, width))] * count + [full((rest, width))],
+            out_specs=[full(x) for x in shapes],
+            scratch_shapes=[pltpu.VMEM((NB, width), f32)] * 2 + [square] * 3,
+        ),
+        out_shape=[jax.ShapeDtypeStruct(x, f32) for x in shapes],
+        compiler_params=params(1),
+        cost_estimate=cost(20e9, 8 << 20),
+        name="first_step",
+    )(scalars, *blocks, panel_rest)
+
+
+def second_step(scalars, lp, d1, l0, bp, share):
+    rest = l0.shape[0]
+    half = share // 2
+    width = 2 * NB
+    count = NB // share
+
+    def body(sc_ref, lp_ref, d1_ref, l0_in, bp_ref, l_ref, l0_ref, d_ref, x1, r_ref):
+        @pl.when(sc_ref[0] != 0)
+        def _():
+            l_ref[...] = jnp.zeros_like(l_ref)
+            l0_ref[...] = jnp.zeros_like(l0_ref)
+
+        @pl.when(sc_ref[0] == 0)
+        def _():
+            d_ref[...] = d1_ref[...]
+            invert(d_ref, x1, r_ref)
+            l1 = dot3(bp_ref[...], x1[...])
+            l_ref[half:, 0:NB] = l0_in[...] - dot3(l1, lp_ref[...])
+            l_ref[half:, NB:width] = l1
+            l_ref[0:half, 0:NB] = lp_ref[0:half, :]
+            l_ref[0:half, NB:width] = lp_ref[half:share, :]
+            back = natural(sc_ref, count, share)
+            l0_ref[0:share, :] = place(lp_ref[0:share, :], back)
+            l0_ref[share:, :] = place(l0_in[...], back)
+
+    full = lambda shape: pl.BlockSpec(shape, lambda i, sc: (0, 0))
+    square = pltpu.VMEM((NB, NB), f32)
+    return pl.pallas_call(
+        body,
+        grid_spec=pltpu.PrefetchScalarGridSpec(
+            num_scalar_prefetch=1,
+            grid=(1,),
+            in_specs=[full((NB, NB)), full((NB, NB)), full((rest, NB)), full((rest, NB))],
             out_specs=[full((half + rest, width)), full((share + rest, NB))],
-            scratch_shapes=[pltpu.VMEM((NB, width), f32)] * 2 + [square] * 5,
+            scratch_shapes=[square] * 3,
         ),
         out_shape=[jax.ShapeDtypeStruct((half + rest, width), f32), jax.ShapeDtypeStruct((share + rest, NB), f32)],
         compiler_params=params(1),
-        cost_estimate=cost(30e9, 8 << 20),
-        name="multipliers",
-    )(scalars, *blocks, panel_rest)
+        cost_estimate=cost(15e9, 4 << 20),
+        name="second_step",
+    )(scalars, lp, d1, l0, bp)
 
 
 def settle(scalars, parts, lower0, share, count):
@@ -267,43 +285,40 @@
     )(scalars, *parts, lower0)
 
 
-def came_from(sc, k, devs):
-    return lax.rem(sc[0] + devs - k, devs)
-
-
-def product(scalars, k, lh, fixed, blocks, share, devs):
+def came_from(sc, k):
+    return sc[0] ^ k
+
+
+def product(scalars, k, lh, fixed, blocks, share):
     tall = fixed.shape[0]
     rest = tall - share
     piv = 2 * share
     width = 2 * NB
     total = blocks[0].shape[1]
-    steps = total // NB
     count = len(blocks)
     piece = NB // 2
+    tile = 2 * NB if total % (2 * NB) == 0 else NB
+    steps = total // tile
 
     def body(sc_ref, lh_ref, fixed_ref, *refs):
         b_refs = refs[:count]
-        vp_ref, pn_ref, uh, ul = refs[count:]
-        for j in range(2):
+        vp_ref, pn_ref = refs[count:]
+        for j in range(tile // piece):
             cols = slice(j * piece, (j + 1) * piece)
-            for m in range(count):
-                hi, lo = split2(b_refs[m][:, cols])
-                for t in range(2):
-                    at = slice(t * NB + m * share, t * NB + (m + 1) * share)
-                    uh[at, cols] = hi[t * share : (t + 1) * share]
-                    ul[at, cols] = lo[t * share : (t + 1) * share]
-            big = dot(lh_ref[...], uh[:, cols])
-            prod = big[0:tall] + (big[tall:] + dot(lh_ref[0:tall, :], ul[:, cols]))
-            vp_ref[0:share, cols] = b_refs[0][0:share, cols]
-            vp_ref[share:piv, cols] = b_refs[0][share:piv, cols] - prod[0:share]
+            raw = [ref[:, cols] for ref in b_refs]
+            hi, lo = split2(jnp.concatenate([x[0:share] for x in raw] + [x[share:] for x in raw], axis=0))
+            big = dot(lh_ref[...], hi)
+            prod = big[0:tall] + (big[tall:] + dot(lh_ref[0:tall, :], lo))
+            vp_ref[0:share, cols] = raw[0][0:share]
+            vp_ref[share:piv, cols] = raw[0][share:] - prod[0:share]
             pn_ref[:, cols] = prod[share:]
 
-        @pl.when((pl.program_id(0) == 0) & (came_from(sc_ref, k, devs) == 0) & (sc_ref[0] == 0))
+        @pl.when((pl.program_id(0) == 0) & (came_from(sc_ref, k) == 0) & (sc_ref[0] == 0))
         def _():
-            vp_ref[share:piv, :] = fixed_ref[0:share, :]
+            vp_ref[share:piv, 0:NB] = fixed_ref[0:share, :]
 
     full = lambda shape: pl.BlockSpec(shape, lambda i, sc: (0, 0))
-    moving = lambda n: pl.BlockSpec((n, NB), lambda i, sc: (0, i))
+    moving = lambda n: pl.BlockSpec((n, tile), lambda i, sc: (0, i))
     return pl.pallas_call(
         body,
         grid_spec=pltpu.PrefetchScalarGridSpec(
@@ -311,7 +326,6 @@
             grid=(steps,),
             in_specs=[full((2 * tall, width)), full((tall, NB))] + [moving(piv)] * count,
             out_specs=[moving(piv), moving(rest)],
-            scratch_shapes=[pltpu.VMEM((width, NB), bf16), pltpu.VMEM((width, NB), bf16)],
         ),
         out_shape=[jax.ShapeDtypeStruct((piv, total), f32), jax.ShapeDtypeStruct((rest, total), f32)],
         compiler_params=params(1),
@@ -320,24 +334,24 @@
     )(scalars, lh, fixed, *blocks)
 
 
-def finish(scalars, k, st, fixed, done, prod, others, out, out_shape, devs):
+def finish(scalars, k, st, fixed, done, prod, others, out, out_shape):
     rows = st.shape[0]
     piv = done.shape[0]
     rest = rows - piv
     total = others.shape[1]
-    tile = NB
+    tile = 2 * NB if total % (2 * NB) == 0 else NB
     steps = total // tile
+    piece = NB // 2
 
     def body(sc_ref, st_ref, fixed_ref, d_ref, p_ref, n_ref, *refs):
-        o_ref, v = refs[-2:]
-        v[0:piv, :] = d_ref[...]
-        v[piv:, :] = n_ref[...] - p_ref[...]
-
-        @pl.when((pl.program_id(0) == 0) & (came_from(sc_ref, k, devs) == 0) & (sc_ref[0] < 2))
-        def _():
-            v[piv:, :] = fixed_ref[piv // 2 :, :]
-
-        o_ref[...] = select(st_ref[...], v[...])
+        o_ref = refs[-1]
+        panel = (pl.program_id(0) == 0) & (came_from(sc_ref, k) == 0) & (sc_ref[0] < 2)
+        for j in range(tile // piece):
+            cols = slice(j * piece, (j + 1) * piece)
+            low = n_ref[:, cols] - p_ref[:, cols]
+            if (j + 1) * piece <= NB:
+                low = jnp.where(panel, fixed_ref[piv // 2 :, cols], low)
+            o_ref[:, cols] = select(st_ref[...], jnp.concatenate([d_ref[:, cols], low], axis=0))
 
     full = lambda shape: pl.BlockSpec(shape, lambda i, sc: (0, 0))
     moving = lambda n: pl.BlockSpec((n, tile), lambda i, sc: (0, i))
@@ -354,8 +368,7 @@
             num_scalar_prefetch=1,
             grid=(steps,),
             in_specs=in_specs,
-            out_specs=pl.BlockSpec((rows, tile), lambda i, sc: (0, came_from(sc, k, devs) * steps + i)),
-            scratch_shapes=[pltpu.VMEM((rows, tile), f32)],
+            out_specs=pl.BlockSpec((rows, tile), lambda i, sc: (0, came_from(sc, k) * steps + i)),
         ),
         out_shape=out_shape,
         input_output_aliases=aliases,
@@ -402,20 +415,27 @@
     share = NB // size
     scalars = jnp.stack([col, row] + block_ids(row, size)).astype(jnp.int32)
     own = lax.dynamic_slice_in_dim(pivots, row * share, share, axis=1) - row * rows
-    pidx = own.reshape(2 * share, 1)
-    onehot, st, panel_piv, panel_rest = panel_rows(pidx, skeleton)
 
     def shift(x, k):
-        return lax.ppermute(x, "pcol", [(i, (i + k) % devs) for i in range(devs)])
+        return lax.ppermute(x, "pcol", [(i, i ^ k) for i in range(devs)])
 
     def send(x, pairs):
         return lax.ppermute(x, "pcol", pairs)
 
     order = rotations(devs)
-    picked = {k: pick(scalars, onehot, skeleton, k, devs, 2 * share) for k in order + [0]}
+    per = local // NB // devs
+    towards = lambda k: [lambda sc, i=i: (sc[0] ^ k) + devs * i for i in range(per)]
+    piv_rows = 2 * share
+    first, *others = order
+    *head, onehot, st = pick(scalars, None, skeleton, towards(first), piv_rows, own)
+    picked = {first: head}
+    for k in others + [0]:
+        picked[k] = pick(scalars, onehot, skeleton, towards(k), piv_rows)
+    panel_piv, panel_rest = pick(scalars, onehot, skeleton, [lambda sc: 0, lambda sc: 1], piv_rows)
     piv = {k: shift(picked[k][0], k) if k else picked[k][0] for k in [0] + order}
     panel = gather_rows(panel_piv, size)
-    lower, lower0 = multipliers(scalars, panel, panel_rest, share)
+    lp, d1, l0, bp = first_step(scalars, panel, panel_rest, share)
+    lower, lower0 = second_step(scalars, lp, d1, l0, bp, share)
     reach = devs // 2
     moved = send(lower, [(0, reach)])
     parts = [lower, moved]
@@ -431,15 +451,15 @@
     ready = {}
     for k in [0] + order:
         blocks = gather_rows(piv[k], size)
-        ready[k] = product(scalars, k, lh, fixed, blocks, share, devs)
+        ready[k] = product(scalars, k, lh, fixed, blocks, share)
     out = None
     for k in [0] + order:
-        out = finish(scalars, k, st, fixed, *ready[k], rest[k], out, shape, devs)
+        out = finish(scalars, k, st, fixed, *ready[k], rest[k], out, shape)
     return out
 
 
 def rotations(devs):
-    return sorted(range(1, devs), key=lambda k: (-min(k, devs - k), -k))
+    return sorted(range(1, devs), key=lambda k: (k != devs - 1, k))
 
 
 def solution(mesh):

time: 381 us -> 334 us (0.88)
  waiting for transfers between devices: 158 us -> 131 us
  starting transfers between devices: 100 us -> 82 us
    ppermute x3, starting transfers between devices: 54.9 us -> 4.57 us  [send(): return lax.ppermute(x, 'pcol', pairs)]
    ppermute x6, waiting for transfers between devices: 102 us -> 52.9 us  [shift(): return lax.ppermute(x, 'pcol', [(i, i ^ k) for i in range(devs)])]
    ppermute x35, waiting for transfers between devices: 46.3 us -> 78.5 us  [across(): return lax.ppermute(x, 'prow', [(i, move(i)) for i in range(size)])]
    ppermute x6, starting transfers between devices: 23.8 us -> 54.8 us  [shift(): return lax.ppermute(x, 'pcol', [(i, i ^ k) for i in range(devs)])]
    ppermute x3, waiting for transfers between devices: 9.77 us -> 0.01 us  [send(): return lax.ppermute(x, 'pcol', pairs)]
    pallas_call x4, Pallas kernels: 22.9 us -> 18.8 us  [finish(): pl.pallas_call(body, grid_spec=pltpu.PrefetchScalarGridSpec(num_scalar_pr...]
    pallas_call x4 -> x5, Pallas kernels: 19 us -> 22.2 us  [pick(): pl.pallas_call(body, grid_spec=pltpu.PrefetchScalarGridSpec(num_scalar_pr...]
  transfers between devices with their start and end apart: 44 -> 44, of which waited for: 10 -> 15; matrix products, arithmetic and copies ran while one was open for 0% -> 0% of each run, Pallas kernels for 28% -> 31%
where the time goes in v2:
time: 334 us
  waiting for transfers between devices  131 us (39%)
  Pallas kernels  115 us (34%)
  starting transfers between devices  82 us (25%)
  local copies, waits for them, and re-layouts  3.62 us (1%)
    ppermute x35, waiting for transfers between devices, across(): return lax.ppermute(x, 'prow', [(i, move(i)) for i in range(size)])  78.5 us
    ppermute x6, starting transfers between devices, shift(): return lax.ppermute(x, 'pcol', [(i, i ^ k) for i in range(devs)])  54.8 us
    ppermute x6, waiting for transfers between devices, shift(): return lax.ppermute(x, 'pcol', [(i, i ^ k) for i in range(devs)])  52.9 us
    pallas_call x4, Pallas kernels, product(): pl.pallas_call(body, grid_spec=pltpu.PrefetchScalarGridSpec(num_scalar_pr...  31.1 us
    ppermute x35, starting transfers between devices, across(): return lax.ppermute(x, 'prow', [(i, move(i)) for i in range(size)])  22.6 us
    pallas_call x5, Pallas kernels, pick(): pl.pallas_call(body, grid_spec=pltpu.PrefetchScalarGridSpec(num_scalar_pr...  22.2 us
    pallas_call x1, Pallas kernels, first_step(): pl.pallas_call(body, grid_spec=pltpu.PrefetchScalarGridSpec(num_scalar_pr...  21 us
    pallas_call x4, Pallas kernels, finish(): pl.pallas_call(body, grid_spec=pltpu.PrefetchScalarGridSpec(num_scalar_pr...  18.8 us
  transfers between devices with their start and end apart: 44, of which 15 were waited for; matrix products, arithmetic and copies ran while one was open for 0% of the time, Pallas kernels for 31%

profile of v2, /device:TPU:0, one launch (start us, length us, event | category | flops | bytes accessed | tf_op | source)
XLA Modules:
  0.0 333.8 jit_solution(7907741942378963825)
XLA Ops:
  0.0 1.3 dynamic-slice_subtract_fusion.s_in
  2.0 4.9 %pick.5 = (f32[128,2048]{1,0:T(8,128)}, f32[128,2048]{1,0:T(8,128)}, bf16[256,256]{1,0:T(8,128)(2,1)}, bf16[256,256]{1,0:T(8,128)(2,1)}) custom-call(s32[10]{0:T(128)} %stack.40.sc_ref, s32[2,64]{1,0:T(2,128)} %dynamic-slice_subtract_fusion.s_in, f32[256,8192]{1,0:T(8,128)} %refs_3_.7, f32[256,8192]{1,0:T(8,128)} %refs_3_.7, f32[256,8192]{1,0:T(8,128)} %refs_3_.7, ...), custom_call_target="tpu_custom_call" | custom-call | flops 805306368 | bytes 4194304 | tf_op jit(solution)/shard_map/pick/pallas_call | solution.py:83
  6.9 3.5 %pick.6 = (f32[128,1024]{1,0:T(8,128)}, f32[128,1024]{1,0:T(8,128)}) custom-call(s32[10]{0:T(128)} %stack.40.sc_ref, bf16[256,256]{1,0:T(8,128)(2,1)} %get-tuple-element.34.s_in, f32[256,8192]{1,0:T(8,128)} %refs_3_.7, f32[256,8192]{1,0:T(8,128)} %refs_3_.7), custom_call_target="tpu_custom_call" | custom-call | flops 402653184 | bytes 2097152 | tf_op jit(solution)/shard_map/pick/pallas_call | solution.py:83
  10.4 3.0 collective-permute-start
  13.4 1.5 collective-permute-start.1
  14.9 4.6 %pick.9 = (f32[128,2048]{1,0:T(8,128)}, f32[128,2048]{1,0:T(8,128)}) custom-call(s32[10]{0:T(128)} %stack.40.sc_ref, bf16[256,256]{1,0:T(8,128)(2,1)} %get-tuple-element.34.s_in, f32[256,8192]{1,0:T(8,128)} %refs_3_.7, f32[256,8192]{1,0:T(8,128)} %refs_3_.7, f32[256,8192]{1,0:T(8,128)} %refs_3_.7, f32[256,8192]{1,0:T(8,128)} %refs_3_.7), custom_call_target="tpu_custom_call" | custom-call | flops 805306368 | bytes 4194304 | tf_op jit(solution)/shard_map/pick/pallas_call | solution.py:83
  20.0 5.9 %collective-permute-done.refs_1_ = f32[128,1024]{1,0:T(8,128)S(1)} collective-permute-done((f32[128,1024]{1,0:T(8,128)}, f32[128,1024]{1,0:T(8,128)S(1)}, u32[]{:S(2)}, u32[]{:S(2)}) %collective-permute-start) | collective-permute-done | bytes 524320 | tf_op jit(solution)/shard_map/ppermute | solution.py:382
  25.9 1.4 collective-permute-start.2
  27.3 1.1 collective-permute-done.1.refs_2_
  28.4 1.6 collective-permute-start.38
  30.0 4.6 %pick.8 = (f32[128,2048]{1,0:T(8,128)}, f32[128,2048]{1,0:T(8,128)}) custom-call(s32[10]{0:T(128)} %stack.40.sc_ref, bf16[256,256]{1,0:T(8,128)(2,1)} %get-tuple-element.34.s_in, f32[256,8192]{1,0:T(8,128)} %refs_3_.7, f32[256,8192]{1,0:T(8,128)} %refs_3_.7, f32[256,8192]{1,0:T(8,128)} %refs_3_.7, f32[256,8192]{1,0:T(8,128)} %refs_3_.7), custom_call_target="tpu_custom_call" | custom-call | flops 805306368 | bytes 4194304 | tf_op jit(solution)/shard_map/pick/pallas_call | solution.py:83
  34.6 6.1 %collective-permute-done.2.refs_3_ = f32[128,1024]{1,0:T(8,128)S(1)} collective-permute-done((f32[128,1024]{1,0:T(8,128)S(1)}, f32[128,1024]{1,0:T(8,128)S(1)}, u32[]{:S(2)}, u32[]{:S(2)}) %collective-permute-start.2) | collective-permute-done | bytes 524320 | tf_op jit(solution)/shard_map/ppermute | solution.py:382
  41.5 4.5 %collective-permute-start.28 = (f32[128,2048]{1,0:T(8,128)}, f32[128,2048]{1,0:T(8,128)S(1)}, u32[]{:S(2)}, u32[]{:S(2)}) collective-permute-start(f32[128,2048]{1,0:T(8,128)} %get-tuple-element.53), channel_id=1, source_target_pairs={{0,3},{1,2},{2,1},{3,0},{4,7},{5,6},{6,5},{7,4},{8,11},{9,10},{10,... | collective-permute-start | bytes 3145736 | tf_op jit(solution)/shard_map/ppermute | solution.py:420
  46.0 2.3 collective-permute-done.37.refs_1_
  48.3 2.5 collective-permute-start.19
  50.8 2.9 collective-permute-done.38.refs_2_
  53.7 0.9 collective-permute-start.6
  54.6 4.6 %pick.7 = (f32[128,2048]{1,0:T(8,128)}, f32[128,2048]{1,0:T(8,128)}) custom-call(s32[10]{0:T(128)} %stack.40.sc_ref, bf16[256,256]{1,0:T(8,128)(2,1)} %get-tuple-element.34.s_in, f32[256,8192]{1,0:T(8,128)} %refs_3_.7, f32[256,8192]{1,0:T(8,128)} %refs_3_.7, f32[256,8192]{1,0:T(8,128)} %refs_3_.7, f32[256,8192]{1,0:T(8,128)} %refs_3_.7), custom_call_target="tpu_custom_call" | custom-call | flops 805306368 | bytes 4194304 | tf_op jit(solution)/shard_map/pick/pallas_call | solution.py:83
  59.3 1.0 copy-done.8
  60.3 2.0 collective-permute-start.27
  62.3 8.1 %collective-permute-done.28.refs_0_ = f32[128,2048]{1,0:T(8,128)S(1)} collective-permute-done((f32[128,2048]{1,0:T(8,128)}, f32[128,2048]{1,0:T(8,128)S(1)}, u32[]{:S(2)}, u32[]{:S(2)}) %collective-permute-start.28) | collective-permute-done | bytes 1048608 | tf_op jit(solution)/shard_map/ppermute | solution.py:420
  70.4 45.8 %collective-permute-start.10 = (f32[128,2048]{1,0:T(8,128)}, f32[128,2048]{1,0:T(8,128)S(1)}, u32[]{:S(2)}, u32[]{:S(2)}) collective-permute-start(f32[128,2048]{1,0:T(8,128)} %get-tuple-element.45), channel_id=1, source_target_pairs={{0,2},{1,3},{2,0},{3,1},{4,6},{5,7},{6,4},{7,5},{8,10},{9,11},{10,... | collective-permute-start | bytes 3145736 | tf_op jit(solution)/shard_map/ppermute | solution.py:420
  118.0 21.0 %first_step.1 = (f32[512,512]{1,0:T(8,128)}, f32[512,512]{1,0:T(8,128)}, f32[128,512]{1,0:T(8,128)}, f32[128,512]{1,0:T(8,128)}) custom-call(s32[10]{0:T(128)} %stack.40.sc_ref, f32[128,1024]{1,0:T(8,128)} %get-tuple-element.35.refs_0_, f32[128,1024]{1,0:T(8,128)} %copy-done.25, f32[128,1024]{1,0:T(8,128)} %copy-done.26, f32[128,1024]{1,0:T(8,128)} %copy-done.28, ...), custom_call_target="tpu_custom_call" | custom-call | flops 20000000000 | bytes 8388608 | tf_op jit(solution)/shard_map/first_step/pallas_call | solution.py:189
  139.0 1.6 collective-permute-start.29
  140.6 40.9 %collective-permute-done.10.refs_0_ = f32[128,2048]{1,0:T(8,128)S(1)} collective-permute-done((f32[128,2048]{1,0:T(8,128)}, f32[128,2048]{1,0:T(8,128)S(1)}, u32[]{:S(2)}, u32[]{:S(2)}) %collective-permute-start.10) | collective-permute-done | bytes 1048608 | tf_op jit(solution)/shard_map/ppermute | solution.py:420
  182.3 1.5 collective-permute-start.20
  183.8 1.3 collective-permute-start.21
  185.1 18.2 %second_step.1 = (f32[160,1024]{1,0:T(8,128)}, f32[192,512]{1,0:T(8,128)}) custom-call(s32[10]{0:T(128)} %stack.40.sc_ref, f32[512,512]{1,0:T(8,128)} %get-tuple-element.37.lp_ref, f32[512,512]{1,0:T(8,128)} %get-tuple-element.38.d1_ref, f32[128,512]{1,0:T(8,128)} %get-tuple-element.39.l0_in, f32[128,512]{1,0:T(8,128)} %get-tuple-element.40.bp_ref), custom_call_target="tpu_custom_call" | custom-call | flops 15000000512 | bytes 4194304 | tf_op jit(solution)/shard_map/second_step/pallas_call | solution.py:232
  203.3 1.3 collective-permute-start.7
  204.6 2.7 collective-permute-done.30.refs_2_
  207.4 1.6 collective-permute-start.11
  209.7 17.4 %collective-permute-done.21.refs_2_ = f32[128,2048]{1,0:T(8,128)S(1)} collective-permute-done((f32[128,2048]{1,0:T(8,128)S(1)}, f32[128,2048]{1,0:T(8,128)S(1)}, u32[]{:S(2)}, u32[]{:S(2)}) %collective-permute-start.21) | collective-permute-done | bytes 1048608 | tf_op jit(solution)/shard_map/ppermute | solution.py:382
  227.1 2.5 collective-permute-start.8
  230.4 3.1 collective-permute-done.11.refs_1_
  233.6 7.6 %collective-permute-done.12.refs_2_ = f32[128,2048]{1,0:T(8,128)S(1)} collective-permute-done((f32[128,2048]{1,0:T(8,128)S(1)}, f32[128,2048]{1,0:T(8,128)S(1)}, u32[]{:S(2)}, u32[]{:S(2)}) %collective-permute-start.12) | collective-permute-done | bytes 1048608 | tf_op jit(solution)/shard_map/ppermute | solution.py:382
  243.1 9.4 %collective-permute-done.31.refs_3_ = f32[128,2048]{1,0:T(8,128)S(1)} collective-permute-done((f32[128,2048]{1,0:T(8,128)S(1)}, f32[128,2048]{1,0:T(8,128)S(1)}, u32[]{:S(2)}, u32[]{:S(2)}) %collective-permute-start.31) | collective-permute-done | bytes 1048608 | tf_op jit(solution)/shard_map/ppermute | solution.py:382
  254.2 9.6 %collective-permute-done.22.refs_3_ = f32[128,2048]{1,0:T(8,128)} collective-permute-done((f32[128,2048]{1,0:T(8,128)S(1)}, f32[128,2048]{1,0:T(8,128)}, u32[]{:S(2)}, u32[]{:S(2)}) %collective-permute-start.22) | collective-permute-done | bytes 1048608 | tf_op jit(solution)/shard_map/ppermute | solution.py:382
  264.5 10.4 %collective-permute-done.13.refs_3_ = f32[128,2048]{1,0:T(8,128)S(1)} collective-permute-done((f32[128,2048]{1,0:T(8,128)S(1)}, f32[128,2048]{1,0:T(8,128)S(1)}, u32[]{:S(2)}, u32[]{:S(2)}) %collective-permute-start.13) | collective-permute-done | bytes 1048608 | tf_op jit(solution)/shard_map/ppermute | solution.py:382
  276.0 4.0 %settle.1 = (bf16[384,1024]{1,0:T(8,128)(2,1)}, f32[192,512]{1,0:T(8,128)}) custom-call(s32[10]{0:T(128)} %stack.40.sc_ref, f32[160,1024]{1,0:T(8,128)} %get-tuple-element.41.refs_0_, f32[160,1024]{1,0:T(8,128)} %copy-done.22, f32[160,1024]{1,0:T(8,128)} %collective-permute-done.8.refs_2_, f32[160,1024]{1,0:T(8,128)} %copy-done.23, ...), custom_call_target="tpu_custom_call" | custom-call | flops 1000000000 | bytes 4718592 | tf_op jit(solution)/shard_map/settle/pallas_call | solution.py:273
  280.1 7.8 %product.7 = (f32[128,2048]{1,0:T(8,128)}, f32[128,2048]{1,0:T(8,128)}) custom-call(s32[10]{0:T(128)} %stack.40.sc_ref, bf16[384,1024]{1,0:T(8,128)(2,1)} %get-tuple-element.44.lh_ref, f32[192,512]{1,0:T(8,128)} %get-tuple-element.43.fixed_ref, f32[128,2048]{1,0:T(8,128)} %get-tuple-element.57.refs_0_, f32[128,2048]{1,0:T(8,128)} %copy-done.1, ...), custom_call_target="tpu_custom_call" | custom-call | flops 2415919104 | bytes 10485760 | tf_op jit(solution)/shard_map/product/pallas_call | solution.py:322
  287.8 4.7 %finish.4.refs_0_ = f32[256,8192]{1,0:T(8,128)} custom-call(s32[10]{0:T(128)} %stack.40.sc_ref, bf16[256,256]{1,0:T(8,128)(2,1)} %get-tuple-element.33.st_ref, f32[192,512]{1,0:T(8,128)} %get-tuple-element.43.fixed_ref, f32[128,2048]{1,0:T(8,128)} %get-tuple-element.58.d_ref, f32[128,2048]{1,0:T(8,128)} %get-tuple-element.59.p_ref, ...), custom_call_target="tpu_custom_call" | custom-call | flops 805306368 | bytes 3145728 | tf_op jit(solution)/shard_map/finish/pallas_call | solution.py:365
  292.6 7.8 %product.6 = (f32[128,2048]{1,0:T(8,128)}, f32[128,2048]{1,0:T(8,128)}) custom-call(s32[10]{0:T(128)} %stack.40.sc_ref, bf16[384,1024]{1,0:T(8,128)(2,1)} %get-tuple-element.44.lh_ref, f32[192,512]{1,0:T(8,128)} %get-tuple-element.43.fixed_ref, f32[128,2048]{1,0:T(8,128)} %copy-done.6, f32[128,2048]{1,0:T(8,128)} %copy-done.9, ...), custom_call_target="tpu_custom_call" | custom-call | flops 2415919104 | bytes 10485760 | tf_op jit(solution)/shard_map/product/pallas_call | solution.py:322
  300.4 4.7 %finish.5.refs_0_ = f32[256,8192]{1,0:T(8,128)} custom-call(s32[10]{0:T(128)} %stack.40.sc_ref, bf16[256,256]{1,0:T(8,128)(2,1)} %get-tuple-element.33.st_ref, f32[192,512]{1,0:T(8,128)} %get-tuple-element.43.fixed_ref, f32[128,2048]{1,0:T(8,128)} %get-tuple-element.54.d_ref, f32[128,2048]{1,0:T(8,128)} %get-tuple-element.55.p_ref, ...), custom_call_target="tpu_custom_call", output_to_operand_aliasing={{}: (6, {})} | custom-call | flops 805306368 | bytes 3145728 | tf_op jit(solution)/shard_map/finish/pallas_call | solution.py:365
  305.1 7.7 %product.5 = (f32[128,2048]{1,0:T(8,128)}, f32[128,2048]{1,0:T(8,128)}) custom-call(s32[10]{0:T(128)} %stack.40.sc_ref, bf16[384,1024]{1,0:T(8,128)(2,1)} %get-tuple-element.44.lh_ref, f32[192,512]{1,0:T(8,128)} %get-tuple-element.43.fixed_ref, f32[128,2048]{1,0:T(8,128)} %copy-done.4, f32[128,2048]{1,0:T(8,128)} %copy-done.10, f32[128,2048]{1,0:T(8,128)} %copy-done.11, ...), custom_call_target="tpu_custom_call" | custom-call | flops 2415919104 | bytes 10485760 | tf_op jit(solution)/shard_map/product/pallas_call | solution.py:322
  312.8 4.7 %finish.6.refs_0_ = f32[256,8192]{1,0:T(8,128)} custom-call(s32[10]{0:T(128)} %stack.40.sc_ref, bf16[256,256]{1,0:T(8,128)(2,1)} %get-tuple-element.33.st_ref, f32[192,512]{1,0:T(8,128)} %get-tuple-element.43.fixed_ref, f32[128,2048]{1,0:T(8,128)} %get-tuple-element.50.d_ref, f32[128,2048]{1,0:T(8,128)} %get-tuple-element.51.p_ref, ...), custom_call_target="tpu_custom_call", output_to_operand_aliasing={{}: (6, {})} | custom-call | flops 805306368 | bytes 3145728 | tf_op jit(solution)/shard_map/finish/pallas_call | solution.py:365
  317.5 7.7 %product.4 = (f32[128,2048]{1,0:T(8,128)}, f32[128,2048]{1,0:T(8,128)}) custom-call(s32[10]{0:T(128)} %stack.40.sc_ref, bf16[384,1024]{1,0:T(8,128)(2,1)} %get-tuple-element.44.lh_ref, f32[192,512]{1,0:T(8,128)} %get-tuple-element.43.fixed_ref, f32[128,2048]{1,0:T(8,128)} %copy-done.2, f32[128,2048]{1,0:T(8,128)} %copy-done.12, f32[128,2048]{1,0:T(8,128)} %copy-done.13, ...), custom_call_target="tpu_custom_call" | custom-call | flops 2415919104 | bytes 10485760 | tf_op jit(solution)/shard_map/product/pallas_call | solution.py:322
  325.3 3.8 %collective-permute-done.18.n_ref = f32[128,2048]{1,0:T(8,128)} collective-permute-done((f32[128,2048]{1,0:T(8,128)}, f32[128,2048]{1,0:T(8,128)}, u32[]{:S(2)}, u32[]{:S(2)}) %collective-permute-start.18) | collective-permute-done | bytes 1048608 | tf_op jit(solution)/shard_map/ppermute | solution.py:420
  329.1 4.7 %finish.7 = f32[256,8192]{1,0:T(8,128)} custom-call(s32[10]{0:T(128)} %stack.40.sc_ref, bf16[256,256]{1,0:T(8,128)(2,1)} %get-tuple-element.33.st_ref, f32[192,512]{1,0:T(8,128)} %get-tuple-element.43.fixed_ref, f32[128,2048]{1,0:T(8,128)} %get-tuple-element.46.d_ref, f32[128,2048]{1,0:T(8,128)} %get-tuple-element.47.p_ref, ...), custom_call_target="tpu_custom_call", output_to_operand_aliasing={{}: (6, {})} | custom-call | flops 805306368 | bytes 3145728 | tf_op jit(solution)/shard_map/finish/pallas_call | solution.py:365
  (120 shorter events, 11.7 us)
Async XLA Ops:
  10.4 15.5 %collective-permute-start = (f32[128,1024]{1,0:T(8,128)}, f32[128,1024]{1,0:T(8,128)S(1)}, u32[]{:S(2)}, u32[]{:S(2)}) collective-permute-start(f32[128,1024]{1,0:T(8,128)} %get-tuple-element.35.refs_0_), channel_id=1, source_target_pairs={{0,8},{4,20},{8,0},{12,28},{16,24},{20,4},{24,16},{28,12},{1,9},{5... | collective-permute-start | bytes 1572872 | tf_op jit(solution)/shard_map/ppermute | solution.py:382
  13.4 15.0 %collective-permute-start.1 = (f32[128,1024]{1,0:T(8,128)}, f32[128,1024]{1,0:T(8,128)S(1)}, u32[]{:S(2)}, u32[]{:S(2)}) collective-permute-start(f32[128,1024]{1,0:T(8,128)} %get-tuple-element.35.refs_0_), channel_id=1, source_target_pairs={{0,16},{4,12},{8,24},{12,4},{16,0},{20,28},{24,8},{28,20},{1,17},{... | collective-permute-start | bytes 1572872 | tf_op jit(solution)/shard_map/ppermute | solution.py:382
  19.5 28.8 %collective-permute-start.37 = (f32[128,2048]{1,0:T(8,128)}, f32[128,2048]{1,0:T(8,128)S(1)}, u32[]{:S(2)}, u32[]{:S(2)}) collective-permute-start(f32[128,2048]{1,0:T(8,128)} %get-tuple-element.57.refs_0_), channel_id=1, source_target_pairs={{0,8},{4,20},{8,0},{12,28},{16,24},{20,4},{24,16},{28,12},{1,9},{5... | collective-permute-start | bytes 3145736 | tf_op jit(solution)/shard_map/ppermute | solution.py:382
  20.0 8.3 %collective-permute-start.3 = (f32[128,1024]{1,0:T(8,128)S(1)}, f32[128,1024]{1,0:T(8,128)S(1)}, u32[]{:S(2)}, u32[]{:S(2)}) collective-permute-start(f32[128,1024]{1,0:T(8,128)S(1)} %copy-done.24), channel_id=1, source_target_pairs={{0,4},{4,0},{8,12},{12,8},{16,20},{20,16},{24,28},{28,24},{1,5},{5... | collective-permute-start | bytes 1572872 | tf_op jit(solution)/shard_map/ppermute | solution.py:382
  25.9 14.8 %collective-permute-start.2 = (f32[128,1024]{1,0:T(8,128)S(1)}, f32[128,1024]{1,0:T(8,128)S(1)}, u32[]{:S(2)}, u32[]{:S(2)}) collective-permute-start(f32[128,1024]{1,0:T(8,128)S(1)} %collective-permute-done.refs_1_), channel_id=1, source_target_pairs={{0,16},{4,12},{8,24},{12,4},{16,0},{20,28},{24,8},{28,20},{1,17},{... | collective-permute-start | bytes 1572872 | tf_op jit(solution)/shard_map/ppermute | solution.py:382
  27.3 13.4 %collective-permute-start.4 = (f32[128,1024]{1,0:T(8,128)S(1)}, f32[128,1024]{1,0:T(8,128)S(1)}, u32[]{:S(2)}, u32[]{:S(2)}) collective-permute-start(f32[128,1024]{1,0:T(8,128)S(1)} %collective-permute-done.refs_1_), channel_id=1, source_target_pairs={{0,4},{4,0},{8,12},{12,8},{16,20},{20,16},{24,28},{28,24},{1,5},{5... | collective-permute-start | bytes 1572872 | tf_op jit(solution)/shard_map/ppermute | solution.py:382
  28.4 17.6 %collective-permute-start.5 = (f32[128,1024]{1,0:T(8,128)S(1)}, f32[128,1024]{1,0:T(8,128)}, u32[]{:S(2)}, u32[]{:S(2)}) collective-permute-start(f32[128,1024]{1,0:T(8,128)S(1)} %collective-permute-done.1.refs_2_), channel_id=1, source_target_pairs={{0,4},{4,0},{8,12},{12,8},{16,20},{20,16},{24,28},{28,24},{1,5},{5... | collective-permute-start | bytes 1572872 | tf_op jit(solution)/shard_map/ppermute | solution.py:382
  28.4 25.3 %collective-permute-start.38 = (f32[128,2048]{1,0:T(8,128)}, f32[128,2048]{1,0:T(8,128)S(1)}, u32[]{:S(2)}, u32[]{:S(2)}) collective-permute-start(f32[128,2048]{1,0:T(8,128)} %get-tuple-element.57.refs_0_), channel_id=1, source_target_pairs={{0,16},{4,12},{8,24},{12,4},{16,0},{20,28},{24,8},{28,20},{1,17},{... | collective-permute-start | bytes 3145736 | tf_op jit(solution)/shard_map/ppermute | solution.py:382
  40.7 18.6 %collective-permute-start.40 = (f32[128,2048]{1,0:T(8,128)S(1)}, f32[128,2048]{1,0:T(8,128)S(1)}, u32[]{:S(2)}, u32[]{:S(2)}) collective-permute-start(f32[128,2048]{1,0:T(8,128)S(1)} %copy-done), channel_id=1, source_target_pairs={{0,4},{4,0},{8,12},{12,8},{16,20},{20,16},{24,28},{28,24},{1,5},{5... | collective-permute-start | bytes 3145736 | tf_op jit(solution)/shard_map/ppermute | solution.py:382
  41.5 28.9 %collective-permute-start.28 = (f32[128,2048]{1,0:T(8,128)}, f32[128,2048]{1,0:T(8,128)S(1)}, u32[]{:S(2)}, u32[]{:S(2)}) collective-permute-start(f32[128,2048]{1,0:T(8,128)} %get-tuple-element.53), channel_id=1, source_target_pairs={{0,3},{1,2},{2,1},{3,0},{4,7},{5,6},{6,5},{7,4},{8,11},{9,10},{10,... | collective-permute-start | bytes 3145736 | tf_op jit(solution)/shard_map/ppermute | solution.py:420
  46.0 70.2 %collective-permute-start.36 = (f32[128,2048]{1,0:T(8,128)}, f32[128,2048]{1,0:T(8,128)S(1)}, u32[]{:S(2)}, u32[]{:S(2)}) collective-permute-start(f32[128,2048]{1,0:T(8,128)} %get-tuple-element.56), channel_id=1, source_target_pairs={{0,3},{1,2},{2,1},{3,0},{4,7},{5,6},{6,5},{7,4},{8,11},{9,10},{10,... | collective-permute-start | bytes 3145736 | tf_op jit(solution)/shard_map/ppermute | solution.py:420
  48.3 68.6 %collective-permute-start.19 = (f32[128,2048]{1,0:T(8,128)}, f32[128,2048]{1,0:T(8,128)S(1)}, u32[]{:S(2)}, u32[]{:S(2)}) collective-permute-start(f32[128,2048]{1,0:T(8,128)} %get-tuple-element.49), channel_id=1, source_target_pairs={{0,1},{1,0},{2,3},{3,2},{4,5},{5,4},{6,7},{7,6},{8,9},{9,8},{10,11... | collective-permute-start | bytes 3145736 | tf_op jit(solution)/shard_map/ppermute | solution.py:420
  53.7 63.3 %collective-permute-start.6 = (f32[128,1024]{1,0:T(8,128)}, f32[128,1024]{1,0:T(8,128)S(1)}, u32[]{:S(2)}, u32[]{:S(2)}) collective-permute-start(f32[128,1024]{1,0:T(8,128)} %copy-done.28), channel_id=1, source_target_pairs={{0,4},{4,0},{8,12},{12,8},{16,20},{20,16},{24,28},{28,24},{1,5},{5... | collective-permute-start | bytes 1572872 | tf_op jit(solution)/shard_map/ppermute | solution.py:382
  60.3 78.8 %collective-permute-start.27 = (f32[128,2048]{1,0:T(8,128)}, f32[128,2048]{1,0:T(8,128)S(1)}, u32[]{:S(2)}, u32[]{:S(2)}) collective-permute-start(f32[128,2048]{1,0:T(8,128)} %get-tuple-element.52), channel_id=1, source_target_pairs={{0,1},{1,0},{2,3},{3,2},{4,5},{5,4},{6,7},{7,6},{8,9},{9,8},{10,11... | collective-permute-start | bytes 3145736 | tf_op jit(solution)/shard_map/ppermute | solution.py:420
  70.4 111.8 %copy-start.6 = (f32[128,2048]{1,0:T(8,128)}, f32[128,2048]{1,0:T(8,128)S(1)}, u32[]{:S(2)}) copy-start(f32[128,2048]{1,0:T(8,128)S(1)} %collective-permute-done.28.refs_0_) | copy-start | bytes 3145732
  70.4 111.1 %collective-permute-start.10 = (f32[128,2048]{1,0:T(8,128)}, f32[128,2048]{1,0:T(8,128)S(1)}, u32[]{:S(2)}, u32[]{:S(2)}) collective-permute-start(f32[128,2048]{1,0:T(8,128)} %get-tuple-element.45), channel_id=1, source_target_pairs={{0,2},{1,3},{2,0},{3,1},{4,6},{5,7},{6,4},{7,5},{8,10},{9,11},{10,... | collective-permute-start | bytes 3145736 | tf_op jit(solution)/shard_map/ppermute | solution.py:420
  116.2 66.0 %collective-permute-start.39 = (f32[128,2048]{1,0:T(8,128)S(1)}, f32[128,2048]{1,0:T(8,128)}, u32[]{:S(2)}, u32[]{:S(2)}) collective-permute-start(f32[128,2048]{1,0:T(8,128)S(1)} %collective-permute-done.37.refs_1_), channel_id=1, source_target_pairs={{0,16},{4,12},{8,24},{12,4},{16,0},{20,28},{24,8},{28,20},{1,17},{... | collective-permute-start | bytes 3145736 | tf_op jit(solution)/shard_map/ppermute | solution.py:382
  116.9 90.5 %copy-start.4 = (f32[128,2048]{1,0:T(8,128)}, f32[128,2048]{1,0:T(8,128)S(1)}, u32[]{:S(2)}) copy-start(f32[128,2048]{1,0:T(8,128)S(1)} %collective-permute-done.19.refs_0_) | copy-start | bytes 3145732
  116.9 65.4 %collective-permute-start.41 = (f32[128,2048]{1,0:T(8,128)S(1)}, f32[128,2048]{1,0:T(8,128)}, u32[]{:S(2)}, u32[]{:S(2)}) collective-permute-start(f32[128,2048]{1,0:T(8,128)S(1)} %collective-permute-done.37.refs_1_), channel_id=1, source_target_pairs={{0,4},{4,0},{8,12},{12,8},{16,20},{20,16},{24,28},{28,24},{1,5},{5... | collective-permute-start | bytes 3145736 | tf_op jit(solution)/shard_map/ppermute | solution.py:382
  117.0 66.8 %collective-permute-start.42 = (f32[128,2048]{1,0:T(8,128)S(1)}, f32[128,2048]{1,0:T(8,128)}, u32[]{:S(2)}, u32[]{:S(2)}) collective-permute-start(f32[128,2048]{1,0:T(8,128)S(1)} %collective-permute-done.38.refs_2_), channel_id=1, source_target_pairs={{0,4},{4,0},{8,12},{12,8},{16,20},{20,16},{24,28},{28,24},{1,5},{5... | collective-permute-start | bytes 3145736 | tf_op jit(solution)/shard_map/ppermute | solution.py:382
  139.0 64.3 %collective-permute-start.29 = (f32[128,2048]{1,0:T(8,128)S(1)}, f32[128,2048]{1,0:T(8,128)S(1)}, u32[]{:S(2)}, u32[]{:S(2)}) collective-permute-start(f32[128,2048]{1,0:T(8,128)S(1)} %collective-permute-done.28.refs_0_), channel_id=1, source_target_pairs={{0,8},{4,20},{8,0},{12,28},{16,24},{20,4},{24,16},{28,12},{1,9},{5... | collective-permute-start | bytes 3145736 | tf_op jit(solution)/shard_map/ppermute | solution.py:382
  181.5 25.9 %collective-permute-start.30 = (f32[128,2048]{1,0:T(8,128)S(1)}, f32[128,2048]{1,0:T(8,128)}, u32[]{:S(2)}, u32[]{:S(2)}) collective-permute-start(f32[128,2048]{1,0:T(8,128)S(1)} %collective-permute-done.28.refs_0_), channel_id=1, source_target_pairs={{0,16},{4,12},{8,24},{12,4},{16,0},{20,28},{24,8},{28,20},{1,17},{... | collective-permute-start | bytes 3145736 | tf_op jit(solution)/shard_map/ppermute | solution.py:382
  182.2 25.1 %collective-permute-start.32 = (f32[128,2048]{1,0:T(8,128)S(1)}, f32[128,2048]{1,0:T(8,128)}, u32[]{:S(2)}, u32[]{:S(2)}) collective-permute-start(f32[128,2048]{1,0:T(8,128)S(1)} %collective-permute-done.28.refs_0_), channel_id=1, source_target_pairs={{0,4},{4,0},{8,12},{12,8},{16,20},{20,16},{24,28},{28,24},{1,5},{5... | collective-permute-start | bytes 3145736 | tf_op jit(solution)/shard_map/ppermute | solution.py:382
  182.3 26.6 %collective-permute-start.20 = (f32[128,2048]{1,0:T(8,128)S(1)}, f32[128,2048]{1,0:T(8,128)S(1)}, u32[]{:S(2)}, u32[]{:S(2)}) collective-permute-start(f32[128,2048]{1,0:T(8,128)S(1)} %collective-permute-done.19.refs_0_), channel_id=1, source_target_pairs={{0,8},{4,20},{8,0},{12,28},{16,24},{20,4},{24,16},{28,12},{1,9},{5... | collective-permute-start | bytes 3145736 | tf_op jit(solution)/shard_map/ppermute | solution.py:382
  183.8 43.3 %collective-permute-start.21 = (f32[128,2048]{1,0:T(8,128)S(1)}, f32[128,2048]{1,0:T(8,128)S(1)}, u32[]{:S(2)}, u32[]{:S(2)}) collective-permute-start(f32[128,2048]{1,0:T(8,128)S(1)} %collective-permute-done.19.refs_0_), channel_id=1, source_target_pairs={{0,16},{4,12},{8,24},{12,4},{16,0},{20,28},{24,8},{28,20},{1,17},{... | collective-permute-start | bytes 3145736 | tf_op jit(solution)/shard_map/ppermute | solution.py:382
  203.3 89.3 %copy-start.9 = (f32[128,2048]{1,0:T(8,128)}, f32[128,2048]{1,0:T(8,128)S(1)}, u32[]{:S(2)}) copy-start(f32[128,2048]{1,0:T(8,128)S(1)} %collective-permute-done.29.refs_1_) | copy-start | bytes 3145732
  203.3 26.3 %collective-permute-start.7 = (f32[160,1024]{1,0:T(8,128)}, f32[160,1024]{1,0:T(8,128)S(1)}, u32[]{:S(2)}, u32[]{:S(2)}) collective-permute-start(f32[160,1024]{1,0:T(8,128)} %get-tuple-element.41.refs_0_), channel_id=1, source_target_pairs={{0,2},{4,6},{8,10},{12,14},{16,18},{20,22},{24,26},{28,30}} | collective-permute-start | bytes 1966088 | tf_op jit(solution)/shard_map/ppermute | solution.py:423
  207.4 23.0 %collective-permute-start.23 = (f32[128,2048]{1,0:T(8,128)S(1)}, f32[128,2048]{1,0:T(8,128)S(1)}, u32[]{:S(2)}, u32[]{:S(2)}) collective-permute-start(f32[128,2048]{1,0:T(8,128)S(1)} %collective-permute-done.19.refs_0_), channel_id=1, source_target_pairs={{0,4},{4,0},{8,12},{12,8},{16,20},{20,16},{24,28},{28,24},{1,5},{5... | collective-permute-start | bytes 3145736 | tf_op jit(solution)/shard_map/ppermute | solution.py:382
  207.4 26.1 %collective-permute-start.11 = (f32[128,2048]{1,0:T(8,128)S(1)}, f32[128,2048]{1,0:T(8,128)S(1)}, u32[]{:S(2)}, u32[]{:S(2)}) collective-permute-start(f32[128,2048]{1,0:T(8,128)S(1)} %collective-permute-done.10.refs_0_), channel_id=1, source_target_pairs={{0,8},{4,20},{8,0},{12,28},{16,24},{20,4},{24,16},{28,12},{1,9},{5... | collective-permute-start | bytes 3145736 | tf_op jit(solution)/shard_map/ppermute | solution.py:382
  208.9 83.6 %copy-start.10 = (f32[128,2048]{1,0:T(8,128)}, f32[128,2048]{1,0:T(8,128)S(1)}, u32[]{:S(2)}) copy-start(f32[128,2048]{1,0:T(8,128)S(1)} %collective-permute-done.20.refs_1_) | copy-start | bytes 3145732
  208.9 32.3 %collective-permute-start.12 = (f32[128,2048]{1,0:T(8,128)S(1)}, f32[128,2048]{1,0:T(8,128)S(1)}, u32[]{:S(2)}, u32[]{:S(2)}) collective-permute-start(f32[128,2048]{1,0:T(8,128)S(1)} %collective-permute-done.10.refs_0_), channel_id=1, source_target_pairs={{0,16},{4,12},{8,24},{12,4},{16,0},{20,28},{24,8},{28,20},{1,17},{... | collective-permute-start | bytes 3145736 | tf_op jit(solution)/shard_map/ppermute | solution.py:382
  227.1 14.2 %collective-permute-start.8 = (f32[160,1024]{1,0:T(8,128)}, f32[160,1024]{1,0:T(8,128)}, u32[]{:S(2)}, u32[]{:S(2)}) collective-permute-start(f32[160,1024]{1,0:T(8,128)} %get-tuple-element.41.refs_0_), channel_id=1, source_target_pairs={{0,1},{4,5},{8,9},{12,13},{16,17},{20,21},{24,25},{28,29}} | collective-permute-start | bytes 1966088 | tf_op jit(solution)/shard_map/ppermute | solution.py:423
  229.6 12.1 %collective-permute-start.9 = (f32[160,1024]{1,0:T(8,128)S(1)}, f32[160,1024]{1,0:T(8,128)S(1)}, u32[]{:S(2)}, u32[]{:S(2)}) collective-permute-start(f32[160,1024]{1,0:T(8,128)S(1)} %collective-permute-done.7.refs_1_), channel_id=1, source_target_pairs={{2,3},{6,7},{10,11},{14,15},{18,19},{22,23},{26,27},{30,31}} | collective-permute-start | bytes 1966088 | tf_op jit(solution)/shard_map/ppermute | solution.py:423
  230.3 12.3 %collective-permute-start.43 = (f32[128,2048]{1,0:T(8,128)}, f32[128,2048]{1,0:T(8,128)S(1)}, u32[]{:S(2)}, u32[]{:S(2)}) collective-permute-start(f32[128,2048]{1,0:T(8,128)} %collective-permute-done.39.refs_3_), channel_id=1, source_target_pairs={{0,4},{4,0},{8,12},{12,8},{16,20},{20,16},{24,28},{28,24},{1,5},{5... | collective-permute-start | bytes 3145736 | tf_op jit(solution)/shard_map/ppermute | solution.py:382
  233.5 19.0 %collective-permute-start.31 = (f32[128,2048]{1,0:T(8,128)S(1)}, f32[128,2048]{1,0:T(8,128)S(1)}, u32[]{:S(2)}, u32[]{:S(2)}) collective-permute-start(f32[128,2048]{1,0:T(8,128)S(1)} %collective-permute-done.29.refs_1_), channel_id=1, source_target_pairs={{0,16},{4,12},{8,24},{12,4},{16,0},{20,28},{24,8},{28,20},{1,17},{... | collective-permute-start | bytes 3145736 | tf_op jit(solution)/shard_map/ppermute | solution.py:382
  241.2 11.2 %collective-permute-start.33 = (f32[128,2048]{1,0:T(8,128)S(1)}, f32[128,2048]{1,0:T(8,128)}, u32[]{:S(2)}, u32[]{:S(2)}) collective-permute-start(f32[128,2048]{1,0:T(8,128)S(1)} %collective-permute-done.29.refs_1_), channel_id=1, source_target_pairs={{0,4},{4,0},{8,12},{12,8},{16,20},{20,16},{24,28},{28,24},{1,5},{5... | collective-permute-start | bytes 3145736 | tf_op jit(solution)/shard_map/ppermute | solution.py:382
  241.3 12.0 %collective-permute-start.34 = (f32[128,2048]{1,0:T(8,128)}, f32[128,2048]{1,0:T(8,128)S(1)}, u32[]{:S(2)}, u32[]{:S(2)}) collective-permute-start(f32[128,2048]{1,0:T(8,128)} %collective-permute-done.30.refs_2_), channel_id=1, source_target_pairs={{0,4},{4,0},{8,12},{12,8},{16,20},{20,16},{24,28},{28,24},{1,5},{5... | collective-permute-start | bytes 3145736 | tf_op jit(solution)/shard_map/ppermute | solution.py:382
  241.8 22.1 %collective-permute-start.22 = (f32[128,2048]{1,0:T(8,128)S(1)}, f32[128,2048]{1,0:T(8,128)}, u32[]{:S(2)}, u32[]{:S(2)}) collective-permute-start(f32[128,2048]{1,0:T(8,128)S(1)} %collective-permute-done.20.refs_1_), channel_id=1, source_target_pairs={{0,16},{4,12},{8,24},{12,4},{16,0},{20,28},{24,8},{28,20},{1,17},{... | collective-permute-start | bytes 3145736 | tf_op jit(solution)/shard_map/ppermute | solution.py:382
  242.6 21.2 %collective-permute-start.24 = (f32[128,2048]{1,0:T(8,128)S(1)}, f32[128,2048]{1,0:T(8,128)S(1)}, u32[]{:S(2)}, u32[]{:S(2)}) collective-permute-start(f32[128,2048]{1,0:T(8,128)S(1)} %collective-permute-done.20.refs_1_), channel_id=1, source_target_pairs={{0,4},{4,0},{8,12},{12,8},{16,20},{20,16},{24,28},{28,24},{1,5},{5... | collective-permute-start | bytes 3145736 | tf_op jit(solution)/shard_map/ppermute | solution.py:382
  252.5 11.9 %collective-permute-start.25 = (f32[128,2048]{1,0:T(8,128)S(1)}, f32[128,2048]{1,0:T(8,128)S(1)}, u32[]{:S(2)}, u32[]{:S(2)}) collective-permute-start(f32[128,2048]{1,0:T(8,128)S(1)} %collective-permute-done.21.refs_2_), channel_id=1, source_target_pairs={{0,4},{4,0},{8,12},{12,8},{16,20},{20,16},{24,28},{28,24},{1,5},{5... | collective-permute-start | bytes 3145736 | tf_op jit(solution)/shard_map/ppermute | solution.py:382
  252.5 22.4 %collective-permute-start.13 = (f32[128,2048]{1,0:T(8,128)S(1)}, f32[128,2048]{1,0:T(8,128)S(1)}, u32[]{:S(2)}, u32[]{:S(2)}) collective-permute-start(f32[128,2048]{1,0:T(8,128)S(1)} %collective-permute-done.11.refs_1_), channel_id=1, source_target_pairs={{0,16},{4,12},{8,24},{12,4},{16,0},{20,28},{24,8},{28,20},{1,17},{... | collective-permute-start | bytes 3145736 | tf_op jit(solution)/shard_map/ppermute | solution.py:382
  253.3 21.7 %collective-permute-start.35 = (f32[128,2048]{1,0:T(8,128)S(1)}, f32[128,2048]{1,0:T(8,128)S(1)}, u32[]{:S(2)}, u32[]{:S(2)}) collective-permute-start(f32[128,2048]{1,0:T(8,128)S(1)} %collective-permute-done.31.refs_3_), channel_id=1, source_target_pairs={{0,4},{4,0},{8,12},{12,8},{16,20},{20,16},{24,28},{28,24},{1,5},{5... | collective-permute-start | bytes 3145736 | tf_op jit(solution)/shard_map/ppermute | solution.py:382
  263.8 16.2 %collective-permute-start.26 = (f32[128,2048]{1,0:T(8,128)}, f32[128,2048]{1,0:T(8,128)}, u32[]{:S(2)}, u32[]{:S(2)}) collective-permute-start(f32[128,2048]{1,0:T(8,128)} %collective-permute-done.22.refs_3_), channel_id=1, source_target_pairs={{0,4},{4,0},{8,12},{12,8},{16,20},{20,16},{24,28},{28,24},{1,5},{5... | collective-permute-start | bytes 3145736 | tf_op jit(solution)/shard_map/ppermute | solution.py:382
  263.8 53.7 %collective-permute-start.14 = (f32[128,2048]{1,0:T(8,128)S(1)}, f32[128,2048]{1,0:T(8,128)}, u32[]{:S(2)}, u32[]{:S(2)}) collective-permute-start(f32[128,2048]{1,0:T(8,128)S(1)} %collective-permute-done.10.refs_0_), channel_id=1, source_target_pairs={{0,4},{4,0},{8,12},{12,8},{16,20},{20,16},{24,28},{28,24},{1,5},{5... | collective-permute-start | bytes 3145736 | tf_op jit(solution)/shard_map/ppermute | solution.py:382
  264.4 53.1 %collective-permute-start.15 = (f32[128,2048]{1,0:T(8,128)S(1)}, f32[128,2048]{1,0:T(8,128)}, u32[]{:S(2)}, u32[]{:S(2)}) collective-permute-start(f32[128,2048]{1,0:T(8,128)S(1)} %collective-permute-done.11.refs_1_), channel_id=1, source_target_pairs={{0,4},{4,0},{8,12},{12,8},{16,20},{20,16},{24,28},{28,24},{1,5},{5... | collective-permute-start | bytes 3145736 | tf_op jit(solution)/shard_map/ppermute | solution.py:382
  275.0 42.6 %collective-permute-start.16 = (f32[128,2048]{1,0:T(8,128)S(1)}, f32[128,2048]{1,0:T(8,128)}, u32[]{:S(2)}, u32[]{:S(2)}) collective-permute-start(f32[128,2048]{1,0:T(8,128)S(1)} %collective-permute-done.12.refs_2_), channel_id=1, source_target_pairs={{0,4},{4,0},{8,12},{12,8},{16,20},{20,16},{24,28},{28,24},{1,5},{5... | collective-permute-start | bytes 3145736 | tf_op jit(solution)/shard_map/ppermute | solution.py:382
  275.0 42.5 %collective-permute-start.17 = (f32[128,2048]{1,0:T(8,128)S(1)}, f32[128,2048]{1,0:T(8,128)}, u32[]{:S(2)}, u32[]{:S(2)}) collective-permute-start(f32[128,2048]{1,0:T(8,128)S(1)} %collective-permute-done.13.refs_3_), channel_id=1, source_target_pairs={{0,4},{4,0},{8,12},{12,8},{16,20},{20,16},{24,28},{28,24},{1,5},{5... | collective-permute-start | bytes 3145736 | tf_op jit(solution)/shard_map/ppermute | solution.py:382
  280.0 49.1 %collective-permute-start.18 = (f32[128,2048]{1,0:T(8,128)}, f32[128,2048]{1,0:T(8,128)}, u32[]{:S(2)}, u32[]{:S(2)}) collective-permute-start(f32[128,2048]{1,0:T(8,128)} %get-tuple-element.48), channel_id=1, source_target_pairs={{0,2},{1,3},{2,0},{3,1},{4,6},{5,7},{6,4},{7,5},{8,10},{9,11},{10,... | collective-permute-start | bytes 3145736 | tf_op jit(solution)/shard_map/ppermute | solution.py:420
  (27 other events, 727.0 us)

commit v3 on v2

--- a/solution.py
+++ b/solution.py
@@ -43,8 +43,8 @@
     return pl.CostEstimate(flops=int(flops), transcendentals=0, bytes_accessed=int(nbytes))
 
 
-def params(n):
-    return pltpu.CompilerParams(dimension_semantics=("arbitrary",) * n, vmem_limit_bytes=56 << 20)
+def params(n, mib=20):
+    return pltpu.CompilerParams(dimension_semantics=("arbitrary",) * n, vmem_limit_bytes=mib << 20)
 
 
 def pick(scalars, onehot, skeleton, columns, piv, own=None):
@@ -196,7 +196,7 @@
             scratch_shapes=[pltpu.VMEM((NB, width), f32)] * 2 + [square] * 3,
         ),
         out_shape=[jax.ShapeDtypeStruct(x, f32) for x in shapes],
-        compiler_params=params(1),
+        compiler_params=params(1, 32),
         cost_estimate=cost(20e9, 8 << 20),
         name="first_step",
     )(scalars, *blocks, panel_rest)
@@ -239,7 +239,7 @@
             scratch_shapes=[square] * 3,
         ),
         out_shape=[jax.ShapeDtypeStruct((half + rest, width), f32), jax.ShapeDtypeStruct((share + rest, NB), f32)],
-        compiler_params=params(1),
+        compiler_params=params(1, 32),
         cost_estimate=cost(15e9, 4 << 20),
         name="second_step",
     )(scalars, lp, d1, l0, bp)
@@ -297,7 +297,7 @@
     total = blocks[0].shape[1]
     count = len(blocks)
     piece = NB // 2
-    tile = 2 * NB if total % (2 * NB) == 0 else NB
+    tile = NB
     steps = total // tile
 
     def body(sc_ref, lh_ref, fixed_ref, *refs):

time: 334 us -> 328 us (0.982)
  Pallas kernels: 115 us -> 74.4 us
  waiting for transfers between devices: 131 us -> 164 us
    ppermute x6, waiting for transfers between devices: 52.9 us -> 76.3 us  [shift(): return lax.ppermute(x, 'pcol', [(i, i ^ k) for i in range(devs)])]
    pallas_call x5, Pallas kernels: 22.2 us -> 8.12 us  [pick(): pl.pallas_call(body, grid_spec=pltpu.PrefetchScalarGridSpec(num_scalar_pr...]
    pallas_call x4, Pallas kernels: 31.1 us -> 19 us  [product(): pl.pallas_call(body, grid_spec=pltpu.PrefetchScalarGridSpec(num_scalar_pr...]
    ppermute x35, waiting for transfers between devices: 78.5 us -> 88.2 us  [across(): return lax.ppermute(x, 'prow', [(i, move(i)) for i in range(size)])]
    pallas_call x4, Pallas kernels: 18.8 us -> 13.6 us  [finish(): pl.pallas_call(body, grid_spec=pltpu.PrefetchScalarGridSpec(num_scalar_pr...]
    pallas_call x1, Pallas kernels: 21 us -> 17.1 us  [first_step(): pl.pallas_call(body, grid_spec=pltpu.PrefetchScalarGridSpec(num_scalar_pr...]
  transfers between devices with their start and end apart: 44 -> 44, of which waited for: 15 -> 16; matrix products, arithmetic and copies ran while one was open for 0% -> 0% of each run, Pallas kernels for 31% -> 21%
where the time goes in v3:
time: 328 us; the launch traced here: 327 us
  waiting for transfers between devices  164 us (50%)
  starting transfers between devices  81.7 us (25%)
  Pallas kernels  74.4 us (23%)
  local copies, waits for them, and re-layouts  5.93 us (2%)
    ppermute x35, waiting for transfers between devices, across(): return lax.ppermute(x, 'prow', [(i, move(i)) for i in range(size)])  88.2 us
    ppermute x6, waiting for transfers between devices, shift(): return lax.ppermute(x, 'pcol', [(i, i ^ k) for i in range(devs)])  76.3 us
    ppermute x6, starting transfers between devices, shift(): return lax.ppermute(x, 'pcol', [(i, i ^ k) for i in range(devs)])  55.3 us
    ppermute x35, starting transfers between devices, across(): return lax.ppermute(x, 'prow', [(i, move(i)) for i in range(size)])  22.7 us
    pallas_call x4, Pallas kernels, product(): pl.pallas_call(body, grid_spec=pltpu.PrefetchScalarGridSpec(num_scalar_pr...  19 us
    pallas_call x1, Pallas kernels, first_step(): pl.pallas_call(body, grid_spec=pltpu.PrefetchScalarGridSpec(num_scalar_pr...  17.1 us
    pallas_call x1, Pallas kernels, second_step(): pl.pallas_call(body, grid_spec=pltpu.PrefetchScalarGridSpec(num_scalar_pr...  15.4 us
    pallas_call x4, Pallas kernels, finish(): pl.pallas_call(body, grid_spec=pltpu.PrefetchScalarGridSpec(num_scalar_pr...  13.6 us
  transfers between devices with their start and end apart: 44, of which 16 were waited for; matrix products, arithmetic and copies ran while one was open for 0% of the time, Pallas kernels for 21%

profile of v3, /device:TPU:0, one launch (start us, length us, event | category | flops | bytes accessed | tf_op | source)
XLA Modules:
  0.0 327.4 jit_solution(7194796818048181887)
XLA Ops:
  0.8 3.4 %copy-done = f32[256,8192]{1,0:T(8,128)S(1)} copy-done((f32[256,8192]{1,0:T(8,128)S(1)}, f32[256,8192]{1,0:T(8,128)}, u32[]{:S(2)}) %copy-start) | copy-done | bytes 8388632
  4.2 1.9 pick.5
  6.1 1.5 copy-done.1
  7.6 1.2 pick.6
  8.8 3.0 collective-permute-start
  11.8 1.5 collective-permute-start.1
  13.4 1.7 pick.9
  15.6 8.4 %collective-permute-done.refs_1_ = f32[128,1024]{1,0:T(8,128)S(1)} collective-permute-done((f32[128,1024]{1,0:T(8,128)S(1)}, f32[128,1024]{1,0:T(8,128)S(1)}, u32[]{:S(2)}, u32[]{:S(2)}) %collective-permute-start) | collective-permute-done | bytes 524320 | tf_op jit(solution)/shard_map/ppermute | solution.py:382
  24.0 1.6 collective-permute-start.2
  25.6 1.0 collective-permute-done.1.refs_2_
  26.6 1.5 collective-permute-start.38
  28.2 1.7 pick.8
  29.9 9.0 %collective-permute-done.2.refs_3_ = f32[128,1024]{1,0:T(8,128)S(1)} collective-permute-done((f32[128,1024]{1,0:T(8,128)S(1)}, f32[128,1024]{1,0:T(8,128)S(1)}, u32[]{:S(2)}, u32[]{:S(2)}) %collective-permute-start.2) | collective-permute-done | bytes 524320 | tf_op jit(solution)/shard_map/ppermute | solution.py:382
  38.9 4.6 %collective-permute-start.28 = (f32[128,2048]{1,0:T(8,128)S(1)}, f32[128,2048]{1,0:T(8,128)S(1)}, u32[]{:S(2)}, u32[]{:S(2)}) collective-permute-start(f32[128,2048]{1,0:T(8,128)S(1)} %get-tuple-element.53), channel_id=1, source_target_pairs={{0,3},{1,2},{2,1},{3,0},{4,7},{5,6},{6,5},{7,4},{8,11},{9,10},{10,... | collective-permute-start | bytes 3145736 | tf_op jit(solution)/shard_map/ppermute | solution.py:420
  43.5 2.9 collective-permute-done.37.refs_1_
  46.5 2.6 collective-permute-start.19
  49.1 2.8 collective-permute-done.38.refs_2_
  52.8 1.7 pick.7
  54.5 2.2 collective-permute-start.27
  56.7 11.0 %collective-permute-done.28.refs_0_ = f32[128,2048]{1,0:T(8,128)S(1)} collective-permute-done((f32[128,2048]{1,0:T(8,128)S(1)}, f32[128,2048]{1,0:T(8,128)S(1)}, u32[]{:S(2)}, u32[]{:S(2)}) %collective-permute-start.28) | collective-permute-done | bytes 1048608 | tf_op jit(solution)/shard_map/ppermute | solution.py:420
  67.7 45.8 %collective-permute-start.10 = (f32[128,2048]{1,0:T(8,128)S(1)}, f32[128,2048]{1,0:T(8,128)S(1)}, u32[]{:S(2)}, u32[]{:S(2)}) collective-permute-start(f32[128,2048]{1,0:T(8,128)S(1)} %get-tuple-element.45), channel_id=1, source_target_pairs={{0,2},{1,3},{2,0},{3,1},{4,6},{5,7},{6,4},{7,5},{8,10},{9,11},{10,... | collective-permute-start | bytes 3145736 | tf_op jit(solution)/shard_map/ppermute | solution.py:420
  114.7 17.1 %first_step.1 = (f32[512,512]{1,0:T(8,128)S(1)}, f32[512,512]{1,0:T(8,128)S(1)}, f32[128,512]{1,0:T(8,128)S(1)}, f32[128,512]{1,0:T(8,128)S(1)}) custom-call(s32[10]{0:T(128)S(1)} %stack.40.sc_ref, f32[128,1024]{1,0:T(8,128)S(1)} %get-tuple-element.35.refs_0_, f32[128,1024]{1,0:T(8,128)S(1)} %collective-permute-done.refs_1_, ...), custom_call_target="tpu_custom_call" | custom-call | flops 20000000000 | bytes 8388608 | tf_op jit(solution)/shard_map/first_step/pallas_call | solution.py:189
  131.8 4.0 %collective-permute-done.27.n_ref = f32[128,2048]{1,0:T(8,128)S(1)} collective-permute-done((f32[128,2048]{1,0:T(8,128)S(1)}, f32[128,2048]{1,0:T(8,128)S(1)}, u32[]{:S(2)}, u32[]{:S(2)}) %collective-permute-start.27) | collective-permute-done | bytes 1048608 | tf_op jit(solution)/shard_map/ppermute | solution.py:420
  135.8 1.5 collective-permute-start.29
  137.3 41.5 %collective-permute-done.10.refs_0_ = f32[128,2048]{1,0:T(8,128)S(1)} collective-permute-done((f32[128,2048]{1,0:T(8,128)S(1)}, f32[128,2048]{1,0:T(8,128)S(1)}, u32[]{:S(2)}, u32[]{:S(2)}) %collective-permute-start.10) | collective-permute-done | bytes 1048608 | tf_op jit(solution)/shard_map/ppermute | solution.py:420
  179.6 1.4 collective-permute-start.20
  181.1 1.3 collective-permute-start.21
  182.4 15.4 %second_step.1 = (f32[160,1024]{1,0:T(8,128)S(1)}, f32[192,512]{1,0:T(8,128)S(1)}) custom-call(s32[10]{0:T(128)S(1)} %stack.40.sc_ref, f32[512,512]{1,0:T(8,128)S(1)} %get-tuple-element.37.lp_ref, f32[512,512]{1,0:T(8,128)S(1)} %get-tuple-element.38.d1_ref, f32[128,512]{1,0:T(8,128)S(1)} %get-tuple-element.39.l0_in, f32[128,512]{1,0:T(8,128)S(1)} %get-tuple-element.40.bp_ref), custom_call_target="tpu_custom_call" | custom-call | flops 15000000512 | bytes 4194304 | tf_op jit(solution)/shard_map/second_step/pallas_call | solution.py:232
  197.8 1.3 collective-permute-start.7
  199.2 5.4 %collective-permute-done.30.refs_2_ = f32[128,2048]{1,0:T(8,128)S(1)} collective-permute-done((f32[128,2048]{1,0:T(8,128)S(1)}, f32[128,2048]{1,0:T(8,128)S(1)}, u32[]{:S(2)}, u32[]{:S(2)}) %collective-permute-start.30) | collective-permute-done | bytes 1048608 | tf_op jit(solution)/shard_map/ppermute | solution.py:382
  204.6 1.5 collective-permute-start.11
  206.9 17.5 %collective-permute-done.21.refs_2_ = f32[128,2048]{1,0:T(8,128)S(1)} collective-permute-done((f32[128,2048]{1,0:T(8,128)S(1)}, f32[128,2048]{1,0:T(8,128)S(1)}, u32[]{:S(2)}, u32[]{:S(2)}) %collective-permute-start.21) | collective-permute-done | bytes 1048608 | tf_op jit(solution)/shard_map/ppermute | solution.py:382
  224.4 1.6 collective-permute-start.8
  226.9 3.7 %collective-permute-done.11.refs_1_ = f32[128,2048]{1,0:T(8,128)S(1)} collective-permute-done((f32[128,2048]{1,0:T(8,128)S(1)}, f32[128,2048]{1,0:T(8,128)S(1)}, u32[]{:S(2)}, u32[]{:S(2)}) %collective-permute-start.11) | collective-permute-done | bytes 1048608 | tf_op jit(solution)/shard_map/ppermute | solution.py:382
  230.7 7.8 %collective-permute-done.12.refs_2_ = f32[128,2048]{1,0:T(8,128)S(1)} collective-permute-done((f32[128,2048]{1,0:T(8,128)S(1)}, f32[128,2048]{1,0:T(8,128)S(1)}, u32[]{:S(2)}, u32[]{:S(2)}) %collective-permute-start.12) | collective-permute-done | bytes 1048608 | tf_op jit(solution)/shard_map/ppermute | solution.py:382
  240.3 9.4 %collective-permute-done.31.refs_3_ = f32[128,2048]{1,0:T(8,128)S(1)} collective-permute-done((f32[128,2048]{1,0:T(8,128)S(1)}, f32[128,2048]{1,0:T(8,128)S(1)}, u32[]{:S(2)}, u32[]{:S(2)}) %collective-permute-start.31) | collective-permute-done | bytes 1048608 | tf_op jit(solution)/shard_map/ppermute | solution.py:382
  251.5 9.5 %collective-permute-done.22.refs_3_ = f32[128,2048]{1,0:T(8,128)S(1)} collective-permute-done((f32[128,2048]{1,0:T(8,128)S(1)}, f32[128,2048]{1,0:T(8,128)S(1)}, u32[]{:S(2)}, u32[]{:S(2)}) %collective-permute-start.22) | collective-permute-done | bytes 1048608 | tf_op jit(solution)/shard_map/ppermute | solution.py:382
  261.6 10.6 %collective-permute-done.13.refs_3_ = f32[128,2048]{1,0:T(8,128)S(1)} collective-permute-done((f32[128,2048]{1,0:T(8,128)S(1)}, f32[128,2048]{1,0:T(8,128)S(1)}, u32[]{:S(2)}, u32[]{:S(2)}) %collective-permute-start.13) | collective-permute-done | bytes 1048608 | tf_op jit(solution)/shard_map/ppermute | solution.py:382
  273.7 1.1 settle.1
  275.0 4.7 %product.7 = (f32[128,2048]{1,0:T(8,128)S(1)}, f32[128,2048]{1,0:T(8,128)S(1)}) custom-call(s32[10]{0:T(128)S(1)} %stack.40.sc_ref, bf16[384,1024]{1,0:T(8,128)(2,1)S(1)} %get-tuple-element.44.lh_ref, f32[192,512]{1,0:T(8,128)S(1)} %get-tuple-element.43.fixed_ref, f32[128,2048]{1,0:T(8,128)S(1)} %get-tuple-element.57.refs_0_, ...), custom_call_target="tpu_custom_call" | custom-call | flops 2415919104 | bytes 10485760 | tf_op jit(solution)/shard_map/product/pallas_call | solution.py:322
  279.7 3.2 finish.4.refs_0_
  282.9 4.7 %product.6 = (f32[128,2048]{1,0:T(8,128)S(1)}, f32[128,2048]{1,0:T(8,128)S(1)}) custom-call(s32[10]{0:T(128)S(1)} %stack.40.sc_ref, bf16[384,1024]{1,0:T(8,128)(2,1)S(1)} %get-tuple-element.44.lh_ref, f32[192,512]{1,0:T(8,128)S(1)} %get-tuple-element.43.fixed_ref, f32[128,2048]{1,0:T(8,128)S(1)} %collective-permute-done.28.refs_0_, ...), custom_call_target="tpu_custom_call" | custom-call | flops 2415919104 | bytes 10485760 | tf_op jit(solution)/shard_map/product/pallas_call | solution.py:322
  287.6 3.2 finish.5.refs_0_
  290.8 4.7 %product.5 = (f32[128,2048]{1,0:T(8,128)S(1)}, f32[128,2048]{1,0:T(8,128)S(1)}) custom-call(s32[10]{0:T(128)S(1)} %stack.40.sc_ref, bf16[384,1024]{1,0:T(8,128)(2,1)S(1)} %get-tuple-element.44.lh_ref, f32[192,512]{1,0:T(8,128)S(1)} %get-tuple-element.43.fixed_ref, f32[128,2048]{1,0:T(8,128)S(1)} %collective-permute-done.19.refs_0_, ...), custom_call_target="tpu_custom_call" | custom-call | flops 2415919104 | bytes 10485760 | tf_op jit(solution)/shard_map/product/pallas_call | solution.py:322
  295.6 3.2 finish.6.refs_0_
  298.8 4.7 %product.4 = (f32[128,2048]{1,0:T(8,128)S(1)}, f32[128,2048]{1,0:T(8,128)S(1)}) custom-call(s32[10]{0:T(128)S(1)} %stack.40.sc_ref, bf16[384,1024]{1,0:T(8,128)(2,1)S(1)} %get-tuple-element.44.lh_ref, f32[192,512]{1,0:T(8,128)S(1)} %get-tuple-element.43.fixed_ref, f32[128,2048]{1,0:T(8,128)S(1)} %collective-permute-done.10.refs_0_, ...), custom_call_target="tpu_custom_call" | custom-call | flops 2415919104 | bytes 10485760 | tf_op jit(solution)/shard_map/product/pallas_call | solution.py:322
  303.5 19.8 %collective-permute-done.18.n_ref = f32[128,2048]{1,0:T(8,128)} collective-permute-done((f32[128,2048]{1,0:T(8,128)S(1)}, f32[128,2048]{1,0:T(8,128)}, u32[]{:S(2)}, u32[]{:S(2)}) %collective-permute-start.18) | collective-permute-done | bytes 1048608 | tf_op jit(solution)/shard_map/ppermute | solution.py:420
  323.4 4.1 %finish.7 = f32[256,8192]{1,0:T(8,128)} custom-call(s32[10]{0:T(128)S(1)} %stack.40.sc_ref, bf16[256,256]{1,0:T(8,128)(2,1)S(1)} %get-tuple-element.33.st_ref, f32[192,512]{1,0:T(8,128)S(1)} %get-tuple-element.43.fixed_ref, f32[128,2048]{1,0:T(8,128)S(1)} %get-tuple-element.46.d_ref, ...), custom_call_target="tpu_custom_call", output_to_operand_aliasing={{}: (6, {})} | custom-call | flops 805306368 | bytes 3145728 | tf_op jit(solution)/shard_map/finish/pallas_call | solution.py:365
  (66 shorter events, 12.1 us)
Async XLA Ops:
  0.8 3.4 %copy-start = (f32[256,8192]{1,0:T(8,128)S(1)}, f32[256,8192]{1,0:T(8,128)}, u32[]{:S(2)}) copy-start(f32[256,8192]{1,0:T(8,128)} %refs_3_.7) | copy-start | bytes 25165828
  4.2 3.4 %copy-start.1 = (f32[256,8192]{1,0:T(8,128)S(1)}, f32[256,8192]{1,0:T(8,128)}, u32[]{:S(2)}) copy-start(f32[256,8192]{1,0:T(8,128)} %refs_3_.7) | copy-start | bytes 25165828
  8.8 15.2 %collective-permute-start = (f32[128,1024]{1,0:T(8,128)S(1)}, f32[128,1024]{1,0:T(8,128)S(1)}, u32[]{:S(2)}, u32[]{:S(2)}) collective-permute-start(f32[128,1024]{1,0:T(8,128)S(1)} %get-tuple-element.35.refs_0_), channel_id=1, source_target_pairs={{0,8},{4,20},{8,0},{12,28},{16,24},{20,4},{24,16},{28,12},{1,9},{5... | collective-permute-start | bytes 1572872 | tf_op jit(solution)/shard_map/ppermute | solution.py:382
  11.8 14.8 %collective-permute-start.1 = (f32[128,1024]{1,0:T(8,128)S(1)}, f32[128,1024]{1,0:T(8,128)S(1)}, u32[]{:S(2)}, u32[]{:S(2)}) collective-permute-start(f32[128,1024]{1,0:T(8,128)S(1)} %get-tuple-element.35.refs_0_), channel_id=1, source_target_pairs={{0,16},{4,12},{8,24},{12,4},{16,0},{20,28},{24,8},{28,20},{1,17},{... | collective-permute-start | bytes 1572872 | tf_op jit(solution)/shard_map/ppermute | solution.py:382
  15.0 31.4 %collective-permute-start.37 = (f32[128,2048]{1,0:T(8,128)S(1)}, f32[128,2048]{1,0:T(8,128)S(1)}, u32[]{:S(2)}, u32[]{:S(2)}) collective-permute-start(f32[128,2048]{1,0:T(8,128)S(1)} %get-tuple-element.57.refs_0_), channel_id=1, source_target_pairs={{0,8},{4,20},{8,0},{12,28},{16,24},{20,4},{24,16},{28,12},{1,9},{5... | collective-permute-start | bytes 3145736 | tf_op jit(solution)/shard_map/ppermute | solution.py:382
  15.6 11.0 %collective-permute-start.3 = (f32[128,1024]{1,0:T(8,128)S(1)}, f32[128,1024]{1,0:T(8,128)S(1)}, u32[]{:S(2)}, u32[]{:S(2)}) collective-permute-start(f32[128,1024]{1,0:T(8,128)S(1)} %get-tuple-element.35.refs_0_), channel_id=1, source_target_pairs={{0,4},{4,0},{8,12},{12,8},{16,20},{20,16},{24,28},{28,24},{1,5},{5... | collective-permute-start | bytes 1572872 | tf_op jit(solution)/shard_map/ppermute | solution.py:382
  24.0 14.8 %collective-permute-start.2 = (f32[128,1024]{1,0:T(8,128)S(1)}, f32[128,1024]{1,0:T(8,128)S(1)}, u32[]{:S(2)}, u32[]{:S(2)}) collective-permute-start(f32[128,1024]{1,0:T(8,128)S(1)} %collective-permute-done.refs_1_), channel_id=1, source_target_pairs={{0,16},{4,12},{8,24},{12,4},{16,0},{20,28},{24,8},{28,20},{1,17},{... | collective-permute-start | bytes 1572872 | tf_op jit(solution)/shard_map/ppermute | solution.py:382
  25.6 13.2 %collective-permute-start.4 = (f32[128,1024]{1,0:T(8,128)S(1)}, f32[128,1024]{1,0:T(8,128)S(1)}, u32[]{:S(2)}, u32[]{:S(2)}) collective-permute-start(f32[128,1024]{1,0:T(8,128)S(1)} %collective-permute-done.refs_1_), channel_id=1, source_target_pairs={{0,4},{4,0},{8,12},{12,8},{16,20},{20,16},{24,28},{28,24},{1,5},{5... | collective-permute-start | bytes 1572872 | tf_op jit(solution)/shard_map/ppermute | solution.py:382
  26.6 16.8 %collective-permute-start.5 = (f32[128,1024]{1,0:T(8,128)S(1)}, f32[128,1024]{1,0:T(8,128)S(1)}, u32[]{:S(2)}, u32[]{:S(2)}) collective-permute-start(f32[128,1024]{1,0:T(8,128)S(1)} %collective-permute-done.1.refs_2_), channel_id=1, source_target_pairs={{0,4},{4,0},{8,12},{12,8},{16,20},{20,16},{24,28},{28,24},{1,5},{5... | collective-permute-start | bytes 1572872 | tf_op jit(solution)/shard_map/ppermute | solution.py:382
  26.6 25.2 %collective-permute-start.38 = (f32[128,2048]{1,0:T(8,128)S(1)}, f32[128,2048]{1,0:T(8,128)S(1)}, u32[]{:S(2)}, u32[]{:S(2)}) collective-permute-start(f32[128,2048]{1,0:T(8,128)S(1)} %get-tuple-element.57.refs_0_), channel_id=1, source_target_pairs={{0,16},{4,12},{8,24},{12,4},{16,0},{20,28},{24,8},{28,20},{1,17},{... | collective-permute-start | bytes 3145736 | tf_op jit(solution)/shard_map/ppermute | solution.py:382
  38.8 15.7 %collective-permute-start.40 = (f32[128,2048]{1,0:T(8,128)S(1)}, f32[128,2048]{1,0:T(8,128)S(1)}, u32[]{:S(2)}, u32[]{:S(2)}) collective-permute-start(f32[128,2048]{1,0:T(8,128)S(1)} %get-tuple-element.57.refs_0_), channel_id=1, source_target_pairs={{0,4},{4,0},{8,12},{12,8},{16,20},{20,16},{24,28},{28,24},{1,5},{5... | collective-permute-start | bytes 3145736 | tf_op jit(solution)/shard_map/ppermute | solution.py:382
  38.9 28.8 %collective-permute-start.28 = (f32[128,2048]{1,0:T(8,128)S(1)}, f32[128,2048]{1,0:T(8,128)S(1)}, u32[]{:S(2)}, u32[]{:S(2)}) collective-permute-start(f32[128,2048]{1,0:T(8,128)S(1)} %get-tuple-element.53), channel_id=1, source_target_pairs={{0,3},{1,2},{2,1},{3,0},{4,7},{5,6},{6,5},{7,4},{8,11},{9,10},{10,... | collective-permute-start | bytes 3145736 | tf_op jit(solution)/shard_map/ppermute | solution.py:420
  43.4 70.0 %collective-permute-start.36 = (f32[128,2048]{1,0:T(8,128)S(1)}, f32[128,2048]{1,0:T(8,128)S(1)}, u32[]{:S(2)}, u32[]{:S(2)}) collective-permute-start(f32[128,2048]{1,0:T(8,128)S(1)} %get-tuple-element.56), channel_id=1, source_target_pairs={{0,3},{1,2},{2,1},{3,0},{4,7},{5,6},{6,5},{7,4},{8,11},{9,10},{10,... | collective-permute-start | bytes 3145736 | tf_op jit(solution)/shard_map/ppermute | solution.py:420
  46.5 67.7 %collective-permute-start.19 = (f32[128,2048]{1,0:T(8,128)S(1)}, f32[128,2048]{1,0:T(8,128)S(1)}, u32[]{:S(2)}, u32[]{:S(2)}) collective-permute-start(f32[128,2048]{1,0:T(8,128)S(1)} %get-tuple-element.49), channel_id=1, source_target_pairs={{0,1},{1,0},{2,3},{3,2},{4,5},{5,4},{6,7},{7,6},{8,9},{9,8},{10,11... | collective-permute-start | bytes 3145736 | tf_op jit(solution)/shard_map/ppermute | solution.py:420
  51.9 62.3 %collective-permute-start.6 = (f32[128,1024]{1,0:T(8,128)S(1)}, f32[128,1024]{1,0:T(8,128)S(1)}, u32[]{:S(2)}, u32[]{:S(2)}) collective-permute-start(f32[128,1024]{1,0:T(8,128)S(1)} %collective-permute-done.2.refs_3_), channel_id=1, source_target_pairs={{0,4},{4,0},{8,12},{12,8},{16,20},{20,16},{24,28},{28,24},{1,5},{5... | collective-permute-start | bytes 1572872 | tf_op jit(solution)/shard_map/ppermute | solution.py:382
  54.5 81.3 %collective-permute-start.27 = (f32[128,2048]{1,0:T(8,128)S(1)}, f32[128,2048]{1,0:T(8,128)S(1)}, u32[]{:S(2)}, u32[]{:S(2)}) collective-permute-start(f32[128,2048]{1,0:T(8,128)S(1)} %get-tuple-element.52), channel_id=1, source_target_pairs={{0,1},{1,0},{2,3},{3,2},{4,5},{5,4},{6,7},{7,6},{8,9},{9,8},{10,11... | collective-permute-start | bytes 3145736 | tf_op jit(solution)/shard_map/ppermute | solution.py:420
  67.7 111.1 %collective-permute-start.10 = (f32[128,2048]{1,0:T(8,128)S(1)}, f32[128,2048]{1,0:T(8,128)S(1)}, u32[]{:S(2)}, u32[]{:S(2)}) collective-permute-start(f32[128,2048]{1,0:T(8,128)S(1)} %get-tuple-element.45), channel_id=1, source_target_pairs={{0,2},{1,3},{2,0},{3,1},{4,6},{5,7},{6,4},{7,5},{8,10},{9,11},{10,... | collective-permute-start | bytes 3145736 | tf_op jit(solution)/shard_map/ppermute | solution.py:420
  113.4 66.1 %collective-permute-start.39 = (f32[128,2048]{1,0:T(8,128)S(1)}, f32[128,2048]{1,0:T(8,128)S(1)}, u32[]{:S(2)}, u32[]{:S(2)}) collective-permute-start(f32[128,2048]{1,0:T(8,128)S(1)} %collective-permute-done.37.refs_1_), channel_id=1, source_target_pairs={{0,16},{4,12},{8,24},{12,4},{16,0},{20,28},{24,8},{28,20},{1,17},{... | collective-permute-start | bytes 3145736 | tf_op jit(solution)/shard_map/ppermute | solution.py:382
  114.1 65.5 %collective-permute-start.41 = (f32[128,2048]{1,0:T(8,128)S(1)}, f32[128,2048]{1,0:T(8,128)S(1)}, u32[]{:S(2)}, u32[]{:S(2)}) collective-permute-start(f32[128,2048]{1,0:T(8,128)S(1)} %collective-permute-done.37.refs_1_), channel_id=1, source_target_pairs={{0,4},{4,0},{8,12},{12,8},{16,20},{20,16},{24,28},{28,24},{1,5},{5... | collective-permute-start | bytes 3145736 | tf_op jit(solution)/shard_map/ppermute | solution.py:382
  114.1 66.9 %collective-permute-start.42 = (f32[128,2048]{1,0:T(8,128)S(1)}, f32[128,2048]{1,0:T(8,128)S(1)}, u32[]{:S(2)}, u32[]{:S(2)}) collective-permute-start(f32[128,2048]{1,0:T(8,128)S(1)} %collective-permute-done.38.refs_2_), channel_id=1, source_target_pairs={{0,4},{4,0},{8,12},{12,8},{16,20},{20,16},{24,28},{28,24},{1,5},{5... | collective-permute-start | bytes 3145736 | tf_op jit(solution)/shard_map/ppermute | solution.py:382
  135.8 62.0 %collective-permute-start.29 = (f32[128,2048]{1,0:T(8,128)S(1)}, f32[128,2048]{1,0:T(8,128)S(1)}, u32[]{:S(2)}, u32[]{:S(2)}) collective-permute-start(f32[128,2048]{1,0:T(8,128)S(1)} %collective-permute-done.28.refs_0_), channel_id=1, source_target_pairs={{0,8},{4,20},{8,0},{12,28},{16,24},{20,4},{24,16},{28,12},{1,9},{5... | collective-permute-start | bytes 3145736 | tf_op jit(solution)/shard_map/ppermute | solution.py:382
  178.8 25.8 %collective-permute-start.30 = (f32[128,2048]{1,0:T(8,128)S(1)}, f32[128,2048]{1,0:T(8,128)S(1)}, u32[]{:S(2)}, u32[]{:S(2)}) collective-permute-start(f32[128,2048]{1,0:T(8,128)S(1)} %collective-permute-done.28.refs_0_), channel_id=1, source_target_pairs={{0,16},{4,12},{8,24},{12,4},{16,0},{20,28},{24,8},{28,20},{1,17},{... | collective-permute-start | bytes 3145736 | tf_op jit(solution)/shard_map/ppermute | solution.py:382
  179.5 25.0 %collective-permute-start.32 = (f32[128,2048]{1,0:T(8,128)S(1)}, f32[128,2048]{1,0:T(8,128)S(1)}, u32[]{:S(2)}, u32[]{:S(2)}) collective-permute-start(f32[128,2048]{1,0:T(8,128)S(1)} %collective-permute-done.28.refs_0_), channel_id=1, source_target_pairs={{0,4},{4,0},{8,12},{12,8},{16,20},{20,16},{24,28},{28,24},{1,5},{5... | collective-permute-start | bytes 3145736 | tf_op jit(solution)/shard_map/ppermute | solution.py:382
  179.6 26.4 %collective-permute-start.20 = (f32[128,2048]{1,0:T(8,128)S(1)}, f32[128,2048]{1,0:T(8,128)S(1)}, u32[]{:S(2)}, u32[]{:S(2)}) collective-permute-start(f32[128,2048]{1,0:T(8,128)S(1)} %collective-permute-done.19.refs_0_), channel_id=1, source_target_pairs={{0,8},{4,20},{8,0},{12,28},{16,24},{20,4},{24,16},{28,12},{1,9},{5... | collective-permute-start | bytes 3145736 | tf_op jit(solution)/shard_map/ppermute | solution.py:382
  181.1 43.4 %collective-permute-start.21 = (f32[128,2048]{1,0:T(8,128)S(1)}, f32[128,2048]{1,0:T(8,128)S(1)}, u32[]{:S(2)}, u32[]{:S(2)}) collective-permute-start(f32[128,2048]{1,0:T(8,128)S(1)} %collective-permute-done.19.refs_0_), channel_id=1, source_target_pairs={{0,16},{4,12},{8,24},{12,4},{16,0},{20,28},{24,8},{28,20},{1,17},{... | collective-permute-start | bytes 3145736 | tf_op jit(solution)/shard_map/ppermute | solution.py:382
  197.8 28.3 %collective-permute-start.7 = (f32[160,1024]{1,0:T(8,128)S(1)}, f32[160,1024]{1,0:T(8,128)S(1)}, u32[]{:S(2)}, u32[]{:S(2)}) collective-permute-start(f32[160,1024]{1,0:T(8,128)S(1)} %get-tuple-element.41.refs_0_), channel_id=1, source_target_pairs={{0,2},{4,6},{8,10},{12,14},{16,18},{20,22},{24,26},{28,30}} | collective-permute-start | bytes 1966088 | tf_op jit(solution)/shard_map/ppermute | solution.py:423
  204.6 22.3 %collective-permute-start.23 = (f32[128,2048]{1,0:T(8,128)S(1)}, f32[128,2048]{1,0:T(8,128)S(1)}, u32[]{:S(2)}, u32[]{:S(2)}) collective-permute-start(f32[128,2048]{1,0:T(8,128)S(1)} %collective-permute-done.19.refs_0_), channel_id=1, source_target_pairs={{0,4},{4,0},{8,12},{12,8},{16,20},{20,16},{24,28},{28,24},{1,5},{5... | collective-permute-start | bytes 3145736 | tf_op jit(solution)/shard_map/ppermute | solution.py:382
  204.6 26.0 %collective-permute-start.11 = (f32[128,2048]{1,0:T(8,128)S(1)}, f32[128,2048]{1,0:T(8,128)S(1)}, u32[]{:S(2)}, u32[]{:S(2)}) collective-permute-start(f32[128,2048]{1,0:T(8,128)S(1)} %collective-permute-done.10.refs_0_), channel_id=1, source_target_pairs={{0,8},{4,20},{8,0},{12,28},{16,24},{20,4},{24,16},{28,12},{1,9},{5... | collective-permute-start | bytes 3145736 | tf_op jit(solution)/shard_map/ppermute | solution.py:382
  206.0 32.5 %collective-permute-start.12 = (f32[128,2048]{1,0:T(8,128)S(1)}, f32[128,2048]{1,0:T(8,128)S(1)}, u32[]{:S(2)}, u32[]{:S(2)}) collective-permute-start(f32[128,2048]{1,0:T(8,128)S(1)} %collective-permute-done.10.refs_0_), channel_id=1, source_target_pairs={{0,16},{4,12},{8,24},{12,4},{16,0},{20,28},{24,8},{28,20},{1,17},{... | collective-permute-start | bytes 3145736 | tf_op jit(solution)/shard_map/ppermute | solution.py:382
  224.4 14.1 %collective-permute-start.8 = (f32[160,1024]{1,0:T(8,128)S(1)}, f32[160,1024]{1,0:T(8,128)S(1)}, u32[]{:S(2)}, u32[]{:S(2)}) collective-permute-start(f32[160,1024]{1,0:T(8,128)S(1)} %get-tuple-element.41.refs_0_), channel_id=1, source_target_pairs={{0,1},{4,5},{8,9},{12,13},{16,17},{20,21},{24,25},{28,29}} | collective-permute-start | bytes 1966088 | tf_op jit(solution)/shard_map/ppermute | solution.py:423
  226.1 12.9 %collective-permute-start.9 = (f32[160,1024]{1,0:T(8,128)S(1)}, f32[160,1024]{1,0:T(8,128)S(1)}, u32[]{:S(2)}, u32[]{:S(2)}) collective-permute-start(f32[160,1024]{1,0:T(8,128)S(1)} %collective-permute-done.7.refs_1_), channel_id=1, source_target_pairs={{2,3},{6,7},{10,11},{14,15},{18,19},{22,23},{26,27},{30,31}} | collective-permute-start | bytes 1966088 | tf_op jit(solution)/shard_map/ppermute | solution.py:423
  226.8 12.9 %collective-permute-start.43 = (f32[128,2048]{1,0:T(8,128)S(1)}, f32[128,2048]{1,0:T(8,128)S(1)}, u32[]{:S(2)}, u32[]{:S(2)}) collective-permute-start(f32[128,2048]{1,0:T(8,128)S(1)} %collective-permute-done.39.refs_3_), channel_id=1, source_target_pairs={{0,4},{4,0},{8,12},{12,8},{16,20},{20,16},{24,28},{28,24},{1,5},{5... | collective-permute-start | bytes 3145736 | tf_op jit(solution)/shard_map/ppermute | solution.py:382
  230.6 19.2 %collective-permute-start.31 = (f32[128,2048]{1,0:T(8,128)S(1)}, f32[128,2048]{1,0:T(8,128)S(1)}, u32[]{:S(2)}, u32[]{:S(2)}) collective-permute-start(f32[128,2048]{1,0:T(8,128)S(1)} %collective-permute-done.29.refs_1_), channel_id=1, source_target_pairs={{0,16},{4,12},{8,24},{12,4},{16,0},{20,28},{24,8},{28,20},{1,17},{... | collective-permute-start | bytes 3145736 | tf_op jit(solution)/shard_map/ppermute | solution.py:382
  238.5 11.2 %collective-permute-start.33 = (f32[128,2048]{1,0:T(8,128)S(1)}, f32[128,2048]{1,0:T(8,128)S(1)}, u32[]{:S(2)}, u32[]{:S(2)}) collective-permute-start(f32[128,2048]{1,0:T(8,128)S(1)} %collective-permute-done.29.refs_1_), channel_id=1, source_target_pairs={{0,4},{4,0},{8,12},{12,8},{16,20},{20,16},{24,28},{28,24},{1,5},{5... | collective-permute-start | bytes 3145736 | tf_op jit(solution)/shard_map/ppermute | solution.py:382
  238.5 12.0 %collective-permute-start.34 = (f32[128,2048]{1,0:T(8,128)S(1)}, f32[128,2048]{1,0:T(8,128)S(1)}, u32[]{:S(2)}, u32[]{:S(2)}) collective-permute-start(f32[128,2048]{1,0:T(8,128)S(1)} %collective-permute-done.30.refs_2_), channel_id=1, source_target_pairs={{0,4},{4,0},{8,12},{12,8},{16,20},{20,16},{24,28},{28,24},{1,5},{5... | collective-permute-start | bytes 3145736 | tf_op jit(solution)/shard_map/ppermute | solution.py:382
  239.0 22.0 %collective-permute-start.22 = (f32[128,2048]{1,0:T(8,128)S(1)}, f32[128,2048]{1,0:T(8,128)S(1)}, u32[]{:S(2)}, u32[]{:S(2)}) collective-permute-start(f32[128,2048]{1,0:T(8,128)S(1)} %collective-permute-done.20.refs_1_), channel_id=1, source_target_pairs={{0,16},{4,12},{8,24},{12,4},{16,0},{20,28},{24,8},{28,20},{1,17},{... | collective-permute-start | bytes 3145736 | tf_op jit(solution)/shard_map/ppermute | solution.py:382
  239.8 21.2 %collective-permute-start.24 = (f32[128,2048]{1,0:T(8,128)S(1)}, f32[128,2048]{1,0:T(8,128)S(1)}, u32[]{:S(2)}, u32[]{:S(2)}) collective-permute-start(f32[128,2048]{1,0:T(8,128)S(1)} %collective-permute-done.20.refs_1_), channel_id=1, source_target_pairs={{0,4},{4,0},{8,12},{12,8},{16,20},{20,16},{24,28},{28,24},{1,5},{5... | collective-permute-start | bytes 3145736 | tf_op jit(solution)/shard_map/ppermute | solution.py:382
  249.8 11.8 %collective-permute-start.25 = (f32[128,2048]{1,0:T(8,128)S(1)}, f32[128,2048]{1,0:T(8,128)S(1)}, u32[]{:S(2)}, u32[]{:S(2)}) collective-permute-start(f32[128,2048]{1,0:T(8,128)S(1)} %collective-permute-done.21.refs_2_), channel_id=1, source_target_pairs={{0,4},{4,0},{8,12},{12,8},{16,20},{20,16},{24,28},{28,24},{1,5},{5... | collective-permute-start | bytes 3145736 | tf_op jit(solution)/shard_map/ppermute | solution.py:382
  249.8 22.5 %collective-permute-start.13 = (f32[128,2048]{1,0:T(8,128)S(1)}, f32[128,2048]{1,0:T(8,128)S(1)}, u32[]{:S(2)}, u32[]{:S(2)}) collective-permute-start(f32[128,2048]{1,0:T(8,128)S(1)} %collective-permute-done.11.refs_1_), channel_id=1, source_target_pairs={{0,16},{4,12},{8,24},{12,4},{16,0},{20,28},{24,8},{28,20},{1,17},{... | collective-permute-start | bytes 3145736 | tf_op jit(solution)/shard_map/ppermute | solution.py:382
  250.5 21.7 %collective-permute-start.35 = (f32[128,2048]{1,0:T(8,128)S(1)}, f32[128,2048]{1,0:T(8,128)S(1)}, u32[]{:S(2)}, u32[]{:S(2)}) collective-permute-start(f32[128,2048]{1,0:T(8,128)S(1)} %collective-permute-done.31.refs_3_), channel_id=1, source_target_pairs={{0,4},{4,0},{8,12},{12,8},{16,20},{20,16},{24,28},{28,24},{1,5},{5... | collective-permute-start | bytes 3145736 | tf_op jit(solution)/shard_map/ppermute | solution.py:382
  261.0 13.9 %collective-permute-start.26 = (f32[128,2048]{1,0:T(8,128)S(1)}, f32[128,2048]{1,0:T(8,128)S(1)}, u32[]{:S(2)}, u32[]{:S(2)}) collective-permute-start(f32[128,2048]{1,0:T(8,128)S(1)} %collective-permute-done.22.refs_3_), channel_id=1, source_target_pairs={{0,4},{4,0},{8,12},{12,8},{16,20},{20,16},{24,28},{28,24},{1,5},{5... | collective-permute-start | bytes 3145736 | tf_op jit(solution)/shard_map/ppermute | solution.py:382
  261.0 37.8 %collective-permute-start.14 = (f32[128,2048]{1,0:T(8,128)S(1)}, f32[128,2048]{1,0:T(8,128)S(1)}, u32[]{:S(2)}, u32[]{:S(2)}) collective-permute-start(f32[128,2048]{1,0:T(8,128)S(1)} %collective-permute-done.10.refs_0_), channel_id=1, source_target_pairs={{0,4},{4,0},{8,12},{12,8},{16,20},{20,16},{24,28},{28,24},{1,5},{5... | collective-permute-start | bytes 3145736 | tf_op jit(solution)/shard_map/ppermute | solution.py:382
  261.5 37.2 %collective-permute-start.15 = (f32[128,2048]{1,0:T(8,128)S(1)}, f32[128,2048]{1,0:T(8,128)S(1)}, u32[]{:S(2)}, u32[]{:S(2)}) collective-permute-start(f32[128,2048]{1,0:T(8,128)S(1)} %collective-permute-done.11.refs_1_), channel_id=1, source_target_pairs={{0,4},{4,0},{8,12},{12,8},{16,20},{20,16},{24,28},{28,24},{1,5},{5... | collective-permute-start | bytes 3145736 | tf_op jit(solution)/shard_map/ppermute | solution.py:382
  272.2 26.5 %collective-permute-start.16 = (f32[128,2048]{1,0:T(8,128)S(1)}, f32[128,2048]{1,0:T(8,128)S(1)}, u32[]{:S(2)}, u32[]{:S(2)}) collective-permute-start(f32[128,2048]{1,0:T(8,128)S(1)} %collective-permute-done.12.refs_2_), channel_id=1, source_target_pairs={{0,4},{4,0},{8,12},{12,8},{16,20},{20,16},{24,28},{28,24},{1,5},{5... | collective-permute-start | bytes 3145736 | tf_op jit(solution)/shard_map/ppermute | solution.py:382
  272.2 1.0 copy-start.2
  273.2 25.5 %collective-permute-start.17 = (f32[128,2048]{1,0:T(8,128)S(1)}, f32[128,2048]{1,0:T(8,128)S(1)}, u32[]{:S(2)}, u32[]{:S(2)}) collective-permute-start(f32[128,2048]{1,0:T(8,128)S(1)} %collective-permute-done.13.refs_3_), channel_id=1, source_target_pairs={{0,4},{4,0},{8,12},{12,8},{16,20},{20,16},{24,28},{28,24},{1,5},{5... | collective-permute-start | bytes 3145736 | tf_op jit(solution)/shard_map/ppermute | solution.py:382
  274.9 48.5 %collective-permute-start.18 = (f32[128,2048]{1,0:T(8,128)S(1)}, f32[128,2048]{1,0:T(8,128)}, u32[]{:S(2)}, u32[]{:S(2)}) collective-permute-start(f32[128,2048]{1,0:T(8,128)S(1)} %get-tuple-element.48), channel_id=1, source_target_pairs={{0,2},{1,3},{2,0},{3,1},{4,6},{5,7},{6,4},{7,5},{8,10},{9,11},{10,... | collective-permute-start | bytes 3145736 | tf_op jit(solution)/shard_map/ppermute | solution.py:420
  279.7 3.2 copy-start.3

commit v4 on v3

--- a/solution.py
+++ b/solution.py
@@ -47,17 +47,20 @@
     return pltpu.CompilerParams(dimension_semantics=("arbitrary",) * n, vmem_limit_bytes=mib << 20)
 
 
-def pick(scalars, onehot, skeleton, columns, piv, own=None):
+def pick(onehot, skeleton, columns, piv, grant, pivots=None):
     rows = skeleton.shape[0]
     rest = rows - piv
     per = len(columns)
-    make = own is not None
-
-    def order(own_ref, s_ref, st_ref):
+    make = pivots is not None
+
+    def order(pivots_ref, s_ref, st_ref):
         share = piv // 2
-        line = lax.broadcasted_iota(jnp.int32, (rows, share), 0)
-        chosen = jnp.concatenate([(line == own_ref[t : t + 1, :]).astype(f32) for t in range(2)], axis=1)
-        sp = chosen.T
+        row = lax.axis_index("prow")
+        line = lax.broadcasted_iota(jnp.int32, (rows, NB), 0) + row * rows
+        entry = lax.broadcasted_iota(jnp.int32, (NB, share), 0) - lax.broadcasted_iota(jnp.int32, (NB, share), 1)
+        mine = (entry == row * share).astype(f32).astype(bf16)
+        hits = [(line == pivots_ref[t : t + 1, :]).astype(f32).astype(bf16) for t in range(2)]
+        sp = jnp.concatenate([dot(hit, mine) for hit in hits], axis=1).T
         free = 1.0 - jnp.sum(sp, axis=0, keepdims=True)
         before = lax.broadcasted_iota(jnp.int32, (rows, rows), 0) < lax.broadcasted_iota(jnp.int32, (rows, rows), 1)
         rank = dot(jnp.broadcast_to(free, (8, rows)).astype(bf16), before.astype(f32).astype(bf16))[0:1]
@@ -66,33 +69,38 @@
         st_ref[...] = full_order.T.astype(bf16)
         s_ref[...] = full_order.astype(bf16)
 
-    def body(sc_ref, s_in, *refs):
-        piv_ref, rest_ref = refs[per : per + 2]
+    def body(s_in, x_hbm, *refs):
+        piv_ref, rest_ref = refs[:2]
+        blocks, sems = refs[-2:]
+        col = lax.axis_index("pcol")
+        copies = []
+        for i, at in enumerate(columns):
+            start = pl.multiple_of(at(col) * NB, NB)
+            copies.append(pltpu.make_async_copy(x_hbm.at[:, pl.ds(start, NB)], blocks.at[i], sems.at[i]))
+            copies[-1].start()
         if make:
-            order(s_in, *refs[per + 2 :])
-            s_in = refs[per + 2]
-        for i in range(per):
-            x = select(s_in[...], refs[i][...])
+            order(s_in, *refs[2:4])
+            s_in = refs[2]
+        for i, copy in enumerate(copies):
+            copy.wait()
+            x = select(s_in[...], blocks[i])
             piv_ref[:, i * NB : (i + 1) * NB] = x[0:piv]
             rest_ref[:, i * NB : (i + 1) * NB] = x[piv:]
 
-    whole = lambda shape: pl.BlockSpec(shape, lambda _, sc: (0, 0))
-    block = lambda at: pl.BlockSpec((rows, NB), lambda _, sc: (0, at(sc)))
+    whole = lambda shape: pl.BlockSpec(shape, lambda _: (0, 0))
     shapes = [((piv, per * NB), f32), ((rest, per * NB), f32)] + [((rows, rows), bf16)] * (2 if make else 0)
-    source = own if make else onehot
-    return pl.pallas_call(
-        body,
-        grid_spec=pltpu.PrefetchScalarGridSpec(
-            num_scalar_prefetch=1,
-            grid=(1,),
-            in_specs=[whole(source.shape)] + [block(at) for at in columns],
-            out_specs=[whole(x) for x, _ in shapes],
-        ),
+    source = pivots if make else onehot
+    return pl.pallas_call(
+        body,
+        grid=(1,),
+        in_specs=[whole(source.shape), pl.BlockSpec(memory_space=pltpu.MemorySpace.HBM)],
+        out_specs=[whole(x) for x, _ in shapes],
         out_shape=[jax.ShapeDtypeStruct(x, d) for x, d in shapes],
-        compiler_params=params(1),
+        scratch_shapes=[pltpu.VMEM((per, rows, NB), f32), pltpu.SemaphoreType.DMA((per,))],
+        compiler_params=params(1, grant),
         cost_estimate=cost(6 * rows * rows * per * NB, 8 * rows * per * NB),
         name="pick",
-    )(scalars, source, *[skeleton] * per)
+    )(source, skeleton)
 
 
 def invert(d_ref, x_ref, r_ref):
@@ -414,7 +422,6 @@
     col = lax.axis_index("pcol")
     share = NB // size
     scalars = jnp.stack([col, row] + block_ids(row, size)).astype(jnp.int32)
-    own = lax.dynamic_slice_in_dim(pivots, row * share, share, axis=1) - row * rows
 
     def shift(x, k):
         return lax.ppermute(x, "pcol", [(i, i ^ k) for i in range(devs)])
@@ -424,14 +431,14 @@
 
     order = rotations(devs)
     per = local // NB // devs
-    towards = lambda k: [lambda sc, i=i: (sc[0] ^ k) + devs * i for i in range(per)]
+    towards = lambda k: [lambda col, i=i: (col ^ k) + devs * i for i in range(per)]
     piv_rows = 2 * share
     first, *others = order
-    *head, onehot, st = pick(scalars, None, skeleton, towards(first), piv_rows, own)
+    *head, onehot, st = pick(None, skeleton, towards(first), piv_rows, 56, pivots)
     picked = {first: head}
-    for k in others + [0]:
-        picked[k] = pick(scalars, onehot, skeleton, towards(k), piv_rows)
-    panel_piv, panel_rest = pick(scalars, onehot, skeleton, [lambda sc: 0, lambda sc: 1], piv_rows)
+    panel_piv, panel_rest = pick(onehot, skeleton, [lambda col: 0, lambda col: 1], piv_rows, 54)
+    for n, k in enumerate(others + [0]):
+        picked[k] = pick(onehot, skeleton, towards(k), piv_rows, max(52 - 2 * n, 48))
     piv = {k: shift(picked[k][0], k) if k else picked[k][0] for k in [0] + order}
     panel = gather_rows(panel_piv, size)
     lp, d1, l0, bp = first_step(scalars, panel, panel_rest, share)

time: 328 us -> 328 us (level)
  Pallas kernels: 74.4 us -> 88.4 us
  waiting for transfers between devices: 164 us -> 151 us
    pallas_call x5, Pallas kernels: 8.12 us -> 19.3 us  [pick(): pl.pallas_call(body, grid=(1,), in_specs=[whole(source.shape), pl.BlockSp...]
    ppermute x6, waiting for transfers between devices: 76.3 us -> 67.1 us  [shift(): return lax.ppermute(x, 'pcol', [(i, i ^ k) for i in range(devs)])]
    ppermute x35, waiting for transfers between devices: 88.2 us -> 83.5 us  [across(): return lax.ppermute(x, 'prow', [(i, move(i)) for i in range(size)])]
  transfers between devices with their start and end apart: 44 -> 44, of which waited for: 16 -> 15; matrix products, arithmetic and copies ran while one was open for 0% -> 0% of each run, Pallas kernels for 21% -> 23%
where the time goes in v4:
time: 328 us; the launch traced here: 327 us
  waiting for transfers between devices  151 us (46%)
  Pallas kernels  88.4 us (27%)
  starting transfers between devices  81.8 us (25%)
  local copies, waits for them, and re-layouts  5.88 us (2%)
    ppermute x35, waiting for transfers between devices, across(): return lax.ppermute(x, 'prow', [(i, move(i)) for i in range(size)])  83.5 us
    ppermute x6, waiting for transfers between devices, shift(): return lax.ppermute(x, 'pcol', [(i, i ^ k) for i in range(devs)])  67.1 us
    ppermute x6, starting transfers between devices, shift(): return lax.ppermute(x, 'pcol', [(i, i ^ k) for i in range(devs)])  55.1 us
    ppermute x35, starting transfers between devices, across(): return lax.ppermute(x, 'prow', [(i, move(i)) for i in range(size)])  22.9 us
    pallas_call x4, Pallas kernels, product(): pl.pallas_call(body, grid_spec=pltpu.PrefetchScalarGridSpec(num_scalar_pr...  20.7 us
    pallas_call x5, Pallas kernels, pick(): pl.pallas_call(body, grid=(1,), in_specs=[whole(source.shape), pl.BlockSp...  19.3 us
    pallas_call x1, Pallas kernels, first_step(): pl.pallas_call(body, grid_spec=pltpu.PrefetchScalarGridSpec(num_scalar_pr...  18.3 us
    pallas_call x1, Pallas kernels, second_step(): pl.pallas_call(body, grid_spec=pltpu.PrefetchScalarGridSpec(num_scalar_pr...  15.4 us
  transfers between devices with their start and end apart: 44, of which 15 were waited for; matrix products, arithmetic and copies ran while one was open for 0% of the time, Pallas kernels for 23%

profile of v4, /device:TPU:0, one launch (start us, length us, event | category | flops | bytes accessed | tf_op | source)
XLA Modules:
  0.0 327.0 jit_solution(3850053415717900971)
XLA Ops:
  0.0 4.8 %pick.5 = (f32[128,2048]{1,0:T(8,128)}, f32[128,2048]{1,0:T(8,128)}, bf16[256,256]{1,0:T(8,128)(2,1)}, bf16[256,256]{1,0:T(8,128)(2,1)}) custom-call(s32[2,512]{1,0:T(2,128)} %s_in.1, f32[256,8192]{1,0:T(8,128)} %x_hbm.9), custom_call_target="tpu_custom_call" | custom-call | flops 805306368 | bytes 4194304 | tf_op jit(solution)/shard_map/pick/pallas_call | solution.py:93
  4.8 3.8 %pick.6 = (f32[128,1024]{1,0:T(8,128)}, f32[128,1024]{1,0:T(8,128)}) custom-call(bf16[256,256]{1,0:T(8,128)(2,1)} %get-tuple-element.34.s_in, f32[256,8192]{1,0:T(8,128)} %x_hbm.9), custom_call_target="tpu_custom_call" | custom-call | flops 402653184 | bytes 2097152 | tf_op jit(solution)/shard_map/pick/pallas_call | solution.py:93
  8.6 3.0 collective-permute-start
  11.7 1.5 collective-permute-start.1
  13.2 2.8 pick.9
  16.6 7.6 %collective-permute-done.refs_1_ = f32[128,1024]{1,0:T(8,128)S(1)} collective-permute-done((f32[128,1024]{1,0:T(8,128)}, f32[128,1024]{1,0:T(8,128)S(1)}, u32[]{:S(2)}, u32[]{:S(2)}) %collective-permute-start) | collective-permute-done | bytes 524320 | tf_op jit(solution)/shard_map/ppermute | solution.py:390
  24.2 1.5 collective-permute-start.2
  26.7 1.6 collective-permute-start.38
  28.3 4.1 %pick.8 = (f32[128,2048]{1,0:T(8,128)}, f32[128,2048]{1,0:T(8,128)}) custom-call(bf16[256,256]{1,0:T(8,128)(2,1)S(1)} %copy-done.1, f32[256,8192]{1,0:T(8,128)} %x_hbm.9), custom_call_target="tpu_custom_call" | custom-call | flops 805306368 | bytes 4194304 | tf_op jit(solution)/shard_map/pick/pallas_call | solution.py:93
  32.4 6.7 %collective-permute-done.2.refs_3_ = f32[128,1024]{1,0:T(8,128)} collective-permute-done((f32[128,1024]{1,0:T(8,128)S(1)}, f32[128,1024]{1,0:T(8,128)}, u32[]{:S(2)}, u32[]{:S(2)}) %collective-permute-start.2) | collective-permute-done | bytes 524320 | tf_op jit(solution)/shard_map/ppermute | solution.py:390
  39.9 4.5 %collective-permute-start.28 = (f32[128,2048]{1,0:T(8,128)}, f32[128,2048]{1,0:T(8,128)}, u32[]{:S(2)}, u32[]{:S(2)}) collective-permute-start(f32[128,2048]{1,0:T(8,128)} %get-tuple-element.53), channel_id=1, source_target_pairs={{0,3},{1,2},{2,1},{3,0},{4,7},{5,6},{6,5},{7,4},{8,11},{9,10},{10,... | collective-permute-start | bytes 3145736 | tf_op jit(solution)/shard_map/ppermute | solution.py:427
  45.1 1.3 collective-permute-done.37.refs_1_
  46.5 2.6 collective-permute-start.19
  49.1 2.8 collective-permute-done.38.refs_2_
  51.9 1.1 copy-done.2
  53.0 1.0 collective-permute-start.6
  54.1 3.9 %pick.7 = (f32[128,2048]{1,0:T(8,128)S(1)}, f32[128,2048]{1,0:T(8,128)}) custom-call(bf16[256,256]{1,0:T(8,128)(2,1)S(1)} %copy-done.1, f32[256,8192]{1,0:T(8,128)} %x_hbm.9), custom_call_target="tpu_custom_call" | custom-call | flops 805306368 | bytes 4194304 | tf_op jit(solution)/shard_map/pick/pallas_call | solution.py:93
  58.0 2.2 collective-permute-start.27
  60.2 8.7 %collective-permute-done.28.refs_0_ = f32[128,2048]{1,0:T(8,128)} collective-permute-done((f32[128,2048]{1,0:T(8,128)}, f32[128,2048]{1,0:T(8,128)}, u32[]{:S(2)}, u32[]{:S(2)}) %collective-permute-start.28) | collective-permute-done | bytes 1048608 | tf_op jit(solution)/shard_map/ppermute | solution.py:427
  68.9 45.8 %collective-permute-start.10 = (f32[128,2048]{1,0:T(8,128)S(1)}, f32[128,2048]{1,0:T(8,128)S(1)}, u32[]{:S(2)}, u32[]{:S(2)}) collective-permute-start(f32[128,2048]{1,0:T(8,128)S(1)} %get-tuple-element.45), channel_id=1, source_target_pairs={{0,2},{1,3},{2,0},{3,1},{4,6},{5,7},{6,4},{7,5},{8,10},{9,11},{10,... | collective-permute-start | bytes 3145736 | tf_op jit(solution)/shard_map/ppermute | solution.py:427
  117.0 1.0 copy-done.14
  118.0 1.0 copy-done.16
  119.0 18.3 %first_step.1 = (f32[512,512]{1,0:T(8,128)S(1)}, f32[512,512]{1,0:T(8,128)S(1)}, f32[128,512]{1,0:T(8,128)S(1)}, f32[128,512]{1,0:T(8,128)S(1)}) custom-call(s32[10]{0:T(128)S(1)} %stack.40.sc_ref, f32[128,1024]{1,0:T(8,128)S(1)} %copy-done.5, f32[128,1024]{1,0:T(8,128)S(1)} %copy-done.8, f32[128,1024]{1,0:T(8,128)S(1)} %copy-done.10, ...), custom_call_target="tpu_custom_call" | custom-call | flops 20000000000 | bytes 8388608 | tf_op jit(solution)/shard_map/first_step/pallas_call | solution.py:197
  137.3 1.6 collective-permute-start.29
  138.9 41.0 %collective-permute-done.10.refs_0_ = f32[128,2048]{1,0:T(8,128)S(1)} collective-permute-done((f32[128,2048]{1,0:T(8,128)S(1)}, f32[128,2048]{1,0:T(8,128)S(1)}, u32[]{:S(2)}, u32[]{:S(2)}) %collective-permute-start.10) | collective-permute-done | bytes 1048608 | tf_op jit(solution)/shard_map/ppermute | solution.py:427
  180.8 1.4 collective-permute-start.20
  182.2 1.3 collective-permute-start.21
  183.5 15.4 %second_step.1 = (f32[160,1024]{1,0:T(8,128)S(1)}, f32[192,512]{1,0:T(8,128)S(1)}) custom-call(s32[10]{0:T(128)S(1)} %stack.40.sc_ref, f32[512,512]{1,0:T(8,128)S(1)} %get-tuple-element.37.lp_ref, f32[512,512]{1,0:T(8,128)S(1)} %get-tuple-element.38.d1_ref, f32[128,512]{1,0:T(8,128)S(1)} %get-tuple-element.39.l0_in, f32[128,512]{1,0:T(8,128)S(1)} %get-tuple-element.40.bp_ref), custom_call_target="tpu_custom_call" | custom-call | flops 15000000512 | bytes 4194304 | tf_op jit(solution)/shard_map/second_step/pallas_call | solution.py:240
  199.0 1.5 collective-permute-start.7
  200.5 5.4 %collective-permute-done.30.refs_2_ = f32[128,2048]{1,0:T(8,128)S(1)} collective-permute-done((f32[128,2048]{1,0:T(8,128)}, f32[128,2048]{1,0:T(8,128)S(1)}, u32[]{:S(2)}, u32[]{:S(2)}) %collective-permute-start.30) | collective-permute-done | bytes 1048608 | tf_op jit(solution)/shard_map/ppermute | solution.py:390
  205.9 1.5 collective-permute-start.11
  208.3 17.5 %collective-permute-done.21.refs_2_ = f32[128,2048]{1,0:T(8,128)S(1)} collective-permute-done((f32[128,2048]{1,0:T(8,128)}, f32[128,2048]{1,0:T(8,128)S(1)}, u32[]{:S(2)}, u32[]{:S(2)}) %collective-permute-start.21) | collective-permute-done | bytes 1048608 | tf_op jit(solution)/shard_map/ppermute | solution.py:390
  225.8 1.6 collective-permute-start.8
  228.2 3.7 %collective-permute-done.11.refs_1_ = f32[128,2048]{1,0:T(8,128)S(1)} collective-permute-done((f32[128,2048]{1,0:T(8,128)S(1)}, f32[128,2048]{1,0:T(8,128)S(1)}, u32[]{:S(2)}, u32[]{:S(2)}) %collective-permute-start.11) | collective-permute-done | bytes 1048608 | tf_op jit(solution)/shard_map/ppermute | solution.py:390
  232.1 7.8 %collective-permute-done.12.refs_2_ = f32[128,2048]{1,0:T(8,128)S(1)} collective-permute-done((f32[128,2048]{1,0:T(8,128)S(1)}, f32[128,2048]{1,0:T(8,128)S(1)}, u32[]{:S(2)}, u32[]{:S(2)}) %collective-permute-start.12) | collective-permute-done | bytes 1048608 | tf_op jit(solution)/shard_map/ppermute | solution.py:390
  241.7 9.4 %collective-permute-done.31.refs_3_ = f32[128,2048]{1,0:T(8,128)S(1)} collective-permute-done((f32[128,2048]{1,0:T(8,128)S(1)}, f32[128,2048]{1,0:T(8,128)S(1)}, u32[]{:S(2)}, u32[]{:S(2)}) %collective-permute-start.31) | collective-permute-done | bytes 1048608 | tf_op jit(solution)/shard_map/ppermute | solution.py:390
  252.9 9.5 %collective-permute-done.22.refs_3_ = f32[128,2048]{1,0:T(8,128)S(1)} collective-permute-done((f32[128,2048]{1,0:T(8,128)S(1)}, f32[128,2048]{1,0:T(8,128)S(1)}, u32[]{:S(2)}, u32[]{:S(2)}) %collective-permute-start.22) | collective-permute-done | bytes 1048608 | tf_op jit(solution)/shard_map/ppermute | solution.py:390
  262.9 10.6 %collective-permute-done.13.refs_3_ = f32[128,2048]{1,0:T(8,128)S(1)} collective-permute-done((f32[128,2048]{1,0:T(8,128)S(1)}, f32[128,2048]{1,0:T(8,128)S(1)}, u32[]{:S(2)}, u32[]{:S(2)}) %collective-permute-start.13) | collective-permute-done | bytes 1048608 | tf_op jit(solution)/shard_map/ppermute | solution.py:390
  274.1 1.1 settle.1
  275.3 5.4 %product.7 = (f32[128,2048]{1,0:T(8,128)S(1)}, f32[128,2048]{1,0:T(8,128)S(1)}) custom-call(s32[10]{0:T(128)S(1)} %stack.40.sc_ref, bf16[384,1024]{1,0:T(8,128)(2,1)S(1)} %get-tuple-element.44.lh_ref, f32[192,512]{1,0:T(8,128)S(1)} %get-tuple-element.43.fixed_ref, f32[128,2048]{1,0:T(8,128)S(1)} %get-tuple-element.57.refs_0_, ...), custom_call_target="tpu_custom_call" | custom-call | flops 2415919104 | bytes 10485760 | tf_op jit(solution)/shard_map/product/pallas_call | solution.py:330
  280.7 3.2 finish.4.refs_0_
  283.9 5.3 %product.6 = (f32[128,2048]{1,0:T(8,128)S(1)}, f32[128,2048]{1,0:T(8,128)S(1)}) custom-call(s32[10]{0:T(128)S(1)} %stack.40.sc_ref, bf16[384,1024]{1,0:T(8,128)(2,1)S(1)} %get-tuple-element.44.lh_ref, f32[192,512]{1,0:T(8,128)S(1)} %get-tuple-element.43.fixed_ref, f32[128,2048]{1,0:T(8,128)} %collective-permute-done.28.refs_0_, ...), custom_call_target="tpu_custom_call" | custom-call | flops 2415919104 | bytes 10485760 | tf_op jit(solution)/shard_map/product/pallas_call | solution.py:330
  289.1 4.0 %finish.5.refs_0_ = f32[256,8192]{1,0:T(8,128)} custom-call(s32[10]{0:T(128)S(1)} %stack.40.sc_ref, bf16[256,256]{1,0:T(8,128)(2,1)S(1)} %copy-done, f32[192,512]{1,0:T(8,128)S(1)} %get-tuple-element.43.fixed_ref, f32[128,2048]{1,0:T(8,128)S(1)} %get-tuple-element.54.d_ref, f32[128,2048]{1,0:T(8,128)S(1)} %get-tuple-element.55.p_ref, ...), custom_call_target="tpu_custom_call", output_to_operand_aliasing={{}: (6, {})} | custom-call | flops 805306368 | bytes 3145728 | tf_op jit(solution)/shard_map/finish/pallas_call | solution.py:373
  293.2 5.3 %product.5 = (f32[128,2048]{1,0:T(8,128)S(1)}, f32[128,2048]{1,0:T(8,128)S(1)}) custom-call(s32[10]{0:T(128)S(1)} %stack.40.sc_ref, bf16[384,1024]{1,0:T(8,128)(2,1)S(1)} %get-tuple-element.44.lh_ref, f32[192,512]{1,0:T(8,128)S(1)} %get-tuple-element.43.fixed_ref, f32[128,2048]{1,0:T(8,128)} %collective-permute-done.19.refs_0_, ...), custom_call_target="tpu_custom_call" | custom-call | flops 2415919104 | bytes 10485760 | tf_op jit(solution)/shard_map/product/pallas_call | solution.py:330
  298.5 3.2 finish.6.refs_0_
  301.7 4.7 %product.4 = (f32[128,2048]{1,0:T(8,128)S(1)}, f32[128,2048]{1,0:T(8,128)S(1)}) custom-call(s32[10]{0:T(128)S(1)} %stack.40.sc_ref, bf16[384,1024]{1,0:T(8,128)(2,1)S(1)} %get-tuple-element.44.lh_ref, f32[192,512]{1,0:T(8,128)S(1)} %get-tuple-element.43.fixed_ref, f32[128,2048]{1,0:T(8,128)S(1)} %collective-permute-done.10.refs_0_, ...), custom_call_target="tpu_custom_call" | custom-call | flops 2415919104 | bytes 10485760 | tf_op jit(solution)/shard_map/product/pallas_call | solution.py:330
  306.4 17.4 %collective-permute-done.18.n_ref = f32[128,2048]{1,0:T(8,128)S(1)} collective-permute-done((f32[128,2048]{1,0:T(8,128)}, f32[128,2048]{1,0:T(8,128)S(1)}, u32[]{:S(2)}, u32[]{:S(2)}) %collective-permute-start.18) | collective-permute-done | bytes 1048608 | tf_op jit(solution)/shard_map/ppermute | solution.py:427
  323.8 3.2 finish.7
  (91 shorter events, 13.0 us)
Async XLA Ops:
  8.6 15.6 %collective-permute-start = (f32[128,1024]{1,0:T(8,128)}, f32[128,1024]{1,0:T(8,128)S(1)}, u32[]{:S(2)}, u32[]{:S(2)}) collective-permute-start(f32[128,1024]{1,0:T(8,128)} %get-tuple-element.35.refs_0_), channel_id=1, source_target_pairs={{0,8},{4,20},{8,0},{12,28},{16,24},{20,4},{24,16},{28,12},{1,9},{5... | collective-permute-start | bytes 1572872 | tf_op jit(solution)/shard_map/ppermute | solution.py:390
  11.7 15.0 %collective-permute-start.1 = (f32[128,1024]{1,0:T(8,128)}, f32[128,1024]{1,0:T(8,128)S(1)}, u32[]{:S(2)}, u32[]{:S(2)}) collective-permute-start(f32[128,1024]{1,0:T(8,128)} %get-tuple-element.35.refs_0_), channel_id=1, source_target_pairs={{0,16},{4,12},{8,24},{12,4},{16,0},{20,28},{24,8},{28,20},{1,17},{... | collective-permute-start | bytes 1572872 | tf_op jit(solution)/shard_map/ppermute | solution.py:390
  15.9 30.5 %collective-permute-start.37 = (f32[128,2048]{1,0:T(8,128)S(1)}, f32[128,2048]{1,0:T(8,128)S(1)}, u32[]{:S(2)}, u32[]{:S(2)}) collective-permute-start(f32[128,2048]{1,0:T(8,128)S(1)} %get-tuple-element.57.refs_0_), channel_id=1, source_target_pairs={{0,8},{4,20},{8,0},{12,28},{16,24},{20,4},{24,16},{28,12},{1,9},{5... | collective-permute-start | bytes 3145736 | tf_op jit(solution)/shard_map/ppermute | solution.py:390
  16.6 10.1 %collective-permute-start.3 = (f32[128,1024]{1,0:T(8,128)S(1)}, f32[128,1024]{1,0:T(8,128)S(1)}, u32[]{:S(2)}, u32[]{:S(2)}) collective-permute-start(f32[128,1024]{1,0:T(8,128)S(1)} %copy-done.4), channel_id=1, source_target_pairs={{0,4},{4,0},{8,12},{12,8},{16,20},{20,16},{24,28},{28,24},{1,5},{5... | collective-permute-start | bytes 1572872 | tf_op jit(solution)/shard_map/ppermute | solution.py:390
  24.2 14.9 %collective-permute-start.2 = (f32[128,1024]{1,0:T(8,128)S(1)}, f32[128,1024]{1,0:T(8,128)}, u32[]{:S(2)}, u32[]{:S(2)}) collective-permute-start(f32[128,1024]{1,0:T(8,128)S(1)} %collective-permute-done.refs_1_), channel_id=1, source_target_pairs={{0,16},{4,12},{8,24},{12,4},{16,0},{20,28},{24,8},{28,20},{1,17},{... | collective-permute-start | bytes 1572872 | tf_op jit(solution)/shard_map/ppermute | solution.py:390
  25.6 13.4 %collective-permute-start.4 = (f32[128,1024]{1,0:T(8,128)S(1)}, f32[128,1024]{1,0:T(8,128)S(1)}, u32[]{:S(2)}, u32[]{:S(2)}) collective-permute-start(f32[128,1024]{1,0:T(8,128)S(1)} %collective-permute-done.refs_1_), channel_id=1, source_target_pairs={{0,4},{4,0},{8,12},{12,8},{16,20},{20,16},{24,28},{28,24},{1,5},{5... | collective-permute-start | bytes 1572872 | tf_op jit(solution)/shard_map/ppermute | solution.py:390
  26.7 17.7 %collective-permute-start.5 = (f32[128,1024]{1,0:T(8,128)S(1)}, f32[128,1024]{1,0:T(8,128)S(1)}, u32[]{:S(2)}, u32[]{:S(2)}) collective-permute-start(f32[128,1024]{1,0:T(8,128)S(1)} %collective-permute-done.1.refs_2_), channel_id=1, source_target_pairs={{0,4},{4,0},{8,12},{12,8},{16,20},{20,16},{24,28},{28,24},{1,5},{5... | collective-permute-start | bytes 1572872 | tf_op jit(solution)/shard_map/ppermute | solution.py:390
  26.7 25.2 %collective-permute-start.38 = (f32[128,2048]{1,0:T(8,128)S(1)}, f32[128,2048]{1,0:T(8,128)S(1)}, u32[]{:S(2)}, u32[]{:S(2)}) collective-permute-start(f32[128,2048]{1,0:T(8,128)S(1)} %get-tuple-element.57.refs_0_), channel_id=1, source_target_pairs={{0,16},{4,12},{8,24},{12,4},{16,0},{20,28},{24,8},{28,20},{1,17},{... | collective-permute-start | bytes 3145736 | tf_op jit(solution)/shard_map/ppermute | solution.py:390
  39.1 19.0 %collective-permute-start.40 = (f32[128,2048]{1,0:T(8,128)S(1)}, f32[128,2048]{1,0:T(8,128)}, u32[]{:S(2)}, u32[]{:S(2)}) collective-permute-start(f32[128,2048]{1,0:T(8,128)S(1)} %get-tuple-element.57.refs_0_), channel_id=1, source_target_pairs={{0,4},{4,0},{8,12},{12,8},{16,20},{20,16},{24,28},{28,24},{1,5},{5... | collective-permute-start | bytes 3145736 | tf_op jit(solution)/shard_map/ppermute | solution.py:390
  39.9 29.0 %collective-permute-start.28 = (f32[128,2048]{1,0:T(8,128)}, f32[128,2048]{1,0:T(8,128)}, u32[]{:S(2)}, u32[]{:S(2)}) collective-permute-start(f32[128,2048]{1,0:T(8,128)} %get-tuple-element.53), channel_id=1, source_target_pairs={{0,3},{1,2},{2,1},{3,0},{4,7},{5,6},{6,5},{7,4},{8,11},{9,10},{10,... | collective-permute-start | bytes 3145736 | tf_op jit(solution)/shard_map/ppermute | solution.py:427
  45.1 69.5 %collective-permute-start.36 = (f32[128,2048]{1,0:T(8,128)}, f32[128,2048]{1,0:T(8,128)}, u32[]{:S(2)}, u32[]{:S(2)}) collective-permute-start(f32[128,2048]{1,0:T(8,128)} %get-tuple-element.56), channel_id=1, source_target_pairs={{0,3},{1,2},{2,1},{3,0},{4,7},{5,6},{6,5},{7,4},{8,11},{9,10},{10,... | collective-permute-start | bytes 3145736 | tf_op jit(solution)/shard_map/ppermute | solution.py:427
  46.5 68.9 %collective-permute-start.19 = (f32[128,2048]{1,0:T(8,128)}, f32[128,2048]{1,0:T(8,128)}, u32[]{:S(2)}, u32[]{:S(2)}) collective-permute-start(f32[128,2048]{1,0:T(8,128)} %get-tuple-element.49), channel_id=1, source_target_pairs={{0,1},{1,0},{2,3},{3,2},{4,5},{5,4},{6,7},{7,6},{8,9},{9,8},{10,11... | collective-permute-start | bytes 3145736 | tf_op jit(solution)/shard_map/ppermute | solution.py:427
  53.0 62.4 %collective-permute-start.6 = (f32[128,1024]{1,0:T(8,128)}, f32[128,1024]{1,0:T(8,128)}, u32[]{:S(2)}, u32[]{:S(2)}) collective-permute-start(f32[128,1024]{1,0:T(8,128)} %collective-permute-done.2.refs_3_), channel_id=1, source_target_pairs={{0,4},{4,0},{8,12},{12,8},{16,20},{20,16},{24,28},{28,24},{1,5},{5... | collective-permute-start | bytes 1572872 | tf_op jit(solution)/shard_map/ppermute | solution.py:390
  54.1 61.8 %copy-start.5 = (f32[128,1024]{1,0:T(8,128)S(1)}, f32[128,1024]{1,0:T(8,128)}, u32[]{:S(2)}) copy-start(f32[128,1024]{1,0:T(8,128)} %get-tuple-element.35.refs_0_) | copy-start | bytes 1572868
  54.1 61.8 %copy-start.6 = (f32[128,1024]{1,0:T(8,128)S(1)}, f32[128,1024]{1,0:T(8,128)}, u32[]{:S(2)}) copy-start(f32[128,1024]{1,0:T(8,128)} %get-tuple-element.36.refs_8_) | copy-start | bytes 1572868
  54.1 61.8 %copy-start.8 = (f32[128,1024]{1,0:T(8,128)S(1)}, f32[128,1024]{1,0:T(8,128)}, u32[]{:S(2)}) copy-start(f32[128,1024]{1,0:T(8,128)} %copy-done.7) | copy-start | bytes 1572868
  58.0 79.3 %collective-permute-start.27 = (f32[128,2048]{1,0:T(8,128)}, f32[128,2048]{1,0:T(8,128)S(1)}, u32[]{:S(2)}, u32[]{:S(2)}) collective-permute-start(f32[128,2048]{1,0:T(8,128)} %get-tuple-element.52), channel_id=1, source_target_pairs={{0,1},{1,0},{2,3},{3,2},{4,5},{5,4},{6,7},{7,6},{8,9},{9,8},{10,11... | collective-permute-start | bytes 3145736 | tf_op jit(solution)/shard_map/ppermute | solution.py:427
  68.9 111.0 %collective-permute-start.10 = (f32[128,2048]{1,0:T(8,128)S(1)}, f32[128,2048]{1,0:T(8,128)S(1)}, u32[]{:S(2)}, u32[]{:S(2)}) collective-permute-start(f32[128,2048]{1,0:T(8,128)S(1)} %get-tuple-element.45), channel_id=1, source_target_pairs={{0,2},{1,3},{2,0},{3,1},{4,6},{5,7},{6,4},{7,5},{8,10},{9,11},{10,... | collective-permute-start | bytes 3145736 | tf_op jit(solution)/shard_map/ppermute | solution.py:427
  114.6 66.0 %collective-permute-start.39 = (f32[128,2048]{1,0:T(8,128)S(1)}, f32[128,2048]{1,0:T(8,128)S(1)}, u32[]{:S(2)}, u32[]{:S(2)}) collective-permute-start(f32[128,2048]{1,0:T(8,128)S(1)} %collective-permute-done.37.refs_1_), channel_id=1, source_target_pairs={{0,16},{4,12},{8,24},{12,4},{16,0},{20,28},{24,8},{28,20},{1,17},{... | collective-permute-start | bytes 3145736 | tf_op jit(solution)/shard_map/ppermute | solution.py:390
  115.4 65.4 %collective-permute-start.41 = (f32[128,2048]{1,0:T(8,128)S(1)}, f32[128,2048]{1,0:T(8,128)S(1)}, u32[]{:S(2)}, u32[]{:S(2)}) collective-permute-start(f32[128,2048]{1,0:T(8,128)S(1)} %collective-permute-done.37.refs_1_), channel_id=1, source_target_pairs={{0,4},{4,0},{8,12},{12,8},{16,20},{20,16},{24,28},{28,24},{1,5},{5... | collective-permute-start | bytes 3145736 | tf_op jit(solution)/shard_map/ppermute | solution.py:390
  115.4 66.8 %collective-permute-start.42 = (f32[128,2048]{1,0:T(8,128)S(1)}, f32[128,2048]{1,0:T(8,128)S(1)}, u32[]{:S(2)}, u32[]{:S(2)}) collective-permute-start(f32[128,2048]{1,0:T(8,128)S(1)} %copy-done.3), channel_id=1, source_target_pairs={{0,4},{4,0},{8,12},{12,8},{16,20},{20,16},{24,28},{28,24},{1,5},{5... | collective-permute-start | bytes 3145736 | tf_op jit(solution)/shard_map/ppermute | solution.py:390
  137.3 61.6 %collective-permute-start.29 = (f32[128,2048]{1,0:T(8,128)}, f32[128,2048]{1,0:T(8,128)S(1)}, u32[]{:S(2)}, u32[]{:S(2)}) collective-permute-start(f32[128,2048]{1,0:T(8,128)} %collective-permute-done.28.refs_0_), channel_id=1, source_target_pairs={{0,8},{4,20},{8,0},{12,28},{16,24},{20,4},{24,16},{28,12},{1,9},{5... | collective-permute-start | bytes 3145736 | tf_op jit(solution)/shard_map/ppermute | solution.py:390
  179.9 26.0 %collective-permute-start.30 = (f32[128,2048]{1,0:T(8,128)}, f32[128,2048]{1,0:T(8,128)S(1)}, u32[]{:S(2)}, u32[]{:S(2)}) collective-permute-start(f32[128,2048]{1,0:T(8,128)} %collective-permute-done.28.refs_0_), channel_id=1, source_target_pairs={{0,16},{4,12},{8,24},{12,4},{16,0},{20,28},{24,8},{28,20},{1,17},{... | collective-permute-start | bytes 3145736 | tf_op jit(solution)/shard_map/ppermute | solution.py:390
  180.6 25.2 %collective-permute-start.32 = (f32[128,2048]{1,0:T(8,128)}, f32[128,2048]{1,0:T(8,128)S(1)}, u32[]{:S(2)}, u32[]{:S(2)}) collective-permute-start(f32[128,2048]{1,0:T(8,128)} %collective-permute-done.28.refs_0_), channel_id=1, source_target_pairs={{0,4},{4,0},{8,12},{12,8},{16,20},{20,16},{24,28},{28,24},{1,5},{5... | collective-permute-start | bytes 3145736 | tf_op jit(solution)/shard_map/ppermute | solution.py:390
  180.8 26.6 %collective-permute-start.20 = (f32[128,2048]{1,0:T(8,128)}, f32[128,2048]{1,0:T(8,128)S(1)}, u32[]{:S(2)}, u32[]{:S(2)}) collective-permute-start(f32[128,2048]{1,0:T(8,128)} %collective-permute-done.19.refs_0_), channel_id=1, source_target_pairs={{0,8},{4,20},{8,0},{12,28},{16,24},{20,4},{24,16},{28,12},{1,9},{5... | collective-permute-start | bytes 3145736 | tf_op jit(solution)/shard_map/ppermute | solution.py:390
  182.2 43.6 %collective-permute-start.21 = (f32[128,2048]{1,0:T(8,128)}, f32[128,2048]{1,0:T(8,128)S(1)}, u32[]{:S(2)}, u32[]{:S(2)}) collective-permute-start(f32[128,2048]{1,0:T(8,128)} %collective-permute-done.19.refs_0_), channel_id=1, source_target_pairs={{0,16},{4,12},{8,24},{12,4},{16,0},{20,28},{24,8},{28,20},{1,17},{... | collective-permute-start | bytes 3145736 | tf_op jit(solution)/shard_map/ppermute | solution.py:390
  199.0 81.7 %copy-start = (bf16[256,256]{1,0:T(8,128)(2,1)S(1)}, bf16[256,256]{1,0:T(8,128)(2,1)}, u32[]{:S(2)}) copy-start(bf16[256,256]{1,0:T(8,128)(2,1)} %get-tuple-element.33.st_ref) | copy-start | bytes 393220
  199.0 28.4 %collective-permute-start.7 = (f32[160,1024]{1,0:T(8,128)S(1)}, f32[160,1024]{1,0:T(8,128)S(1)}, u32[]{:S(2)}, u32[]{:S(2)}) collective-permute-start(f32[160,1024]{1,0:T(8,128)S(1)} %get-tuple-element.41.refs_0_), channel_id=1, source_target_pairs={{0,2},{4,6},{8,10},{12,14},{16,18},{20,22},{24,26},{28,30}} | collective-permute-start | bytes 1966088 | tf_op jit(solution)/shard_map/ppermute | solution.py:430
  205.9 22.3 %collective-permute-start.23 = (f32[128,2048]{1,0:T(8,128)}, f32[128,2048]{1,0:T(8,128)S(1)}, u32[]{:S(2)}, u32[]{:S(2)}) collective-permute-start(f32[128,2048]{1,0:T(8,128)} %collective-permute-done.19.refs_0_), channel_id=1, source_target_pairs={{0,4},{4,0},{8,12},{12,8},{16,20},{20,16},{24,28},{28,24},{1,5},{5... | collective-permute-start | bytes 3145736 | tf_op jit(solution)/shard_map/ppermute | solution.py:390
  205.9 26.0 %collective-permute-start.11 = (f32[128,2048]{1,0:T(8,128)S(1)}, f32[128,2048]{1,0:T(8,128)S(1)}, u32[]{:S(2)}, u32[]{:S(2)}) collective-permute-start(f32[128,2048]{1,0:T(8,128)S(1)} %collective-permute-done.10.refs_0_), channel_id=1, source_target_pairs={{0,8},{4,20},{8,0},{12,28},{16,24},{20,4},{24,16},{28,12},{1,9},{5... | collective-permute-start | bytes 3145736 | tf_op jit(solution)/shard_map/ppermute | solution.py:390
  207.4 32.4 %collective-permute-start.12 = (f32[128,2048]{1,0:T(8,128)S(1)}, f32[128,2048]{1,0:T(8,128)S(1)}, u32[]{:S(2)}, u32[]{:S(2)}) collective-permute-start(f32[128,2048]{1,0:T(8,128)S(1)} %collective-permute-done.10.refs_0_), channel_id=1, source_target_pairs={{0,16},{4,12},{8,24},{12,4},{16,0},{20,28},{24,8},{28,20},{1,17},{... | collective-permute-start | bytes 3145736 | tf_op jit(solution)/shard_map/ppermute | solution.py:390
  225.8 14.1 %collective-permute-start.8 = (f32[160,1024]{1,0:T(8,128)S(1)}, f32[160,1024]{1,0:T(8,128)S(1)}, u32[]{:S(2)}, u32[]{:S(2)}) collective-permute-start(f32[160,1024]{1,0:T(8,128)S(1)} %get-tuple-element.41.refs_0_), channel_id=1, source_target_pairs={{0,1},{4,5},{8,9},{12,13},{16,17},{20,21},{24,25},{28,29}} | collective-permute-start | bytes 1966088 | tf_op jit(solution)/shard_map/ppermute | solution.py:430
  227.4 12.9 %collective-permute-start.9 = (f32[160,1024]{1,0:T(8,128)S(1)}, f32[160,1024]{1,0:T(8,128)S(1)}, u32[]{:S(2)}, u32[]{:S(2)}) collective-permute-start(f32[160,1024]{1,0:T(8,128)S(1)} %collective-permute-done.7.refs_1_), channel_id=1, source_target_pairs={{2,3},{6,7},{10,11},{14,15},{18,19},{22,23},{26,27},{30,31}} | collective-permute-start | bytes 1966088 | tf_op jit(solution)/shard_map/ppermute | solution.py:430
  228.2 12.9 %collective-permute-start.43 = (f32[128,2048]{1,0:T(8,128)S(1)}, f32[128,2048]{1,0:T(8,128)S(1)}, u32[]{:S(2)}, u32[]{:S(2)}) collective-permute-start(f32[128,2048]{1,0:T(8,128)S(1)} %collective-permute-done.39.refs_3_), channel_id=1, source_target_pairs={{0,4},{4,0},{8,12},{12,8},{16,20},{20,16},{24,28},{28,24},{1,5},{5... | collective-permute-start | bytes 3145736 | tf_op jit(solution)/shard_map/ppermute | solution.py:390
  231.9 19.2 %collective-permute-start.31 = (f32[128,2048]{1,0:T(8,128)S(1)}, f32[128,2048]{1,0:T(8,128)S(1)}, u32[]{:S(2)}, u32[]{:S(2)}) collective-permute-start(f32[128,2048]{1,0:T(8,128)S(1)} %collective-permute-done.29.refs_1_), channel_id=1, source_target_pairs={{0,16},{4,12},{8,24},{12,4},{16,0},{20,28},{24,8},{28,20},{1,17},{... | collective-permute-start | bytes 3145736 | tf_op jit(solution)/shard_map/ppermute | solution.py:390
  239.9 11.2 %collective-permute-start.33 = (f32[128,2048]{1,0:T(8,128)S(1)}, f32[128,2048]{1,0:T(8,128)S(1)}, u32[]{:S(2)}, u32[]{:S(2)}) collective-permute-start(f32[128,2048]{1,0:T(8,128)S(1)} %collective-permute-done.29.refs_1_), channel_id=1, source_target_pairs={{0,4},{4,0},{8,12},{12,8},{16,20},{20,16},{24,28},{28,24},{1,5},{5... | collective-permute-start | bytes 3145736 | tf_op jit(solution)/shard_map/ppermute | solution.py:390
  239.9 12.0 %collective-permute-start.34 = (f32[128,2048]{1,0:T(8,128)S(1)}, f32[128,2048]{1,0:T(8,128)S(1)}, u32[]{:S(2)}, u32[]{:S(2)}) collective-permute-start(f32[128,2048]{1,0:T(8,128)S(1)} %collective-permute-done.30.refs_2_), channel_id=1, source_target_pairs={{0,4},{4,0},{8,12},{12,8},{16,20},{20,16},{24,28},{28,24},{1,5},{5... | collective-permute-start | bytes 3145736 | tf_op jit(solution)/shard_map/ppermute | solution.py:390
  240.4 22.0 %collective-permute-start.22 = (f32[128,2048]{1,0:T(8,128)S(1)}, f32[128,2048]{1,0:T(8,128)S(1)}, u32[]{:S(2)}, u32[]{:S(2)}) collective-permute-start(f32[128,2048]{1,0:T(8,128)S(1)} %collective-permute-done.20.refs_1_), channel_id=1, source_target_pairs={{0,16},{4,12},{8,24},{12,4},{16,0},{20,28},{24,8},{28,20},{1,17},{... | collective-permute-start | bytes 3145736 | tf_op jit(solution)/shard_map/ppermute | solution.py:390
  241.1 21.2 %collective-permute-start.24 = (f32[128,2048]{1,0:T(8,128)S(1)}, f32[128,2048]{1,0:T(8,128)S(1)}, u32[]{:S(2)}, u32[]{:S(2)}) collective-permute-start(f32[128,2048]{1,0:T(8,128)S(1)} %collective-permute-done.20.refs_1_), channel_id=1, source_target_pairs={{0,4},{4,0},{8,12},{12,8},{16,20},{20,16},{24,28},{28,24},{1,5},{5... | collective-permute-start | bytes 3145736 | tf_op jit(solution)/shard_map/ppermute | solution.py:390
  251.1 11.8 %collective-permute-start.25 = (f32[128,2048]{1,0:T(8,128)S(1)}, f32[128,2048]{1,0:T(8,128)S(1)}, u32[]{:S(2)}, u32[]{:S(2)}) collective-permute-start(f32[128,2048]{1,0:T(8,128)S(1)} %collective-permute-done.21.refs_2_), channel_id=1, source_target_pairs={{0,4},{4,0},{8,12},{12,8},{16,20},{20,16},{24,28},{28,24},{1,5},{5... | collective-permute-start | bytes 3145736 | tf_op jit(solution)/shard_map/ppermute | solution.py:390
  251.1 22.5 %collective-permute-start.13 = (f32[128,2048]{1,0:T(8,128)S(1)}, f32[128,2048]{1,0:T(8,128)S(1)}, u32[]{:S(2)}, u32[]{:S(2)}) collective-permute-start(f32[128,2048]{1,0:T(8,128)S(1)} %collective-permute-done.11.refs_1_), channel_id=1, source_target_pairs={{0,16},{4,12},{8,24},{12,4},{16,0},{20,28},{24,8},{28,20},{1,17},{... | collective-permute-start | bytes 3145736 | tf_op jit(solution)/shard_map/ppermute | solution.py:390
  251.8 21.7 %collective-permute-start.35 = (f32[128,2048]{1,0:T(8,128)S(1)}, f32[128,2048]{1,0:T(8,128)S(1)}, u32[]{:S(2)}, u32[]{:S(2)}) collective-permute-start(f32[128,2048]{1,0:T(8,128)S(1)} %collective-permute-done.31.refs_3_), channel_id=1, source_target_pairs={{0,4},{4,0},{8,12},{12,8},{16,20},{20,16},{24,28},{28,24},{1,5},{5... | collective-permute-start | bytes 3145736 | tf_op jit(solution)/shard_map/ppermute | solution.py:390
  262.3 12.9 %collective-permute-start.26 = (f32[128,2048]{1,0:T(8,128)S(1)}, f32[128,2048]{1,0:T(8,128)S(1)}, u32[]{:S(2)}, u32[]{:S(2)}) collective-permute-start(f32[128,2048]{1,0:T(8,128)S(1)} %collective-permute-done.22.refs_3_), channel_id=1, source_target_pairs={{0,4},{4,0},{8,12},{12,8},{16,20},{20,16},{24,28},{28,24},{1,5},{5... | collective-permute-start | bytes 3145736 | tf_op jit(solution)/shard_map/ppermute | solution.py:390
  262.3 39.3 %collective-permute-start.14 = (f32[128,2048]{1,0:T(8,128)S(1)}, f32[128,2048]{1,0:T(8,128)S(1)}, u32[]{:S(2)}, u32[]{:S(2)}) collective-permute-start(f32[128,2048]{1,0:T(8,128)S(1)} %collective-permute-done.10.refs_0_), channel_id=1, source_target_pairs={{0,4},{4,0},{8,12},{12,8},{16,20},{20,16},{24,28},{28,24},{1,5},{5... | collective-permute-start | bytes 3145736 | tf_op jit(solution)/shard_map/ppermute | solution.py:390
  262.9 38.8 %collective-permute-start.15 = (f32[128,2048]{1,0:T(8,128)S(1)}, f32[128,2048]{1,0:T(8,128)S(1)}, u32[]{:S(2)}, u32[]{:S(2)}) collective-permute-start(f32[128,2048]{1,0:T(8,128)S(1)} %collective-permute-done.11.refs_1_), channel_id=1, source_target_pairs={{0,4},{4,0},{8,12},{12,8},{16,20},{20,16},{24,28},{28,24},{1,5},{5... | collective-permute-start | bytes 3145736 | tf_op jit(solution)/shard_map/ppermute | solution.py:390
  273.6 28.1 %collective-permute-start.16 = (f32[128,2048]{1,0:T(8,128)S(1)}, f32[128,2048]{1,0:T(8,128)S(1)}, u32[]{:S(2)}, u32[]{:S(2)}) collective-permute-start(f32[128,2048]{1,0:T(8,128)S(1)} %collective-permute-done.12.refs_2_), channel_id=1, source_target_pairs={{0,4},{4,0},{8,12},{12,8},{16,20},{20,16},{24,28},{28,24},{1,5},{5... | collective-permute-start | bytes 3145736 | tf_op jit(solution)/shard_map/ppermute | solution.py:390
  273.6 28.1 %collective-permute-start.17 = (f32[128,2048]{1,0:T(8,128)S(1)}, f32[128,2048]{1,0:T(8,128)S(1)}, u32[]{:S(2)}, u32[]{:S(2)}) collective-permute-start(f32[128,2048]{1,0:T(8,128)S(1)} %collective-permute-done.13.refs_3_), channel_id=1, source_target_pairs={{0,4},{4,0},{8,12},{12,8},{16,20},{20,16},{24,28},{28,24},{1,5},{5... | collective-permute-start | bytes 3145736 | tf_op jit(solution)/shard_map/ppermute | solution.py:390
  275.2 48.6 %collective-permute-start.18 = (f32[128,2048]{1,0:T(8,128)}, f32[128,2048]{1,0:T(8,128)S(1)}, u32[]{:S(2)}, u32[]{:S(2)}) collective-permute-start(f32[128,2048]{1,0:T(8,128)} %get-tuple-element.48), channel_id=1, source_target_pairs={{0,2},{1,3},{2,0},{3,1},{4,6},{5,7},{6,4},{7,5},{8,10},{9,11},{10,... | collective-permute-start | bytes 3145736 | tf_op jit(solution)/shard_map/ppermute | solution.py:427
  (13 other events, 229.7 us)
